TPU v7x, 512 devices: a 4x2x32 block of a 4x8x32 slice. The times are simulated.
512 devices in a mesh: parts: 2 (over y), section: 4 (over x), tile: 64 (over z, core).
Axes of the slice: x: 4, y: 2, z: 32, core: 2. Of those that a mesh axis runs over, the one named last changes fastest.
The devices are a block of a 4x8x32 slice.
Arguments:
- frames: bfloat16 [8, 64, 16, 16, 128], P('parts', 'tile'), parts along dimension 0, may hold values from -8 to 8
- cache: bfloat16 [4, 4, 64, 16, 16, 128], P('section', 'parts', 'tile'), parts along dimension 1, may hold values from -4 to 4
- conv_weight: bfloat16 [4, 3, 3, 3, 128, 128], P('section'), may hold values from -0.109375 to 0.109375
- conv_bias: float32 [4, 128], P('section'), may hold values from -2 to 2
- norm_gain: float32 [4, 128], P('section'), may hold values from 0.1 to 1.9
- norm_bias: float32 [4, 128], P('section'), may hold values from -2 to 2
Outputs:
- section_outputs: bfloat16 [4, 8, 64, 16, 16, 128], P('section', 'parts', 'tile'), parts along dimension 1
There are 2 independent parts, one for each index of `parts`. A program takes and returns all parts, laid end to end along the dimension named above; an argument that names none is the same for every part. Nothing has to cross between parts.
All inputs are finite; a program needn't handle non-finite values.
Results may differ from a plain program's by a relative error of at most 0.0056.
Values may be sent and summed in bfloat16 or wider, within the bound.
No kernel may reach another device: no remote copies, remote signals or barrier semaphores. Data moves between devices by JAX's collectives and lax.ppermute only.
A program may use at most 64 MiB of HBM per device.

v0:
```python
import jax
import jax.numpy as jnp
from jax import lax
from jax.sharding import PartitionSpec as P

GROUPS = 32


EPSILON = 1e-06


def copy_for_each(array, axis):
    peers = lax.axis_size(axis)
    return lax.all_to_all(
        jnp.broadcast_to(array[None], (peers, *array.shape)), axis, 0, 0, tiled=True
    )


def of_everyone(array, axis):
    return copy_for_each(array, axis).sum(axis=0)


def in_one(arrays, axis):
    ends = [0]
    for a in arrays:
        ends.append(ends[-1] + a.size)
    subtotal = of_everyone(jnp.concatenate([a.ravel() for a in arrays]), axis)
    return tuple((subtotal[b:e].reshape(a.shape) for a, b, e in zip(arrays, ends, ends[1:])))


def from_behind(array, axis, by):
    peers = lax.axis_size(axis)
    return lax.ppermute(array, axis, [(i, (i + by) % peers) for i in range(peers)])


def passed_along(value, axis, steps):
    count = lax.axis_size(axis)
    first, last = (max(0, -steps), min(count, count - steps))
    return lax.ppermute(value, axis, [(source, source + steps) for source in range(first, last)])


def normalize(inputs, gain, offset):
    count, height, width, channels = inputs.shape
    values = inputs.astype(jnp.float32).reshape(count, height * width, GROUPS, channels // GROUPS)
    members = height * width * (channels // GROUPS) * lax.axis_size("tile")
    total, squares = in_one(
        (jnp.sum(values, axis=(1, 3)), jnp.sum(values * values, axis=(1, 3))), "tile"
    )
    mean = (total / members)[:, None, :, None]
    variance = jnp.maximum((squares / members)[:, None, :, None] - mean * mean, 0.0)
    centered = values - mean
    normed = (centered / jnp.sqrt(variance + EPSILON)).reshape(inputs.shape)
    return jax.nn.silu(normed * gain + offset).astype(jnp.bfloat16)


def extend(active):
    tiles = lax.axis_size("tile")
    across = min(8, tiles // 2)
    rows_all = tiles // across
    placed = (lax.axis_index("tile") + across + 2) % tiles
    column = placed % across
    row_at = placed // across
    nothing = jnp.zeros((), active.dtype)
    left = from_behind(active[:, :, -1:], "tile", 1)
    left = jnp.where(column == 0, nothing, left)
    right = from_behind(active[:, :, :1], "tile", -1)
    right = jnp.where(column == across - 1, nothing, right)
    wide = jnp.concatenate([left, active, right], axis=2)
    above = from_behind(wide[:, -1:], "tile", across)
    above = jnp.where(row_at == 0, nothing, above)
    below = from_behind(wide[:, :1], "tile", -across)
    below = jnp.where(row_at == rows_all - 1, nothing, below)
    return jnp.concatenate([above, wide, below], axis=1)


def convolve(padded, kernel, count):
    height = padded.shape[1] - 2
    width = padded.shape[2] - 2
    channels = padded.shape[3]
    pieces = [
        padded[step_t : step_t + count, step_y : step_y + height, step_x : step_x + width]
        for step_t in range(3)
        for step_y in range(3)
        for step_x in range(3)
    ]
    patches = jnp.concatenate(pieces, axis=3).reshape(count * height * width, 27 * channels)
    result = jnp.dot(
        patches, kernel.reshape(27 * channels, channels), preferred_element_type=jnp.float32
    )
    return result.reshape(count, height, width, channels)


def local(frames, cache, conv_weight, conv_bias, norm_gain, norm_bias):
    kernel = conv_weight[0]
    bias = conv_bias[0]
    gain = norm_gain[0]
    offset = norm_bias[0]
    sections = lax.axis_size("section")
    position = lax.axis_index("section")
    inputs = frames[:, 0]
    history = extend(cache[0, :, 0])
    count = inputs.shape[0]
    result = jnp.zeros_like(inputs)
    current = inputs
    for tick in range(sections):
        active = normalize(current, gain, offset)
        padded = jnp.concatenate([history, extend(active)], axis=0)
        output = (current.astype(jnp.float32) + convolve(padded, kernel, count) + bias).astype(
            jnp.bfloat16
        )
        result = jnp.where(position == tick, output, result)
        if tick + 1 < sections:
            current = passed_along(output, "section", 1)
    return result[None, :, None]


def solution(mesh):
    placed = (
        P("parts", "tile", None, None, None),
        P("section", "parts", "tile", None, None, None),
        P("section", None, None, None, None, None),
        P("section", None),
        P("section", None),
        P("section", None),
    )
    return jax.shard_map(
        local,
        mesh=mesh,
        in_specs=placed,
        out_specs=P("section", "parts", "tile", None, None, None),
        check_vma=False,
    )
```

profile of v0, /device:TPU:42, one launch (start us, length us, event | category | flops | bytes accessed | tf_op | source)
XLA Modules:
  0.0 315.7 jit_solution(55437010632432407)
XLA Ops:
  0.0 1.0 fusion.39
  1.0 43.0 %collective-permute-start.1 = (bf16[2,16,1,128]{3,2,1,0:T(2,128)(2,1)S(1)}, bf16[2,16,1,128]{3,2,1,0:T(2,128)(2,1)S(1)}, u32[]{:S(2)}, u32[]{:S(2)}) collective-permute-start(bf16[2,16,1,128]{3,2,1,0:T(2,128)(2,1)S(1)} %get-tuple-element.40), channel_id=1, source_target_pairs={{0,63},{1,0},{2,1},{3,2},{4,3},{5,4},{6,5},{7,6},{8,7},{9,8},{10,9... | collective-permute-start | bytes 24584 | tf_op jit(solution)/shard_map/ppermute | solution.py:33
  43.9 1.0 convert_reduce_fusion.3
  45.6 0.7 broadcast_in_dim.74
  46.3 6.5 %all-to-all-start = ((f32[64,1,256]{2,1,0:T(1,128)}), f32[64,1,256]{2,1,0:T(1,128)S(1)}, u32[]{:S(2)}, u32[]{:S(2)}) async-start(f32[64,1,256]{2,1,0:T(1,128)} %broadcast_in_dim.74), calls=%async_computation | async-start | bytes 131072 | tf_op jit(solution)/shard_map/all_to_all | solution.py:14
  52.9 4.9 %collective-permute-done = bf16[2,16,1,128]{3,2,1,0:T(2,128)(2,1)S(1)} collective-permute-done((bf16[2,16,1,128]{3,2,1,0:T(2,128)(2,1)S(1)}, bf16[2,16,1,128]{3,2,1,0:T(2,128)(2,1)S(1)}, u32[]{:S(2)}, u32[]{:S(2)}) %collective-permute-start) | collective-permute-done | bytes 8224 | tf_op jit(solution)/shard_map/ppermute | solution.py:33
  57.8 0.7 pad_maximum_fusion.27
  58.5 7.2 %collective-permute-start.3 = (bf16[2,1,18,128]{3,2,1,0:T(8,128)(2,1)S(1)}, bf16[2,1,18,128]{3,2,1,0:T(8,128)(2,1)S(1)}, u32[]{:S(2)}, u32[]{:S(2)}) collective-permute-start(bf16[2,1,18,128]{3,2,1,0:T(8,128)(2,1)S(1)} %get-tuple-element.38), channel_id=1, source_target_pairs={{0,56},{1,57},{2,58},{3,59},{4,60},{5,61},{6,62},{7,63},{8,0},{9,1... | collective-permute-start | bytes 27656 | tf_op jit(solution)/shard_map/ppermute | solution.py:33
  65.7 2.6 collective-permute-start.2
  68.4 9.3 %all-to-all-done = f32[64,1,256]{2,1,0:T(1,128)S(1)} async-done(((f32[64,1,256]{2,1,0:T(1,128)}), f32[64,1,256]{2,1,0:T(1,128)S(1)}, u32[]{:S(2)}, u32[]{:S(2)}) %all-to-all-start) | async-done | bytes 65568 | tf_op jit(solution)/shard_map/all_to_all | solution.py:14
  78.3 1.2 multiply_convert_fusion.3
  79.7 0.5 collective-permute-start.4
  80.2 1.0 collective-permute-done.5
  81.3 3.0 collective-permute-done.4
  84.4 2.5 collective-permute-start.7
  86.9 7.4 %collective-permute-start.6 = (bf16[4,1,18,128]{3,2,1,0:T(8,128)(2,1)S(1)}, bf16[4,1,18,128]{3,2,1,0:T(8,128)(2,1)S(1)}, u32[]{:S(2)}, u32[]{:S(2)}) collective-permute-start(bf16[4,1,18,128]{3,2,1,0:T(8,128)(2,1)S(1)} %get-tuple-element.27), channel_id=1, source_target_pairs={{0,8},{1,9},{2,10},{3,11},{4,12},{5,13},{6,14},{7,15},{8,16},{9,17... | collective-permute-start | bytes 55304 | tf_op jit(solution)/shard_map/ppermute | solution.py:33
  94.4 2.2 collective-permute-done.6
  96.9 1.3 maximum_maximum_fusion
  101.4 2.0 fusion.7
  103.4 3.6 %collective-permute-start.8 = (bf16[4,16,16,128]{3,2,1,0:T(8,128)(2,1)S(1)}, bf16[4,16,16,128]{3,2,1,0:T(8,128)(2,1)S(1)}, u32[]{:S(2)}, u32[]{:S(2)}) collective-permute-start(bf16[4,16,16,128]{3,2,1,0:T(8,128)(2,1)S(1)} %fusion.7), channel_id=1, source_target_pairs={{0,64},{64,128},{128,192},{1,65},{65,129},{129,193},{2,66},{66,130... | collective-permute-start | bytes 786440 | tf_op jit(solution)/shard_map/ppermute | solution.py:39
  107.0 4.7 %collective-permute-done.8 = bf16[4,16,16,128]{3,2,1,0:T(8,128)(2,1)S(1)} collective-permute-done((bf16[4,16,16,128]{3,2,1,0:T(8,128)(2,1)S(1)}, bf16[4,16,16,128]{3,2,1,0:T(8,128)(2,1)S(1)}, u32[]{:S(2)}, u32[]{:S(2)}) %collective-permute-start.8) | collective-permute-done | bytes 262176 | tf_op jit(solution)/shard_map/ppermute | solution.py:39
  112.5 40.6 %all_to_all.24 = f32[64,1,256]{2,1,0:T(1,128)S(1)} all-to-all(f32[64,1,256]{2,1,0:T(1,128)S(1)} %broadcast_in_dim.75), channel_id=1, replica_groups=mesh['parts'=2,'section'=4,'tile'=64] {'tile'}, dimensions={0} | all-to-all | bytes 131072 | tf_op jit(solution)/shard_map/all_to_all | solution.py:14
  154.1 0.5 collective-permute-start.9
  154.5 1.1 collective-permute-done.10
  155.7 3.0 collective-permute-done.9
  158.7 2.5 collective-permute-start.12
  161.3 7.3 %collective-permute-start.11 = (bf16[4,1,18,128]{3,2,1,0:T(8,128)(2,1)S(1)}, bf16[4,1,18,128]{3,2,1,0:T(8,128)(2,1)S(1)}, u32[]{:S(2)}, u32[]{:S(2)}) collective-permute-start(bf16[4,1,18,128]{3,2,1,0:T(8,128)(2,1)S(1)} %get-tuple-element.23), channel_id=1, source_target_pairs={{0,8},{1,9},{2,10},{3,11},{4,12},{5,13},{6,14},{7,15},{8,16},{9,17... | collective-permute-start | bytes 55304 | tf_op jit(solution)/shard_map/ppermute | solution.py:33
  168.6 2.3 collective-permute-done.11
  174.8 2.0 fusion.6
  176.8 3.6 %collective-permute-start.13 = (bf16[4,16,16,128]{3,2,1,0:T(8,128)(2,1)S(1)}, bf16[4,16,16,128]{3,2,1,0:T(8,128)(2,1)S(1)}, u32[]{:S(2)}, u32[]{:S(2)}) collective-permute-start(bf16[4,16,16,128]{3,2,1,0:T(8,128)(2,1)S(1)} %fusion.6), channel_id=1, source_target_pairs={{0,64},{64,128},{128,192},{1,65},{65,129},{129,193},{2,66},{66,130... | collective-permute-start | bytes 786440 | tf_op jit(solution)/shard_map/ppermute | solution.py:39
  180.4 4.7 %collective-permute-done.13 = bf16[4,16,16,128]{3,2,1,0:T(8,128)(2,1)S(1)} collective-permute-done((bf16[4,16,16,128]{3,2,1,0:T(8,128)(2,1)S(1)}, bf16[4,16,16,128]{3,2,1,0:T(8,128)(2,1)S(1)}, u32[]{:S(2)}, u32[]{:S(2)}) %collective-permute-start.13) | collective-permute-done | bytes 262176 | tf_op jit(solution)/shard_map/ppermute | solution.py:39
  185.8 36.3 %all_to_all.25 = f32[64,1,256]{2,1,0:T(1,128)S(1)} all-to-all(f32[64,1,256]{2,1,0:T(1,128)S(1)} %broadcast_in_dim.76), channel_id=1, replica_groups=mesh['parts'=2,'section'=4,'tile'=64] {'tile'}, dimensions={0} | all-to-all | bytes 131072 | tf_op jit(solution)/shard_map/all_to_all | solution.py:14
  223.2 0.5 collective-permute-start.14
  223.7 1.1 collective-permute-done.15
  224.8 3.0 collective-permute-done.14
  227.8 2.5 collective-permute-start.17
  230.4 7.5 %collective-permute-start.16 = (bf16[4,1,18,128]{3,2,1,0:T(8,128)(2,1)S(1)}, bf16[4,1,18,128]{3,2,1,0:T(8,128)(2,1)S(1)}, u32[]{:S(2)}, u32[]{:S(2)}) collective-permute-start(bf16[4,1,18,128]{3,2,1,0:T(8,128)(2,1)S(1)} %get-tuple-element.19), channel_id=1, source_target_pairs={{0,8},{1,9},{2,10},{3,11},{4,12},{5,13},{6,14},{7,15},{8,16},{9,17... | collective-permute-start | bytes 55304 | tf_op jit(solution)/shard_map/ppermute | solution.py:33
  237.9 2.1 collective-permute-done.16
  243.9 2.0 fusion.5
  245.9 3.6 %collective-permute-start.18 = (bf16[4,16,16,128]{3,2,1,0:T(8,128)(2,1)S(1)}, bf16[4,16,16,128]{3,2,1,0:T(8,128)(2,1)S(1)}, u32[]{:S(2)}, u32[]{:S(2)}) collective-permute-start(bf16[4,16,16,128]{3,2,1,0:T(8,128)(2,1)S(1)} %fusion.5), channel_id=1, source_target_pairs={{0,64},{64,128},{128,192},{1,65},{65,129},{129,193},{2,66},{66,130... | collective-permute-start | bytes 786440 | tf_op jit(solution)/shard_map/ppermute | solution.py:39
  249.5 4.7 %collective-permute-done.18 = bf16[4,16,16,128]{3,2,1,0:T(8,128)(2,1)S(1)} collective-permute-done((bf16[4,16,16,128]{3,2,1,0:T(8,128)(2,1)S(1)}, bf16[4,16,16,128]{3,2,1,0:T(8,128)(2,1)S(1)}, u32[]{:S(2)}, u32[]{:S(2)}) %collective-permute-start.18) | collective-permute-done | bytes 262176 | tf_op jit(solution)/shard_map/ppermute | solution.py:39
  254.9 36.3 %all_to_all.26 = f32[64,1,256]{2,1,0:T(1,128)S(1)} all-to-all(f32[64,1,256]{2,1,0:T(1,128)S(1)} %broadcast_in_dim.77), channel_id=1, replica_groups=mesh['parts'=2,'section'=4,'tile'=64] {'tile'}, dimensions={0} | all-to-all | bytes 131072 | tf_op jit(solution)/shard_map/all_to_all | solution.py:14
  292.8 1.1 collective-permute-done.20
  293.9 3.0 collective-permute-done.19
  296.9 2.5 collective-permute-start.22
  299.5 7.6 %collective-permute-start.21 = (bf16[4,1,18,128]{3,2,1,0:T(8,128)(2,1)S(1)}, bf16[4,1,18,128]{3,2,1,0:T(8,128)(2,1)S(1)}, u32[]{:S(2)}, u32[]{:S(2)}) collective-permute-start(bf16[4,1,18,128]{3,2,1,0:T(8,128)(2,1)S(1)} %get-tuple-element.15), channel_id=1, source_target_pairs={{0,8},{1,9},{2,10},{3,11},{4,12},{5,13},{6,14},{7,15},{8,16},{9,17... | collective-permute-start | bytes 55304 | tf_op jit(solution)/shard_map/ppermute | solution.py:33
  307.1 2.1 collective-permute-done.21
  313.0 2.7 fusion.9
  (241 shorter events, 22.0 us)
Async XLA Ops:
  0.0 101.4 %copy-start = (bf16[1,3,3,3,128,128]{5,4,3,2,1,0:T(8,128)(2,1)S(1)}, bf16[1,3,3,3,128,128]{5,4,3,2,1,0:T(8,128)(2,1)}, u32[]{:S(2)}) copy-start(bf16[1,3,3,3,128,128]{5,4,3,2,1,0:T(8,128)(2,1)} %param.8) | copy-start | bytes 2654212
  1.0 51.9 %collective-permute-start.1 = (bf16[2,16,1,128]{3,2,1,0:T(2,128)(2,1)S(1)}, bf16[2,16,1,128]{3,2,1,0:T(2,128)(2,1)S(1)}, u32[]{:S(2)}, u32[]{:S(2)}) collective-permute-start(bf16[2,16,1,128]{3,2,1,0:T(2,128)(2,1)S(1)} %get-tuple-element.40), channel_id=1, source_target_pairs={{0,63},{1,0},{2,1},{3,2},{4,3},{5,4},{6,5},{7,6},{8,7},{9,8},{10,9... | collective-permute-start | bytes 24584 | tf_op jit(solution)/shard_map/ppermute | solution.py:33
  46.3 31.4 %all-to-all-start = ((f32[64,1,256]{2,1,0:T(1,128)}), f32[64,1,256]{2,1,0:T(1,128)S(1)}, u32[]{:S(2)}, u32[]{:S(2)}) async-start(f32[64,1,256]{2,1,0:T(1,128)} %broadcast_in_dim.74), calls=%async_computation | async-start | bytes 131072 | tf_op jit(solution)/shard_map/all_to_all | solution.py:14
  52.7 5.0 %collective-permute-start = (bf16[2,16,1,128]{3,2,1,0:T(2,128)(2,1)S(1)}, bf16[2,16,1,128]{3,2,1,0:T(2,128)(2,1)S(1)}, u32[]{:S(2)}, u32[]{:S(2)}) collective-permute-start(bf16[2,16,1,128]{3,2,1,0:T(2,128)(2,1)S(1)} %get-tuple-element.39), channel_id=1, source_target_pairs={{0,1},{1,2},{2,3},{3,4},{4,5},{5,6},{6,7},{7,8},{8,9},{9,10},{10,1... | collective-permute-start | bytes 24584 | tf_op jit(solution)/shard_map/ppermute | solution.py:33
  58.5 21.1 %collective-permute-start.3 = (bf16[2,1,18,128]{3,2,1,0:T(8,128)(2,1)S(1)}, bf16[2,1,18,128]{3,2,1,0:T(8,128)(2,1)S(1)}, u32[]{:S(2)}, u32[]{:S(2)}) collective-permute-start(bf16[2,1,18,128]{3,2,1,0:T(8,128)(2,1)S(1)} %get-tuple-element.38), channel_id=1, source_target_pairs={{0,56},{1,57},{2,58},{3,59},{4,60},{5,61},{6,62},{7,63},{8,0},{9,1... | collective-permute-start | bytes 27656 | tf_op jit(solution)/shard_map/ppermute | solution.py:33
  65.7 21.2 %collective-permute-start.2 = (bf16[2,1,18,128]{3,2,1,0:T(8,128)(2,1)S(1)}, bf16[2,1,18,128]{3,2,1,0:T(8,128)(2,1)S(1)}, u32[]{:S(2)}, u32[]{:S(2)}) collective-permute-start(bf16[2,1,18,128]{3,2,1,0:T(8,128)(2,1)S(1)} %get-tuple-element.37), channel_id=1, source_target_pairs={{0,8},{1,9},{2,10},{3,11},{4,12},{5,13},{6,14},{7,15},{8,16},{9,17... | collective-permute-start | bytes 27656 | tf_op jit(solution)/shard_map/ppermute | solution.py:33
  79.6 1.7 collective-permute-start.5
  79.7 4.6 %collective-permute-start.4 = (bf16[4,16,1,128]{3,2,1,0:T(2,128)(2,1)S(1)}, bf16[4,16,1,128]{3,2,1,0:T(2,128)(2,1)S(1)}, u32[]{:S(2)}, u32[]{:S(2)}) collective-permute-start(bf16[4,16,1,128]{3,2,1,0:T(2,128)(2,1)S(1)} %get-tuple-element.35), channel_id=1, source_target_pairs={{0,1},{1,2},{2,3},{3,4},{4,5},{5,6},{6,7},{7,8},{8,9},{9,10},{10,1... | collective-permute-start | bytes 49160 | tf_op jit(solution)/shard_map/ppermute | solution.py:33
  84.3 16.2 %copy-start.2 = (bf16[4,1,16,16,128]{4,3,2,1,0:T(8,128)(2,1)S(1)}, bf16[4,1,16,16,128]{4,3,2,1,0:T(8,128)(2,1)}, u32[]{:S(2)}) copy-start(bf16[4,1,16,16,128]{4,3,2,1,0:T(8,128)(2,1)} %param.6) | copy-start | bytes 786436
  84.4 16.2 %copy-start.3 = (f32[1,128]{1,0:T(1,128)S(1)}, f32[1,128]{1,0:T(1,128)}, u32[]{:S(2)}) copy-start(f32[1,128]{1,0:T(1,128)} %param.11) | copy-start | bytes 1540
  84.4 16.2 %copy-start.4 = (f32[1,128]{1,0:T(1,128)S(1)}, f32[1,128]{1,0:T(1,128)}, u32[]{:S(2)}) copy-start(f32[1,128]{1,0:T(1,128)} %param.10) | copy-start | bytes 1540
  84.4 10.0 %collective-permute-start.7 = (bf16[4,1,18,128]{3,2,1,0:T(8,128)(2,1)S(1)}, bf16[4,1,18,128]{3,2,1,0:T(8,128)(2,1)S(1)}, u32[]{:S(2)}, u32[]{:S(2)}) collective-permute-start(bf16[4,1,18,128]{3,2,1,0:T(8,128)(2,1)S(1)} %get-tuple-element.28), channel_id=1, source_target_pairs={{0,56},{1,57},{2,58},{3,59},{4,60},{5,61},{6,62},{7,63},{8,0},{9,1... | collective-permute-start | bytes 55304 | tf_op jit(solution)/shard_map/ppermute | solution.py:33
  86.9 9.7 %collective-permute-start.6 = (bf16[4,1,18,128]{3,2,1,0:T(8,128)(2,1)S(1)}, bf16[4,1,18,128]{3,2,1,0:T(8,128)(2,1)S(1)}, u32[]{:S(2)}, u32[]{:S(2)}) collective-permute-start(bf16[4,1,18,128]{3,2,1,0:T(8,128)(2,1)S(1)} %get-tuple-element.27), channel_id=1, source_target_pairs={{0,8},{1,9},{2,10},{3,11},{4,12},{5,13},{6,14},{7,15},{8,16},{9,17... | collective-permute-start | bytes 55304 | tf_op jit(solution)/shard_map/ppermute | solution.py:33
  98.2 3.2 %copy-start.5 = (f32[1,128]{1,0:T(1,128)S(1)}, f32[1,128]{1,0:T(1,128)}, u32[]{:S(2)}) copy-start(f32[1,128]{1,0:T(1,128)} %param.9) | copy-start | bytes 1540
  100.6 70.3 %copy-start.1 = (bf16[1,2,1,16,16,128]{5,4,3,2,1,0:T(8,128)(2,1)S(1)}, bf16[1,2,1,16,16,128]{5,4,3,2,1,0:T(8,128)(2,1)}, u32[]{:S(2)}) copy-start(bf16[1,2,1,16,16,128]{5,4,3,2,1,0:T(8,128)(2,1)} %param.7) | copy-start | bytes 393220
  103.4 8.3 %collective-permute-start.8 = (bf16[4,16,16,128]{3,2,1,0:T(8,128)(2,1)S(1)}, bf16[4,16,16,128]{3,2,1,0:T(8,128)(2,1)S(1)}, u32[]{:S(2)}, u32[]{:S(2)}) collective-permute-start(bf16[4,16,16,128]{3,2,1,0:T(8,128)(2,1)S(1)} %fusion.7), channel_id=1, source_target_pairs={{0,64},{64,128},{128,192},{1,65},{65,129},{129,193},{2,66},{66,130... | collective-permute-start | bytes 786440 | tf_op jit(solution)/shard_map/ppermute | solution.py:39
  154.0 1.7 collective-permute-start.10
  154.1 4.6 %collective-permute-start.9 = (bf16[4,16,1,128]{3,2,1,0:T(2,128)(2,1)S(1)}, bf16[4,16,1,128]{3,2,1,0:T(2,128)(2,1)S(1)}, u32[]{:S(2)}, u32[]{:S(2)}) collective-permute-start(bf16[4,16,1,128]{3,2,1,0:T(2,128)(2,1)S(1)} %get-tuple-element.33), channel_id=1, source_target_pairs={{0,1},{1,2},{2,3},{3,4},{4,5},{5,6},{6,7},{7,8},{8,9},{9,10},{10,1... | collective-permute-start | bytes 49160 | tf_op jit(solution)/shard_map/ppermute | solution.py:33
  158.7 9.8 %collective-permute-start.12 = (bf16[4,1,18,128]{3,2,1,0:T(8,128)(2,1)S(1)}, bf16[4,1,18,128]{3,2,1,0:T(8,128)(2,1)S(1)}, u32[]{:S(2)}, u32[]{:S(2)}) collective-permute-start(bf16[4,1,18,128]{3,2,1,0:T(8,128)(2,1)S(1)} %get-tuple-element.24), channel_id=1, source_target_pairs={{0,56},{1,57},{2,58},{3,59},{4,60},{5,61},{6,62},{7,63},{8,0},{9,1... | collective-permute-start | bytes 55304 | tf_op jit(solution)/shard_map/ppermute | solution.py:33
  161.3 9.7 %collective-permute-start.11 = (bf16[4,1,18,128]{3,2,1,0:T(8,128)(2,1)S(1)}, bf16[4,1,18,128]{3,2,1,0:T(8,128)(2,1)S(1)}, u32[]{:S(2)}, u32[]{:S(2)}) collective-permute-start(bf16[4,1,18,128]{3,2,1,0:T(8,128)(2,1)S(1)} %get-tuple-element.23), channel_id=1, source_target_pairs={{0,8},{1,9},{2,10},{3,11},{4,12},{5,13},{6,14},{7,15},{8,16},{9,17... | collective-permute-start | bytes 55304 | tf_op jit(solution)/shard_map/ppermute | solution.py:33
  176.8 8.3 %collective-permute-start.13 = (bf16[4,16,16,128]{3,2,1,0:T(8,128)(2,1)S(1)}, bf16[4,16,16,128]{3,2,1,0:T(8,128)(2,1)S(1)}, u32[]{:S(2)}, u32[]{:S(2)}) collective-permute-start(bf16[4,16,16,128]{3,2,1,0:T(8,128)(2,1)S(1)} %fusion.6), channel_id=1, source_target_pairs={{0,64},{64,128},{128,192},{1,65},{65,129},{129,193},{2,66},{66,130... | collective-permute-start | bytes 786440 | tf_op jit(solution)/shard_map/ppermute | solution.py:39
  223.1 1.7 collective-permute-start.15
  223.2 4.6 %collective-permute-start.14 = (bf16[4,16,1,128]{3,2,1,0:T(2,128)(2,1)S(1)}, bf16[4,16,1,128]{3,2,1,0:T(2,128)(2,1)S(1)}, u32[]{:S(2)}, u32[]{:S(2)}) collective-permute-start(bf16[4,16,1,128]{3,2,1,0:T(2,128)(2,1)S(1)} %get-tuple-element.31), channel_id=1, source_target_pairs={{0,1},{1,2},{2,3},{3,4},{4,5},{5,6},{6,7},{7,8},{8,9},{9,10},{10,1... | collective-permute-start | bytes 49160 | tf_op jit(solution)/shard_map/ppermute | solution.py:33
  227.8 10.1 %collective-permute-start.17 = (bf16[4,1,18,128]{3,2,1,0:T(8,128)(2,1)S(1)}, bf16[4,1,18,128]{3,2,1,0:T(8,128)(2,1)S(1)}, u32[]{:S(2)}, u32[]{:S(2)}) collective-permute-start(bf16[4,1,18,128]{3,2,1,0:T(8,128)(2,1)S(1)} %get-tuple-element.20), channel_id=1, source_target_pairs={{0,56},{1,57},{2,58},{3,59},{4,60},{5,61},{6,62},{7,63},{8,0},{9,1... | collective-permute-start | bytes 55304 | tf_op jit(solution)/shard_map/ppermute | solution.py:33
  230.4 9.7 %collective-permute-start.16 = (bf16[4,1,18,128]{3,2,1,0:T(8,128)(2,1)S(1)}, bf16[4,1,18,128]{3,2,1,0:T(8,128)(2,1)S(1)}, u32[]{:S(2)}, u32[]{:S(2)}) collective-permute-start(bf16[4,1,18,128]{3,2,1,0:T(8,128)(2,1)S(1)} %get-tuple-element.19), channel_id=1, source_target_pairs={{0,8},{1,9},{2,10},{3,11},{4,12},{5,13},{6,14},{7,15},{8,16},{9,17... | collective-permute-start | bytes 55304 | tf_op jit(solution)/shard_map/ppermute | solution.py:33
  245.9 8.3 %collective-permute-start.18 = (bf16[4,16,16,128]{3,2,1,0:T(8,128)(2,1)S(1)}, bf16[4,16,16,128]{3,2,1,0:T(8,128)(2,1)S(1)}, u32[]{:S(2)}, u32[]{:S(2)}) collective-permute-start(bf16[4,16,16,128]{3,2,1,0:T(8,128)(2,1)S(1)} %fusion.5), channel_id=1, source_target_pairs={{0,64},{64,128},{128,192},{1,65},{65,129},{129,193},{2,66},{66,130... | collective-permute-start | bytes 786440 | tf_op jit(solution)/shard_map/ppermute | solution.py:39
  292.2 1.7 collective-permute-start.20
  292.3 4.6 %collective-permute-start.19 = (bf16[4,16,1,128]{3,2,1,0:T(2,128)(2,1)S(1)}, bf16[4,16,1,128]{3,2,1,0:T(2,128)(2,1)S(1)}, u32[]{:S(2)}, u32[]{:S(2)}) collective-permute-start(bf16[4,16,1,128]{3,2,1,0:T(2,128)(2,1)S(1)} %get-tuple-element.29), channel_id=1, source_target_pairs={{0,1},{1,2},{2,3},{3,4},{4,5},{5,6},{6,7},{7,8},{8,9},{9,10},{10,1... | collective-permute-start | bytes 49160 | tf_op jit(solution)/shard_map/ppermute | solution.py:33
  296.9 10.1 %collective-permute-start.22 = (bf16[4,1,18,128]{3,2,1,0:T(8,128)(2,1)S(1)}, bf16[4,1,18,128]{3,2,1,0:T(8,128)(2,1)S(1)}, u32[]{:S(2)}, u32[]{:S(2)}) collective-permute-start(bf16[4,1,18,128]{3,2,1,0:T(8,128)(2,1)S(1)} %get-tuple-element.16), channel_id=1, source_target_pairs={{0,56},{1,57},{2,58},{3,59},{4,60},{5,61},{6,62},{7,63},{8,0},{9,1... | collective-permute-start | bytes 55304 | tf_op jit(solution)/shard_map/ppermute | solution.py:33
  299.5 9.7 %collective-permute-start.21 = (bf16[4,1,18,128]{3,2,1,0:T(8,128)(2,1)S(1)}, bf16[4,1,18,128]{3,2,1,0:T(8,128)(2,1)S(1)}, u32[]{:S(2)}, u32[]{:S(2)}) collective-permute-start(bf16[4,1,18,128]{3,2,1,0:T(8,128)(2,1)S(1)} %get-tuple-element.15), channel_id=1, source_target_pairs={{0,8},{1,9},{2,10},{3,11},{4,12},{5,13},{6,14},{7,15},{8,16},{9,17... | collective-permute-start | bytes 55304 | tf_op jit(solution)/shard_map/ppermute | solution.py:33
where the time goes:
time: 316 us
  blocking collectives  113 us (36%)
  starting transfers between devices  112 us (35%)
  waiting for transfers between devices  53.3 us (17%)
  local copies, waits for them, and re-layouts  15.6 us (5%)
  other arithmetic  11.5 us (4%)
  matrix products  8.73 us (3%)
    all_to_all x3, blocking collectives, copy_for_each(): lax.all_to_all(jnp.broadcast_to(array[None], (peers, *array.shape)), axis...  113 us
    ppermute x20, starting transfers between devices, from_behind(): lax.ppermute(array, axis, [(i, (i + by) % peers) for i in range(peers)])  94.9 us
    ppermute x20, waiting for transfers between devices, from_behind(): lax.ppermute(array, axis, [(i, (i + by) % peers) for i in range(peers)])  29.8 us
    ppermute x3, waiting for transfers between devices, passed_along(): lax.ppermute(value, axis, [(source, source + steps) for source in range(f...  14.2 us
    ppermute x3, starting transfers between devices, passed_along(): lax.ppermute(value, axis, [(source, source + steps) for source in range(f...  10.7 us
    unnamed x104, local copies, waits for them, and re-layouts  9.32 us
    all_to_all x1, waiting for transfers between devices, copy_for_each(): lax.all_to_all(jnp.broadcast_to(array[None], (peers, *array.shape)), axis...  9.27 us
    dot_general x4, matrix products, convolve(): jnp.dot(patches, kernel.reshape(27 * channels, channels), preferred_eleme...  8.73 us
  transfers between devices with their start and end apart: 24, of which 17 were waited for; matrix products, arithmetic and copies ran while one was open for 2% of the time, Pallas kernels for 0%

commit v1 on v0

v1 whole, which is shorter than its diff:
```python
import functools

import jax
import jax.numpy as jnp
from jax import lax
from jax.experimental import pallas as pl
from jax.experimental.pallas import tpu as pltpu
from jax.sharding import PartitionSpec as P

GROUPS = 32
EPSILON = 1e-06
TAPS = 3


def shifted(array, by):
    peers = lax.axis_size("tile")
    return lax.ppermute(array, "tile", [(i, (i + by) % peers) for i in range(peers)])


def summed(array, groups):
    return jnp.sum(lax.all_gather(array, "tile", axis_index_groups=groups), axis=0)


def over_lanes(value, members):
    lanes = value.shape[-1]
    lane = lax.broadcasted_iota(jnp.int32, value.shape, value.ndim - 1)
    step = 1
    while step < members:
        up = pltpu.roll(value, lanes - step, value.ndim - 1)
        down = pltpu.roll(value, step, value.ndim - 1)
        value = value + jnp.where((lane // step) % 2 == 0, up, down)
        step *= 2
    return value


def packed(totals, members):
    totals = over_lanes(totals, members)
    lane = lax.broadcasted_iota(jnp.int32, (1, totals.shape[-1]), 1)
    row = jnp.zeros((1, totals.shape[-1]), jnp.float32)
    for frame in range(totals.shape[0]):
        row = row + jnp.where(lane % members == frame, totals[frame : frame + 1], 0.0)
    return row


def unpacked(row, frame, members):
    lane = lax.broadcasted_iota(jnp.int32, row.shape, 1)
    return over_lanes(jnp.where(lane % members == frame, row, 0.0), members)


def sums_kernel(members, x_ref, sums_ref):
    values = x_ref[...].astype(jnp.float32)
    count = values.shape[0]
    values = values.reshape(count, -1, values.shape[-1])
    sums_ref[0:1, :] = packed(jnp.sum(values, axis=1), members)
    sums_ref[1:2, :] = packed(jnp.sum(values * values, axis=1), members)


def first_sums(frames, members):
    return pl.pallas_call(
        functools.partial(sums_kernel, members),
        out_shape=jax.ShapeDtypeStruct((2, frames.shape[-1]), jnp.float32),
        in_specs=[pl.BlockSpec(memory_space=pltpu.VMEM)],
        out_specs=pl.BlockSpec(memory_space=pltpu.VMEM),
    )(frames)


def section_kernel(
    shape, tick, place_ref, x_ref, sums_ref, cache_ref, kernel_ref, bias_ref, gain_ref, offset_ref,
    kept_ref, next_ref, result_ref, out_sums_ref, act, held, cols, made,
):
    count, context, side, wide, sections, pixels, members = shape
    rows_in = wide - 2 * tick
    rows_out = rows_in - 2
    channels = x_ref.shape[-1]
    flat_in = rows_in * wide
    flat_out = rows_out * wide
    first_row, last_row, first_col, last_col, mine = (place_ref[i] for i in range(5))

    def inside(edge, rows):
        row = lax.broadcasted_iota(jnp.int32, (rows, wide, channels), 0)
        col = lax.broadcasted_iota(jnp.int32, (rows, wide, channels), 1)
        far = edge + side
        low_r = jnp.where(first_row == 1, edge, 0)
        high_r = jnp.where(last_row == 1, far, far + edge)
        low_c = jnp.where(first_col == 1, edge, 0)
        high_c = jnp.where(last_col == 1, far, far + edge)
        return (row >= low_r) & (row < high_r) & (col >= low_c) & (col < high_c)

    halo = (wide - side) // 2
    valid = inside(halo, wide)
    for f in range(context):
        values = cache_ref[f].astype(jnp.float32).reshape(wide, wide, channels)
        act[f, : wide * wide] = jnp.where(valid, values, 0.0).reshape(wide * wide, channels)
    total = jnp.sum(sums_ref[...], axis=0)
    mean_row = total[0:1] / pixels
    square_row = total[1:2] / pixels
    valid = inside(halo - tick, rows_in)
    gain = gain_ref[...].reshape(1, channels)
    offset = offset_ref[...].reshape(1, channels)
    for f in range(count):
        mean = unpacked(mean_row, f, members)
        variance = jnp.maximum(unpacked(square_row, f, members) - mean * mean, 0.0)
        scale = gain / jnp.sqrt(variance + EPSILON)
        values = x_ref[f].astype(jnp.float32)
        held[f, :flat_in] = values
        normed = (values - mean) * scale + offset
        half = 0.5 * normed
        active = (half + half * jnp.tanh(half)).reshape(rows_in, wide, channels)
        active = jnp.where(valid, active, 0.0).reshape(flat_in, channels)
        act[context + f, :flat_in] = active
    for f in range(context + count):
        base = tick * (wide + 1) if f < context else 0
        for dy in range(TAPS):
            for dx in range(TAPS):
                at = base + dy * wide + dx
                piece = act[f, at : at + flat_out].astype(jnp.bfloat16)
                tap = (dy * TAPS + dx) * channels
                cols[f, :flat_out, tap : tap + channels] = piece
    w0, w1, w2 = (kernel_ref[i] for i in range(TAPS))
    both_1 = jnp.concatenate([w1, w0], axis=1)
    both_2 = jnp.concatenate([w2, w1], axis=1)
    bias = bias_ref[...].reshape(1, channels)

    def dot(f, weights):
        return jnp.dot(cols[f, :flat_out], weights, preferred_element_type=jnp.float32)

    for f in range(0, count, 2):
        pair = dot(f + 1, both_1) + dot(f + 2, both_2)
        first = pair[:, :channels] + dot(f, w0)
        second = pair[:, channels:] + dot(f + 3, w2)
        for g, value in ((f, first), (f + 1, second)):
            new = value + bias + held[g, wide + 1 : wide + 1 + flat_out]
            made[g, :flat_out] = new.astype(jnp.bfloat16).astype(jnp.float32)
    edge = halo - tick - 1
    sums, squares = [], []
    for f in range(count):
        if next_ref is not None:
            next_ref[f] = made[f, :flat_out].astype(jnp.bfloat16)
        total_f = jnp.zeros((1, channels), jnp.float32)
        square_f = jnp.zeros((1, channels), jnp.float32)
        for y in range(side):
            at = (y + edge) * wide + edge
            row = made[f, at : at + side]
            if out_sums_ref is not None:
                total_f = total_f + jnp.sum(row, axis=0, keepdims=True)
                square_f = square_f + jnp.sum(row * row, axis=0, keepdims=True)
            row = row.astype(jnp.bfloat16)
            if kept_ref is not None:
                row = jnp.where(mine == 1, row, kept_ref[f, y])
            result_ref[f, y] = row
        sums.append(total_f)
        squares.append(square_f)
    if out_sums_ref is not None:
        out_sums_ref[0:1, :] = packed(jnp.concatenate(sums, axis=0), members)
        out_sums_ref[1:2, :] = packed(jnp.concatenate(squares, axis=0), members)


def section_step(shape, tick, place, x, sums, cache, kernel, bias, gain, offset, kept):
    count, context, side, wide, sections, pixels, members = shape
    channels = x.shape[-1]
    rows_out = wide - 2 * tick - 2
    last = tick == sections - 1
    vmem = pl.BlockSpec(memory_space=pltpu.VMEM)
    inputs = [place, x, sums, cache, kernel, bias, gain, offset]
    if kept is not None:
        inputs.append(kept)
    outs = [jax.ShapeDtypeStruct((count, side, side, channels), jnp.bfloat16)]
    if not last:
        outs.insert(0, jax.ShapeDtypeStruct((count, rows_out * wide, channels), jnp.bfloat16))
        outs.append(jax.ShapeDtypeStruct((2, channels), jnp.float32))

    def body(*refs):
        refs = list(refs)
        given = refs[:8]
        del refs[:8]
        kept_ref = refs.pop(0) if kept is not None else None
        next_ref = refs.pop(0) if not last else None
        result_ref = refs.pop(0)
        out_sums_ref = refs.pop(0) if not last else None
        section_kernel(shape, tick, *given, kept_ref, next_ref, result_ref, out_sums_ref, *refs)

    full = wide * wide + 8
    return pl.pallas_call(
        body,
        out_shape=tuple(outs),
        in_specs=[pl.BlockSpec(memory_space=pltpu.SMEM)] + [vmem] * (len(inputs) - 1),
        out_specs=tuple([vmem] * len(outs)),
        scratch_shapes=[
            pltpu.VMEM((context + count, full, channels), jnp.float32),
            pltpu.VMEM((count, full, channels), jnp.float32),
            pltpu.VMEM((context + count, rows_out * wide, TAPS * TAPS * channels), jnp.bfloat16),
            pltpu.VMEM((count, rows_out * wide, channels), jnp.float32),
        ],
        name=f"section_{tick}",
    )(*inputs)


def local(frames, cache, conv_weight, conv_bias, norm_gain, norm_bias):
    sections = lax.axis_size("section")
    tiles = lax.axis_size("tile")
    across = min(8, tiles // 2)
    down = tiles // across
    position = lax.axis_index("section")
    placed = (lax.axis_index("tile") + across + 2) % tiles
    column, row_at = placed % across, placed // across
    x = frames[:, 0]
    count, side, _, channels = x.shape
    members = channels // GROUPS
    halo = sections
    wide = side + 2 * halo
    pixels = float(side * side * members * tiles)
    shape = (count, cache.shape[1], side, wide, sections, pixels, members)
    near = [[across * g + j for j in range(across)] for g in range(down)]
    far = [[g + across * j for j in range(down)] for g in range(across)]

    seq = jnp.concatenate([cache[0, :, 0], x], axis=0)
    left = shifted(seq[:, :, side - halo :], 1)
    right = shifted(seq[:, :, :halo], -1)
    sums = summed(first_sums(x, members), near)
    seq = jnp.concatenate([left, seq, right], axis=2)
    above = shifted(seq[:, side - halo :], across)
    below = shifted(seq[:, :halo], -across)
    sums = lax.all_gather(sums, "tile", axis_index_groups=far)
    seq = jnp.concatenate([above, seq, below], axis=1).reshape(seq.shape[0], wide * wide, channels)
    held_cache, x = seq[: cache.shape[1]], seq[cache.shape[1] :]

    flags = [row_at == 0, row_at == down - 1, column == 0, column == across - 1]
    kernel = conv_weight[0].reshape(TAPS, TAPS * TAPS * channels, channels)
    result = None
    for tick in range(sections):
        place = jnp.stack(flags + [position == tick]).astype(jnp.int32)
        made = section_step(
            shape, tick, place, x, sums, held_cache, kernel, conv_bias, norm_gain, norm_bias, result
        )
        if tick + 1 == sections:
            (result,) = made
            break
        x, result, sums = made
        hop = [(tick, tick + 1)]
        sums = lax.ppermute(sums, "section", hop)
        x = lax.ppermute(x, "section", hop)
        sums = summed(sums, near)
        sums = lax.all_gather(sums, "tile", axis_index_groups=far)
    return result[None, :, None]


def solution(mesh):
    placed = (
        P("parts", "tile", None, None, None),
        P("section", "parts", "tile", None, None, None),
        P("section", None, None, None, None, None),
        P("section", None),
        P("section", None),
        P("section", None),
    )
    return jax.shard_map(
        local,
        mesh=mesh,
        in_specs=placed,
        out_specs=P("section", "parts", "tile", None, None, None),
        check_vma=False,
    )
```

time: 316 us -> 251 us (0.79)
  the two profiles are of different devices: /device:TPU:42 before, /device:TPU:46 now
where the time goes in v1:
time: 251 us; the launch traced here: 250 us
  blocking collectives  132 us (53%)
  starting transfers between devices  58.1 us (23%)
  waiting for transfers between devices  26.7 us (11%)
  Pallas kernels  23.4 us (9%)
  other arithmetic  5.57 us (2%)
  local copies, waits for them, and re-layouts  3.68 us (1%)
    all_gather x4, blocking collectives, local(): sums = lax.all_gather(sums, 'tile', axis_index_groups=far)  93.6 us
    ppermute x4, starting transfers between devices, shifted(): lax.ppermute(array, 'tile', [(i, (i + by) % peers) for i in range(peers)])  52.8 us
    all_gather x4, blocking collectives, summed(): lax.all_gather(array, 'tile', axis_index_groups=groups)  38.9 us
    ppermute x3, waiting for transfers between devices, local(): sums = lax.ppermute(sums, 'section', hop)  24.4 us
    pallas_call x4, Pallas kernels, section_step(): pl.pallas_call(body, out_shape=tuple(outs), in_specs=[pl.BlockSpec(memory...  21.6 us
  transfers between devices with their start and end apart: 10, of which 2 were waited for; matrix products, arithmetic and copies ran while one was open for 1% of the time, Pallas kernels for 1%

profile of v1, /device:TPU:46, one launch (start us, length us, event | category | flops | bytes accessed | tf_op | source)
XLA Modules:
  0.0 250.1 jit_solution(14695486135330625910)
XLA Ops:
  0.0 1.1 pad_maximum_fusion.7
  1.1 0.1 collective-permute-start
  1.2 43.0 %collective-permute-start.1 = (bf16[6,16,4,128]{3,2,1,0:T(4,128)(2,1)S(1)}, bf16[6,16,4,128]{3,2,1,0:T(4,128)(2,1)S(1)}, u32[]{:S(2)}, u32[]{:S(2)}) collective-permute-start(bf16[6,16,4,128]{3,2,1,0:T(4,128)(2,1)S(1)} %get-tuple-element.26), channel_id=1, source_target_pairs={{0,63},{1,0},{2,1},{3,2},{4,3},{5,4},{6,5},{7,6},{8,7},{9,8},{10,9... | collective-permute-start | bytes 294920 | tf_op jit(solution)/shard_map/ppermute | solution.py:17
  44.2 2.2 collective-permute-done
  46.4 1.0 pad_maximum_fusion.5
  47.4 2.0 collective-permute-start.2
  49.4 7.9 %collective-permute-start.3 = (bf16[6,4,24,128]{3,2,1,0:T(8,128)(2,1)S(1)}, bf16[6,4,24,128]{3,2,1,0:T(8,128)(2,1)S(1)}, u32[]{:S(2)}, u32[]{:S(2)}) collective-permute-start(bf16[6,4,24,128]{3,2,1,0:T(8,128)(2,1)S(1)} %get-tuple-element.24), channel_id=1, source_target_pairs={{0,56},{1,57},{2,58},{3,59},{4,60},{5,61},{6,62},{7,63},{8,0},{9,1... | collective-permute-start | bytes 442376 | tf_op jit(solution)/shard_map/ppermute | solution.py:17
  57.3 1.7 shard_map.64
  59.1 0.1 stack.59
  59.2 0.5 convert_element_type.15.refs_0_
  59.7 8.9 %all-gather.8 = f32[8,2,128]{2,1,0:T(2,128)S(1)} all-gather(f32[1,2,128]{2,1,0:T(2,128)} %bitcast.42), channel_id=2, replica_groups={{0,1,2,3,4,5,6,7},{8,9,10,11,12,13,14,15},{16,17,18,19,20,21,22,23},{24..., dimensions={0}, use_global_device_ids=true | all-gather | bytes 9216 | tf_op jit(solution)/shard_map/all_gather | solution.py:21
  68.6 27.0 %all-gather.9.refs_2_ = f32[8,2,128]{2,1,0:T(2,128)} all-gather(f32[1,2,128]{2,1,0:T(2,128)S(1)} %bitcast.44), channel_id=3, replica_groups={{0,8,16,24,32,40,48,56},{1,9,17,25,33,41,49,57},{2,10,18,26,34,42,50,58..., dimensions={0}, use_global_device_ids=true | all-gather | bytes 9216 | tf_op jit(solution)/shard_map/all_gather | solution.py:223
  95.6 0.0 collective-permute-done.2
  95.6 0.0 collective-permute-done.3
  95.7 0.3 pad_maximum_fusion
  96.0 0.9 slice.32
  96.9 0.8 pad_maximum_fusion.1
  97.7 5.9 %section_0.1 = (bf16[4,528,128]{2,1,0:T(8,128)(2,1)}, bf16[4,16,16,128]{3,2,1,0:T(8,128)(2,1)}, f32[2,128]{1,0:T(2,128)}) custom-call(s32[5]{0:T(128)} %convert_element_type.15.refs_0_, bf16[4,576,128]{2,1,0:T(8,128)(2,1)} %bitcast.37, f32[8,2,128]{2,1,0:T(2,128)} %all-gather.9.refs_2_, bf16[2,576,128]{2,1,0:T(8,128)(2,1)} %bitcast.28, ...), custom_call_target="tpu_custom_call" | custom-call | tf_op jit(solution)/shard_map/section_0/pallas_call | solution.py:183
  103.6 0.7 collective-permute-start.4
  104.3 0.7 collective-permute-start.5
  105.0 0.1 stack.57
  105.1 0.5 convert_element_type.14.refs_0_
  105.6 0.0 collective-permute-done.5
  105.6 11.0 %all-gather.10 = f32[8,2,128]{2,1,0:T(2,128)S(1)} all-gather(f32[1,2,128]{2,1,0:T(2,128)S(1)} %bitcast.48), channel_id=4, replica_groups={{0,1,2,3,4,5,6,7},{8,9,10,11,12,13,14,15},{16,17,18,19,20,21,22,23},{24..., dimensions={0}, use_global_device_ids=true | all-gather | bytes 9216 | tf_op jit(solution)/shard_map/all_gather | solution.py:21
  116.7 19.9 %all-gather.11.refs_2_ = f32[8,2,128]{2,1,0:T(2,128)} all-gather(f32[1,2,128]{2,1,0:T(2,128)S(1)} %bitcast.45), channel_id=5, replica_groups={{0,8,16,24,32,40,48,56},{1,9,17,25,33,41,49,57},{2,10,18,26,34,42,50,58..., dimensions={0}, use_global_device_ids=true | all-gather | bytes 9216 | tf_op jit(solution)/shard_map/all_gather | solution.py:243
  136.6 0.0 collective-permute-done.4.refs_1_
  136.6 0.8 copy-done.2
  137.4 5.6 %section_1.1 = (bf16[4,480,128]{2,1,0:T(8,128)(2,1)}, bf16[4,16,16,128]{3,2,1,0:T(8,128)(2,1)}, f32[2,128]{1,0:T(2,128)}) custom-call(s32[5]{0:T(128)} %convert_element_type.14.refs_0_, bf16[4,528,128]{2,1,0:T(8,128)(2,1)} %copy-done.2, f32[8,2,128]{2,1,0:T(2,128)} %all-gather.11.refs_2_, bf16[2,576,128]{2,1,0:T(8,128)(2,1)} %bitcast.29, ...), custom_call_target="tpu_custom_call" | custom-call | tf_op jit(solution)/shard_map/section_1/pallas_call | solution.py:183
  143.0 0.7 collective-permute-start.6
  143.7 0.7 collective-permute-start.7
  144.3 0.1 stack.55
  144.4 0.5 convert_element_type.13.refs_0_
  145.0 0.0 collective-permute-done.7
  145.0 8.6 %all-gather.12 = f32[8,2,128]{2,1,0:T(2,128)S(1)} all-gather(f32[1,2,128]{2,1,0:T(2,128)S(1)} %bitcast.49), channel_id=6, replica_groups={{0,1,2,3,4,5,6,7},{8,9,10,11,12,13,14,15},{16,17,18,19,20,21,22,23},{24..., dimensions={0}, use_global_device_ids=true | all-gather | bytes 9216 | tf_op jit(solution)/shard_map/all_gather | solution.py:21
  153.6 25.8 %all-gather.13.refs_2_ = f32[8,2,128]{2,1,0:T(2,128)} all-gather(f32[1,2,128]{2,1,0:T(2,128)S(1)} %bitcast.46), channel_id=7, replica_groups={{0,8,16,24,32,40,48,56},{1,9,17,25,33,41,49,57},{2,10,18,26,34,42,50,58..., dimensions={0}, use_global_device_ids=true | all-gather | bytes 9216 | tf_op jit(solution)/shard_map/all_gather | solution.py:243
  179.4 0.0 collective-permute-done.6.refs_1_
  179.4 0.8 copy-done.3
  180.2 5.4 %section_2.1 = (bf16[4,432,128]{2,1,0:T(8,128)(2,1)}, bf16[4,16,16,128]{3,2,1,0:T(8,128)(2,1)}, f32[2,128]{1,0:T(2,128)}) custom-call(s32[5]{0:T(128)} %convert_element_type.13.refs_0_, bf16[4,480,128]{2,1,0:T(8,128)(2,1)} %copy-done.3, f32[8,2,128]{2,1,0:T(2,128)} %all-gather.13.refs_2_, bf16[2,576,128]{2,1,0:T(8,128)(2,1)} %bitcast.30, ...), custom_call_target="tpu_custom_call" | custom-call | tf_op jit(solution)/shard_map/section_2/pallas_call | solution.py:183
  185.6 1.3 collective-permute-start.8
  186.9 1.3 collective-permute-start.9
  188.2 0.1 stack.53
  188.3 0.6 convert_element_type.12.refs_0_
  188.9 24.4 %collective-permute-done.9 = f32[2,128]{1,0:T(2,128)S(1)} collective-permute-done((f32[2,128]{1,0:T(2,128)}, f32[2,128]{1,0:T(2,128)S(1)}, u32[]{:S(2)}, u32[]{:S(2)}) %collective-permute-start.9) | collective-permute-done | bytes 1056 | tf_op jit(solution)/shard_map/ppermute | solution.py:240
  213.3 10.4 %all-gather.14 = f32[8,2,128]{2,1,0:T(2,128)S(1)} all-gather(f32[1,2,128]{2,1,0:T(2,128)S(1)} %bitcast.47), channel_id=8, replica_groups={{0,1,2,3,4,5,6,7},{8,9,10,11,12,13,14,15},{16,17,18,19,20,21,22,23},{24..., dimensions={0}, use_global_device_ids=true | all-gather | bytes 9216 | tf_op jit(solution)/shard_map/all_gather | solution.py:21
  223.7 20.9 %all-gather.15.refs_2_ = f32[8,2,128]{2,1,0:T(2,128)} all-gather(f32[1,2,128]{2,1,0:T(2,128)S(1)} %bitcast.43), channel_id=9, replica_groups={{0,8,16,24,32,40,48,56},{1,9,17,25,33,41,49,57},{2,10,18,26,34,42,50,58..., dimensions={0}, use_global_device_ids=true | all-gather | bytes 9216 | tf_op jit(solution)/shard_map/all_gather | solution.py:243
  244.6 0.0 collective-permute-done.8.refs_1_
  244.6 0.7 copy-done.4
  245.3 4.8 %section_3.1 = bf16[4,16,16,128]{3,2,1,0:T(8,128)(2,1)} custom-call(s32[5]{0:T(128)} %convert_element_type.12.refs_0_, bf16[4,432,128]{2,1,0:T(8,128)(2,1)} %copy-done.4, f32[8,2,128]{2,1,0:T(2,128)} %all-gather.15.refs_2_, bf16[2,576,128]{2,1,0:T(8,128)(2,1)} %bitcast.31, bf16[3,1152,128]{2,1,0:T(8,128)(2,1)} %bitcast.27, f32[1,128]{1,0:T(1,128)} %refs_5_.7, ...), custom_call_target="tpu_custom_call" | custom-call | tf_op jit(solution)/shard_map/section_3/pallas_call | solution.py:183
  (12 shorter events, 0.1 us)
Async XLA Ops:
  0.0 95.6 %copy-start = (bf16[4,1,16,16,128]{4,3,2,1,0:T(8,128)(2,1)S(1)}, bf16[4,1,16,16,128]{4,3,2,1,0:T(8,128)(2,1)}, u32[]{:S(2)}) copy-start(bf16[4,1,16,16,128]{4,3,2,1,0:T(8,128)(2,1)} %param.6) | copy-start | bytes 786436
  0.0 95.7 %copy-start.1 = (bf16[1,2,1,16,16,128]{5,4,3,2,1,0:T(8,128)(2,1)S(1)}, bf16[1,2,1,16,16,128]{5,4,3,2,1,0:T(8,128)(2,1)}, u32[]{:S(2)}) copy-start(bf16[1,2,1,16,16,128]{5,4,3,2,1,0:T(8,128)(2,1)} %param.7) | copy-start | bytes 393220
  1.1 45.3 %collective-permute-start = (bf16[6,16,4,128]{3,2,1,0:T(4,128)(2,1)S(1)}, bf16[6,16,4,128]{3,2,1,0:T(4,128)(2,1)S(1)}, u32[]{:S(2)}, u32[]{:S(2)}) collective-permute-start(bf16[6,16,4,128]{3,2,1,0:T(4,128)(2,1)S(1)} %get-tuple-element.25), channel_id=1, source_target_pairs={{0,1},{1,2},{2,3},{3,4},{4,5},{5,6},{6,7},{7,8},{8,9},{9,10},{10,1... | collective-permute-start | bytes 294920 | tf_op jit(solution)/shard_map/ppermute | solution.py:17
  1.2 45.2 %collective-permute-start.1 = (bf16[6,16,4,128]{3,2,1,0:T(4,128)(2,1)S(1)}, bf16[6,16,4,128]{3,2,1,0:T(4,128)(2,1)S(1)}, u32[]{:S(2)}, u32[]{:S(2)}) collective-permute-start(bf16[6,16,4,128]{3,2,1,0:T(4,128)(2,1)S(1)} %get-tuple-element.26), channel_id=1, source_target_pairs={{0,63},{1,0},{2,1},{3,2},{4,3},{5,4},{6,5},{7,6},{8,7},{9,8},{10,9... | collective-permute-start | bytes 294920 | tf_op jit(solution)/shard_map/ppermute | solution.py:17
  47.4 48.2 %collective-permute-start.2 = (bf16[6,4,24,128]{3,2,1,0:T(8,128)(2,1)S(1)}, bf16[6,4,24,128]{3,2,1,0:T(8,128)(2,1)S(1)}, u32[]{:S(2)}, u32[]{:S(2)}) collective-permute-start(bf16[6,4,24,128]{3,2,1,0:T(8,128)(2,1)S(1)} %get-tuple-element.23), channel_id=1, source_target_pairs={{0,8},{1,9},{2,10},{3,11},{4,12},{5,13},{6,14},{7,15},{8,16},{9,17... | collective-permute-start | bytes 442376 | tf_op jit(solution)/shard_map/ppermute | solution.py:17
  49.4 46.2 %collective-permute-start.3 = (bf16[6,4,24,128]{3,2,1,0:T(8,128)(2,1)S(1)}, bf16[6,4,24,128]{3,2,1,0:T(8,128)(2,1)S(1)}, u32[]{:S(2)}, u32[]{:S(2)}) collective-permute-start(bf16[6,4,24,128]{3,2,1,0:T(8,128)(2,1)S(1)} %get-tuple-element.24), channel_id=1, source_target_pairs={{0,56},{1,57},{2,58},{3,59},{4,60},{5,61},{6,62},{7,63},{8,0},{9,1... | collective-permute-start | bytes 442376 | tf_op jit(solution)/shard_map/ppermute | solution.py:17
  103.6 32.9 %collective-permute-start.4 = (bf16[4,528,128]{2,1,0:T(8,128)(2,1)}, bf16[4,528,128]{2,1,0:T(8,128)(2,1)S(1)}, u32[]{:S(2)}, u32[]{:S(2)}) collective-permute-start(bf16[4,528,128]{2,1,0:T(8,128)(2,1)} %get-tuple-element.14), channel_id=1, source_target_pairs={{0,64},{1,65},{2,66},{3,67},{4,68},{5,69},{6,70},{7,71},{8,72},{9,... | collective-permute-start | bytes 1622024 | tf_op jit(solution)/shard_map/ppermute | solution.py:241
  104.3 1.3 collective-permute-start.5
  136.6 0.8 copy-start.2
  143.0 36.4 %collective-permute-start.6 = (bf16[4,480,128]{2,1,0:T(8,128)(2,1)}, bf16[4,480,128]{2,1,0:T(8,128)(2,1)S(1)}, u32[]{:S(2)}, u32[]{:S(2)}) collective-permute-start(bf16[4,480,128]{2,1,0:T(8,128)(2,1)} %get-tuple-element.17), channel_id=1, source_target_pairs={{64,128},{65,129},{66,130},{67,131},{68,132},{69,133},{70,134},{71... | collective-permute-start | bytes 1474568 | tf_op jit(solution)/shard_map/ppermute | solution.py:241
  143.7 1.3 collective-permute-start.7
  179.4 0.8 copy-start.3
  185.6 59.0 %collective-permute-start.8 = (bf16[4,432,128]{2,1,0:T(8,128)(2,1)}, bf16[4,432,128]{2,1,0:T(8,128)(2,1)S(1)}, u32[]{:S(2)}, u32[]{:S(2)}) collective-permute-start(bf16[4,432,128]{2,1,0:T(8,128)(2,1)} %get-tuple-element.20), channel_id=1, source_target_pairs={{128,192},{129,193},{130,194},{131,195},{132,196},{133,197},{134,1... | collective-permute-start | bytes 1327112 | tf_op jit(solution)/shard_map/ppermute | solution.py:241
  186.9 26.4 %collective-permute-start.9 = (f32[2,128]{1,0:T(2,128)}, f32[2,128]{1,0:T(2,128)S(1)}, u32[]{:S(2)}, u32[]{:S(2)}) collective-permute-start(f32[2,128]{1,0:T(2,128)} %get-tuple-element.21), channel_id=1, source_target_pairs={{128,192},{129,193},{130,194},{131,195},{132,196},{133,197},{134,1... | collective-permute-start | bytes 3080 | tf_op jit(solution)/shard_map/ppermute | solution.py:240
  244.6 0.8 copy-start.4

commit v2 on v1

v2 whole, which is shorter than its diff:
```python
import functools

import jax
import jax.numpy as jnp
from jax import lax
from jax.experimental import pallas as pl
from jax.experimental.pallas import tpu as pltpu
from jax.sharding import PartitionSpec as P

GROUPS = 32
EPSILON = 1e-06
TAPS = 3
VMEM_LIMIT = 20 * 1024 * 1024


def shifted(array, by):
    peers = lax.axis_size("tile")
    return lax.ppermute(array, "tile", [(i, (i + by) % peers) for i in range(peers)])


def of_everyone(sums):
    peers = lax.axis_size("tile")
    copies = jnp.broadcast_to(sums.reshape(1, 1, sums.size), (peers, 1, sums.size))
    return jnp.sum(lax.all_to_all(copies, "tile", 0, 0, tiled=True), axis=0).reshape(sums.shape)


def over_lanes(value, members):
    lanes = value.shape[-1]
    lane = lax.broadcasted_iota(jnp.int32, value.shape, value.ndim - 1)
    step = 1
    while step < members:
        up = pltpu.roll(value, lanes - step, value.ndim - 1)
        down = pltpu.roll(value, step, value.ndim - 1)
        value = value + jnp.where((lane // step) % 2 == 0, up, down)
        step *= 2
    return value


def packed(totals, members):
    totals = over_lanes(totals, members)
    lane = lax.broadcasted_iota(jnp.int32, (1, totals.shape[-1]), 1)
    row = jnp.zeros((1, totals.shape[-1]), jnp.float32)
    for frame in range(totals.shape[0]):
        row = row + jnp.where(lane % members == frame, totals[frame : frame + 1], 0.0)
    return row


def unpacked(row, frame, members):
    lane = lax.broadcasted_iota(jnp.int32, row.shape, 1)
    return over_lanes(jnp.where(lane % members == frame, row, 0.0), members)


def sums_kernel(members, x_ref, sums_ref):
    values = x_ref[...].astype(jnp.float32)
    count = values.shape[0]
    values = values.reshape(count, -1, values.shape[-1])
    sums_ref[0:1, :] = packed(jnp.sum(values, axis=1), members)
    sums_ref[1:2, :] = packed(jnp.sum(values * values, axis=1), members)


def first_sums(frames, members):
    return pl.pallas_call(
        functools.partial(sums_kernel, members),
        out_shape=jax.ShapeDtypeStruct((2, frames.shape[-1]), jnp.float32),
        in_specs=[pl.BlockSpec(memory_space=pltpu.VMEM)],
        out_specs=pl.BlockSpec(memory_space=pltpu.VMEM),
    )(frames)


def masked(flags, edge, rows, wide, side, channels):
    first_row, last_row, first_col, last_col = flags
    row = lax.broadcasted_iota(jnp.int32, (rows, wide, channels), 0)
    col = lax.broadcasted_iota(jnp.int32, (rows, wide, channels), 1)
    far = edge + side
    low_r = jnp.where(first_row == 1, edge, 0)
    high_r = jnp.where(last_row == 1, far, far + edge)
    low_c = jnp.where(first_col == 1, edge, 0)
    high_c = jnp.where(last_col == 1, far, far + edge)
    return (row >= low_r) & (row < high_r) & (col >= low_c) & (col < high_c)


def unfold(act, cols, frame, wide, rows, channels):
    for dy in range(TAPS):
        for dx in range(TAPS):
            at = dy * wide + dx
            tap = (dy * TAPS + dx) * channels
            cols[frame, :rows, tap : tap + channels] = act[frame, at : at + rows].astype(jnp.bfloat16)


def matmul(cols, frame, rows, weights):
    return jnp.dot(cols[frame, :rows], weights, preferred_element_type=jnp.float32)


def context_kernel(side, wide, place_ref, cache_ref, kernel_ref, bias_ref, part_ref, act, cols):
    context = cache_ref.shape[0]
    channels = cache_ref.shape[-1]
    flags = [place_ref[i] for i in range(4)]
    valid = masked(flags, (wide - side) // 2, wide, wide, side, channels)
    rows = (wide - 2) * wide
    for f in range(context):
        values = cache_ref[f].astype(jnp.float32).reshape(wide, wide, channels)
        act[f, : wide * wide] = jnp.where(valid, values, 0.0).reshape(wide * wide, channels)
        act[f, wide * wide :] = jnp.zeros((act.shape[1] - wide * wide, channels), jnp.float32)
        unfold(act, cols, f, wide, rows, channels)
    w0, w1 = kernel_ref[0], kernel_ref[1]
    bias = bias_ref[...].reshape(1, channels)
    pair = matmul(cols, 1, rows, jnp.concatenate([w1, w0], axis=1))
    part_ref[0] = pair[:, :channels] + matmul(cols, 0, rows, w0) + bias
    part_ref[1] = pair[:, channels:] + bias


def context_part(side, wide, place, cache, kernel, bias):
    channels = cache.shape[-1]
    vmem = pl.BlockSpec(memory_space=pltpu.VMEM)
    rows = (wide - 2) * wide
    return pl.pallas_call(
        functools.partial(context_kernel, side, wide),
        out_shape=jax.ShapeDtypeStruct((2, rows, channels), jnp.float32),
        in_specs=[pl.BlockSpec(memory_space=pltpu.SMEM), vmem, vmem, vmem],
        out_specs=vmem,
        scratch_shapes=[
            pltpu.VMEM((cache.shape[0], wide * wide + 8, channels), jnp.float32),
            pltpu.VMEM((cache.shape[0], rows, TAPS * TAPS * channels), jnp.bfloat16),
        ],
        compiler_params=pltpu.CompilerParams(vmem_limit_bytes=VMEM_LIMIT),
        name="context",
    )(place, cache, kernel, bias)


def section_kernel(
    shape, tick, place_ref, x_ref, sums_ref, part_ref, kernel_ref, bias_ref, gain_ref, offset_ref,
    kept_ref, next_ref, result_ref, out_sums_ref, act, held, cols, made,
):
    count, side, wide, sections, pixels, members = shape
    rows_in = wide - 2 * tick
    rows_out = rows_in - 2
    channels = x_ref.shape[-1]
    flat_in = rows_in * wide
    flat_out = rows_out * wide
    halo = (wide - side) // 2
    flags = [place_ref[i] for i in range(4)]
    position = place_ref[4]
    mean_row = sums_ref[0:1] / pixels
    square_row = sums_ref[1:2] / pixels
    valid = masked(flags, halo - tick, rows_in, wide, side, channels)
    gain = gain_ref[...].reshape(1, channels)
    offset = offset_ref[...].reshape(1, channels)
    for f in range(count):
        mean = unpacked(mean_row, f, members)
        variance = jnp.maximum(unpacked(square_row, f, members) - mean * mean, 0.0)
        scale = gain / jnp.sqrt(variance + EPSILON)
        values = x_ref[f].astype(jnp.float32)
        held[f, :flat_in] = values
        normed = (values - mean) * scale + offset
        half = 0.5 * normed
        active = (half + half * jnp.tanh(half)).reshape(rows_in, wide, channels)
        active = jnp.where(valid, active, 0.0).reshape(flat_in, channels)
        act[f, :flat_in] = active
        unfold(act, cols, f, wide, flat_out, channels)
    w0, w1, w2 = (kernel_ref[i] for i in range(TAPS))
    both_1 = jnp.concatenate([w1, w0], axis=1)
    both_2 = jnp.concatenate([w2, w1], axis=1)
    bias = bias_ref[...].reshape(1, channels)
    base = tick * (wide + 1)

    def finish(g, value):
        new = value + held[g, wide + 1 : wide + 1 + flat_out]
        made[g, :flat_out] = new.astype(jnp.bfloat16).astype(jnp.float32)

    for f in range(0, count, 2):
        pair = matmul(cols, f, flat_out, both_2)
        first = pair[:, :channels]
        second = pair[:, channels:] + matmul(cols, f + 1, flat_out, w2)
        if f == 0:
            finish(f, first + part_ref[0, base : base + flat_out])
            finish(f + 1, second + part_ref[1, base : base + flat_out])
        else:
            pair = matmul(cols, f - 1, flat_out, both_1)
            first = first + pair[:, :channels] + matmul(cols, f - 2, flat_out, w0)
            finish(f, first + bias)
            finish(f + 1, second + pair[:, channels:] + bias)
    edge = halo - tick - 1
    sums, squares = [], []
    for f in range(count):
        if next_ref is not None:
            next_ref[f] = made[f, :flat_out].astype(jnp.bfloat16)
        total_f = jnp.zeros((side, channels), jnp.float32)
        square_f = jnp.zeros((side, channels), jnp.float32)
        for y in range(side):
            at = (y + edge) * wide + edge
            row = made[f, at : at + side]
            if out_sums_ref is not None:
                total_f = total_f + row
                square_f = square_f + row * row
            row = row.astype(jnp.bfloat16)
            if kept_ref is not None:
                row = jnp.where(position == tick, row, kept_ref[f, y])
            result_ref[f, y] = row
        sums.append(jnp.sum(total_f, axis=0, keepdims=True))
        squares.append(jnp.sum(square_f, axis=0, keepdims=True))
    if out_sums_ref is not None:
        out_sums_ref[0:1, :] = packed(jnp.concatenate(sums, axis=0), members)
        out_sums_ref[1:2, :] = packed(jnp.concatenate(squares, axis=0), members)


def section_step(shape, tick, place, x, sums, part, kernel, bias, gain, offset, kept):
    count, side, wide, sections, pixels, members = shape
    channels = x.shape[-1]
    rows_out = wide - 2 * tick - 2
    last = tick == sections - 1
    vmem = pl.BlockSpec(memory_space=pltpu.VMEM)
    inputs = [place, x, sums, part, kernel, bias, gain, offset]
    if kept is not None:
        inputs.append(kept)
    outs = [jax.ShapeDtypeStruct((count, side, side, channels), jnp.bfloat16)]
    if not last:
        outs.insert(0, jax.ShapeDtypeStruct((count, rows_out * wide, channels), jnp.bfloat16))
        outs.append(jax.ShapeDtypeStruct((2, channels), jnp.float32))

    def body(*refs):
        refs = list(refs)
        given = refs[:8]
        del refs[:8]
        kept_ref = refs.pop(0) if kept is not None else None
        next_ref = refs.pop(0) if not last else None
        result_ref = refs.pop(0)
        out_sums_ref = refs.pop(0) if not last else None
        section_kernel(shape, tick, *given, kept_ref, next_ref, result_ref, out_sums_ref, *refs)

    full = wide * wide + 8
    return pl.pallas_call(
        body,
        out_shape=tuple(outs),
        in_specs=[pl.BlockSpec(memory_space=pltpu.SMEM)] + [vmem] * (len(inputs) - 1),
        out_specs=tuple([vmem] * len(outs)),
        scratch_shapes=[
            pltpu.VMEM((count, full, channels), jnp.float32),
            pltpu.VMEM((count, full, channels), jnp.float32),
            pltpu.VMEM((count, rows_out * wide, TAPS * TAPS * channels), jnp.bfloat16),
            pltpu.VMEM((count, rows_out * wide, channels), jnp.float32),
        ],
        compiler_params=pltpu.CompilerParams(vmem_limit_bytes=VMEM_LIMIT),
        name=f"section_{tick}",
    )(*inputs)


def local(frames, cache, conv_weight, conv_bias, norm_gain, norm_bias):
    sections = lax.axis_size("section")
    tiles = lax.axis_size("tile")
    across = min(8, tiles // 2)
    down = tiles // across
    position = lax.axis_index("section")
    placed = (lax.axis_index("tile") + across + 2) % tiles
    column, row_at = placed % across, placed // across
    x = frames[:, 0]
    count, side, _, channels = x.shape
    members = channels // GROUPS
    halo = sections
    wide = side + 2 * halo
    pixels = float(side * side * members * tiles)
    shape = (count, side, wide, sections, pixels, members)
    flags = [row_at == 0, row_at == down - 1, column == 0, column == across - 1]
    place = jnp.stack([f.astype(jnp.int32) for f in flags] + [position.astype(jnp.int32)])
    kernel = conv_weight[0].reshape(TAPS, TAPS * TAPS * channels, channels)

    old = cache[0, :, 0]
    sums = first_sums(x, members)
    sums, seq = lax.optimization_barrier((sums, jnp.concatenate([old, x], axis=0)))
    sums = of_everyone(sums)
    left = shifted(seq[:, :, side - halo :], 1)
    right = shifted(seq[:, :, :halo], -1)
    middle = jnp.concatenate([left, seq, right], axis=2)
    above = shifted(middle[:, side - halo :], across)
    below = shifted(middle[:, :halo], -across)
    whole = jnp.concatenate([above, middle, below], axis=1)
    whole = whole.reshape(whole.shape[0], wide * wide, channels)
    context = old.shape[0]
    x = whole[context:]
    part = context_part(side, wide, place, whole[:context], kernel, conv_bias)

    result = None
    for tick in range(sections):
        made = section_step(
            shape, tick, place, x, sums, part, kernel, conv_bias, norm_gain, norm_bias, result
        )
        if tick + 1 == sections:
            (result,) = made
            break
        x, result, sums = made
        hop = [(tick, tick + 1)]
        sums = lax.ppermute(sums, "section", hop)
        sums, x = lax.optimization_barrier((sums, x))
        sums = of_everyone(sums)
        x = lax.ppermute(x, "section", hop)
    return result[None, :, None]


def solution(mesh):
    placed = (
        P("parts", "tile", None, None, None),
        P("section", "parts", "tile", None, None, None),
        P("section", None, None, None, None, None),
        P("section", None),
        P("section", None),
        P("section", None),
    )
    return jax.shard_map(
        local,
        mesh=mesh,
        in_specs=placed,
        out_specs=P("section", "parts", "tile", None, None, None),
        check_vma=False,
    )
```

time: 251 us -> 227 us (0.904)
  blocking collectives: 132 us -> 42.9 us
  waiting for transfers between devices: 26.7 us -> 76.6 us
  starting transfers between devices: 58.1 us -> 84.7 us
  Pallas kernels: 23.4 us -> 16.5 us
  other arithmetic: 5.57 us -> 2.03 us
    all_gather x8 -> x0, blocking collectives: 132 us -> none  [the longest x4 93.6 us: local(): sums = lax.all_gather(sums, 'tile', axis_index_groups=far)]
    all_to_all x0 -> x3, waiting for transfers between devices: none -> 47.7 us  [of_everyone(): lax.all_to_all(copies, 'tile', 0, 0, tiled=True)]
    all_to_all x0 -> x1, blocking collectives: none -> 42.9 us  [of_everyone(): lax.all_to_all(copies, 'tile', 0, 0, tiled=True)]
    all_to_all x0 -> x3, starting transfers between devices: none -> 26.6 us  [of_everyone(): lax.all_to_all(copies, 'tile', 0, 0, tiled=True)]
    ppermute x4, waiting for transfers between devices: 2.25 us -> 18.6 us  [shifted(): lax.ppermute(array, 'tile', [(i, (i + by) % peers) for i in range(peers)])]
    ppermute x3, waiting for transfers between devices: 24.4 us -> 10.2 us  [local(): sums = lax.ppermute(sums, 'section', hop)]
    pallas_call x4, Pallas kernels: 21.6 us -> 13.3 us  [section_step(): pl.pallas_call(body, out_shape=tuple(outs), in_specs=[pl.BlockSpec(memory...]
    slice x3 -> x2, other arithmetic: 2.99 us -> 0.27 us  [the longest x1 0.16 us: local(): above = shifted(middle[:, side - halo:], across)]
  transfers between devices with their start and end apart: 10 -> 13, of which waited for: 2 -> 5; matrix products, arithmetic and copies ran while one was open for 1% -> 1% of each run, Pallas kernels for 1% -> 1%
where the time goes in v2:
time: 227 us; the launch traced here: 226 us
  starting transfers between devices  84.7 us (37%)
  waiting for transfers between devices  76.6 us (34%)
  blocking collectives  42.9 us (19%)
  Pallas kernels  16.5 us (7%)
  local copies, waits for them, and re-layouts  3.32 us (1%)
    ppermute x4, starting transfers between devices, shifted(): lax.ppermute(array, 'tile', [(i, (i + by) % peers) for i in range(peers)])  52.8 us
    all_to_all x3, waiting for transfers between devices, of_everyone(): lax.all_to_all(copies, 'tile', 0, 0, tiled=True)  47.7 us
    all_to_all x1, blocking collectives, of_everyone(): lax.all_to_all(copies, 'tile', 0, 0, tiled=True)  42.9 us
    all_to_all x3, starting transfers between devices, of_everyone(): lax.all_to_all(copies, 'tile', 0, 0, tiled=True)  26.6 us
    ppermute x4, waiting for transfers between devices, shifted(): lax.ppermute(array, 'tile', [(i, (i + by) % peers) for i in range(peers)])  18.6 us
    pallas_call x4, Pallas kernels, section_step(): pl.pallas_call(body, out_shape=tuple(outs), in_specs=[pl.BlockSpec(memory...  13.3 us
    ppermute x3, waiting for transfers between devices, local(): sums = lax.ppermute(sums, 'section', hop)  10.2 us
  transfers between devices with their start and end apart: 13, of which 5 were waited for; matrix products, arithmetic and copies ran while one was open for 1% of the time, Pallas kernels for 1%

profile of v2, /device:TPU:46, one launch (start us, length us, event | category | flops | bytes accessed | tf_op | source)
XLA Modules:
  0.0 226.3 jit_solution(13125049009688012266)
XLA Ops:
  0.0 1.7 shard_map.64
  1.7 1.0 pad_maximum_fusion.1
  2.8 0.1 fusion
  2.9 0.1 collective-permute-start
  2.9 43.0 %collective-permute-start.1 = (bf16[6,16,4,128]{3,2,1,0:T(4,128)(2,1)S(1)}, bf16[6,16,4,128]{3,2,1,0:T(4,128)(2,1)S(1)}, u32[]{:S(2)}, u32[]{:S(2)}) collective-permute-start(bf16[6,16,4,128]{3,2,1,0:T(4,128)(2,1)S(1)} %get-tuple-element.42), channel_id=1, source_target_pairs={{0,63},{1,0},{2,1},{3,2},{4,3},{5,4},{6,5},{7,6},{8,7},{9,8},{10,9... | collective-permute-start | bytes 294920 | tf_op jit(solution)/shard_map/ppermute | solution.py:18
  45.9 0.7 broadcast_in_dim.32
  46.6 6.5 %all-to-all-start = ((f32[64,1,256]{2,1,0:T(1,128)}), f32[64,1,256]{2,1,0:T(1,128)S(1)}, u32[]{:S(2)}, u32[]{:S(2)}) async-start(f32[64,1,256]{2,1,0:T(1,128)} %broadcast_in_dim.32), calls=%async_computation | async-start | bytes 131072 | tf_op jit(solution)/shard_map/all_to_all | solution.py:24
  53.0 0.0 collective-permute-done
  53.1 0.0 collective-permute-done.1
  53.1 0.2 pad_maximum_fusion.5
  53.2 6.4 %collective-permute-start.2 = (bf16[6,4,24,128]{3,2,1,0:T(8,128)(2,1)S(1)}, bf16[6,4,24,128]{3,2,1,0:T(8,128)(2,1)S(1)}, u32[]{:S(2)}, u32[]{:S(2)}) collective-permute-start(bf16[6,4,24,128]{3,2,1,0:T(8,128)(2,1)S(1)} %get-tuple-element.39), channel_id=1, source_target_pairs={{0,8},{1,9},{2,10},{3,11},{4,12},{5,13},{6,14},{7,15},{8,16},{9,17... | collective-permute-start | bytes 442376 | tf_op jit(solution)/shard_map/ppermute | solution.py:18
  59.6 3.5 %collective-permute-start.3 = (bf16[6,4,24,128]{3,2,1,0:T(8,128)(2,1)S(1)}, bf16[6,4,24,128]{3,2,1,0:T(8,128)(2,1)S(1)}, u32[]{:S(2)}, u32[]{:S(2)}) collective-permute-start(bf16[6,4,24,128]{3,2,1,0:T(8,128)(2,1)S(1)} %get-tuple-element.40), channel_id=1, source_target_pairs={{0,56},{1,57},{2,58},{3,59},{4,60},{5,61},{6,62},{7,63},{8,0},{9,1... | collective-permute-start | bytes 442376 | tf_op jit(solution)/shard_map/ppermute | solution.py:18
  63.1 0.1 stack.39.place_ref.refs_0_
  63.2 12.0 %collective-permute-done.2 = bf16[6,4,24,128]{3,2,1,0:T(8,128)(2,1)S(1)} collective-permute-done((bf16[6,4,24,128]{3,2,1,0:T(8,128)(2,1)S(1)}, bf16[6,4,24,128]{3,2,1,0:T(8,128)(2,1)S(1)}, u32[]{:S(2)}, u32[]{:S(2)}) %collective-permute-start.2) | collective-permute-done | bytes 147488 | tf_op jit(solution)/shard_map/ppermute | solution.py:18
  75.2 6.6 %collective-permute-done.3 = bf16[6,4,24,128]{3,2,1,0:T(8,128)(2,1)S(1)} collective-permute-done((bf16[6,4,24,128]{3,2,1,0:T(8,128)(2,1)S(1)}, bf16[6,4,24,128]{3,2,1,0:T(8,128)(2,1)S(1)}, u32[]{:S(2)}, u32[]{:S(2)}) %collective-permute-start.3) | collective-permute-done | bytes 147488 | tf_op jit(solution)/shard_map/ppermute | solution.py:18
  81.8 0.3 pad_maximum_fusion
  82.2 0.1 slice.32
  82.3 0.0 copy-start
  82.3 0.0 copy-start.1
  82.3 0.1 pad_maximum_fusion.2
  82.4 1.0 copy-done
  83.4 1.5 context.1.refs_3_
  84.9 0.0 all-to-all-done
  84.9 0.1 reduce_sum.36
  85.0 3.6 %section_0.1 = (bf16[4,528,128]{2,1,0:T(8,128)(2,1)S(1)}, bf16[4,16,16,128]{3,2,1,0:T(8,128)(2,1)S(1)}, f32[2,128]{1,0:T(2,128)S(1)}) custom-call(s32[5]{0:T(128)S(1)} %stack.39.place_ref.refs_0_, bf16[4,576,128]{2,1,0:T(8,128)(2,1)S(1)} %bitcast.26, f32[2,128]{1,0:T(2,128)S(1)} %bitcast.31, f32[2,528,128]{2,1,0:T(8,128)S(1)} %context.1.refs_3_, ...), custom_call_target="tpu_custom_call" | custom-call | tf_op jit(solution)/shard_map/section_0/pallas_call | solution.py:231
  88.6 0.7 collective-permute-start.4
  89.3 0.0 collective-permute-done.4
  89.3 0.7 collective-permute-start.5
  90.0 42.9 %all_to_all.20 = f32[64,1,256]{2,1,0:T(1,128)S(1)} all-to-all(f32[64,1,256]{2,1,0:T(1,128)S(1)} %broadcast_in_dim.34), channel_id=1, replica_groups=mesh['parts'=2,'section'=4,'tile'=64] {'tile'}, dimensions={0} | all-to-all | bytes 131072 | tf_op jit(solution)/shard_map/all_to_all | solution.py:24
  132.9 0.1 reduce_sum.37
  133.0 3.3 %section_1.1 = (bf16[4,480,128]{2,1,0:T(8,128)(2,1)S(1)}, bf16[4,16,16,128]{3,2,1,0:T(8,128)(2,1)S(1)}, f32[2,128]{1,0:T(2,128)S(1)}) custom-call(s32[5]{0:T(128)S(1)} %stack.39.place_ref.refs_0_, bf16[4,528,128]{2,1,0:T(8,128)(2,1)S(1)} %collective-permute-done.5.refs_1_, f32[2,128]{1,0:T(2,128)S(1)} %bitcast.29, f32[2,528,128]{2,1,0:T(8,128)S(1)} %context.1.refs_3_, ...), custom_call_target="tpu_custom_call" | custom-call | tf_op jit(solution)/shard_map/section_1/pallas_call | solution.py:231
  136.3 0.7 collective-permute-start.6
  137.0 0.0 collective-permute-done.6
  137.0 0.7 broadcast_in_dim.36
  137.7 6.7 %all-to-all-start.2 = ((f32[64,1,256]{2,1,0:T(1,128)}), f32[64,1,256]{2,1,0:T(1,128)S(1)}, u32[]{:S(2)}, u32[]{:S(2)}) async-start(f32[64,1,256]{2,1,0:T(1,128)} %broadcast_in_dim.36), calls=%async_computation.2 | async-start | bytes 131072 | tf_op jit(solution)/shard_map/all_to_all | solution.py:24
  144.3 0.7 collective-permute-start.7
  145.0 24.1 %all-to-all-done.2 = f32[64,1,256]{2,1,0:T(1,128)S(1)} async-done(((f32[64,1,256]{2,1,0:T(1,128)}), f32[64,1,256]{2,1,0:T(1,128)S(1)}, u32[]{:S(2)}, u32[]{:S(2)}) %all-to-all-start.2) | async-done | bytes 65568 | tf_op jit(solution)/shard_map/all_to_all | solution.py:24
  169.2 0.1 reduce_sum.38
  169.3 3.1 %section_2.1 = (bf16[4,432,128]{2,1,0:T(8,128)(2,1)S(1)}, bf16[4,16,16,128]{3,2,1,0:T(8,128)(2,1)S(1)}, f32[2,128]{1,0:T(2,128)S(1)}) custom-call(s32[5]{0:T(128)S(1)} %stack.39.place_ref.refs_0_, bf16[4,480,128]{2,1,0:T(8,128)(2,1)S(1)} %collective-permute-done.7.refs_1_, f32[2,128]{1,0:T(2,128)S(1)} %bitcast.30, f32[2,528,128]{2,1,0:T(8,128)S(1)} %context.1.refs_3_, ...), custom_call_target="tpu_custom_call" | custom-call | tf_op jit(solution)/shard_map/section_2/pallas_call | solution.py:231
  172.3 1.3 collective-permute-start.8
  173.6 10.2 %collective-permute-done.8 = f32[2,128]{1,0:T(2,128)S(1)} collective-permute-done((f32[2,128]{1,0:T(2,128)S(1)}, f32[2,128]{1,0:T(2,128)S(1)}, u32[]{:S(2)}, u32[]{:S(2)}) %collective-permute-start.8) | collective-permute-done | bytes 1056 | tf_op jit(solution)/shard_map/ppermute | solution.py:291
  183.8 0.7 broadcast_in_dim.38
  184.5 13.5 %all-to-all-start.3 = ((f32[64,1,256]{2,1,0:T(1,128)}), f32[64,1,256]{2,1,0:T(1,128)S(1)}, u32[]{:S(2)}, u32[]{:S(2)}) async-start(f32[64,1,256]{2,1,0:T(1,128)} %broadcast_in_dim.38), calls=%async_computation.3 | async-start | bytes 131072 | tf_op jit(solution)/shard_map/all_to_all | solution.py:24
  198.0 1.3 collective-permute-start.9
  199.3 23.6 %all-to-all-done.3 = f32[64,1,256]{2,1,0:T(1,128)S(1)} async-done(((f32[64,1,256]{2,1,0:T(1,128)}), f32[64,1,256]{2,1,0:T(1,128)S(1)}, u32[]{:S(2)}, u32[]{:S(2)}) %all-to-all-start.3) | async-done | bytes 65568 | tf_op jit(solution)/shard_map/all_to_all | solution.py:24
  222.9 0.1 reduce_sum.39
  223.0 0.0 collective-permute-done.9.refs_1_
  223.0 3.3 %section_3.1 = bf16[4,16,16,128]{3,2,1,0:T(8,128)(2,1)} custom-call(s32[5]{0:T(128)S(1)} %stack.39.place_ref.refs_0_, bf16[4,432,128]{2,1,0:T(8,128)(2,1)S(1)} %collective-permute-done.9.refs_1_, f32[2,128]{1,0:T(2,128)S(1)} %bitcast.28, f32[2,528,128]{2,1,0:T(8,128)S(1)} %context.1.refs_3_, bf16[3,1152,128]{2,1,0:T(8,128)(2,1)S(1)} %bitcast.25, ...), custom_call_target="tpu_custom_call" | custom-call | tf_op jit(solution)/shard_map/section_3/pallas_call | solution.py:231
  (10 shorter events, 0.1 us)
Async XLA Ops:
  1.7 44.2 %copy-start.4 = (f32[2,128]{1,0:T(2,128)S(1)}, f32[2,128]{1,0:T(2,128)}, u32[]{:S(2)}) copy-start(f32[2,128]{1,0:T(2,128)} %shard_map.64) | copy-start | bytes 3076
  2.9 50.2 %collective-permute-start = (bf16[6,16,4,128]{3,2,1,0:T(4,128)(2,1)S(1)}, bf16[6,16,4,128]{3,2,1,0:T(4,128)(2,1)S(1)}, u32[]{:S(2)}, u32[]{:S(2)}) collective-permute-start(bf16[6,16,4,128]{3,2,1,0:T(4,128)(2,1)S(1)} %get-tuple-element.41), channel_id=1, source_target_pairs={{0,1},{1,2},{2,3},{3,4},{4,5},{5,6},{6,7},{7,8},{8,9},{9,10},{10,1... | collective-permute-start | bytes 294920 | tf_op jit(solution)/shard_map/ppermute | solution.py:18
  2.9 50.1 %collective-permute-start.1 = (bf16[6,16,4,128]{3,2,1,0:T(4,128)(2,1)S(1)}, bf16[6,16,4,128]{3,2,1,0:T(4,128)(2,1)S(1)}, u32[]{:S(2)}, u32[]{:S(2)}) collective-permute-start(bf16[6,16,4,128]{3,2,1,0:T(4,128)(2,1)S(1)} %get-tuple-element.42), channel_id=1, source_target_pairs={{0,63},{1,0},{2,1},{3,2},{4,3},{5,4},{6,5},{7,6},{8,7},{9,8},{10,9... | collective-permute-start | bytes 294920 | tf_op jit(solution)/shard_map/ppermute | solution.py:18
  46.6 38.4 %all-to-all-start = ((f32[64,1,256]{2,1,0:T(1,128)}), f32[64,1,256]{2,1,0:T(1,128)S(1)}, u32[]{:S(2)}, u32[]{:S(2)}) async-start(f32[64,1,256]{2,1,0:T(1,128)} %broadcast_in_dim.32), calls=%async_computation | async-start | bytes 131072 | tf_op jit(solution)/shard_map/all_to_all | solution.py:24
  53.2 22.0 %collective-permute-start.2 = (bf16[6,4,24,128]{3,2,1,0:T(8,128)(2,1)S(1)}, bf16[6,4,24,128]{3,2,1,0:T(8,128)(2,1)S(1)}, u32[]{:S(2)}, u32[]{:S(2)}) collective-permute-start(bf16[6,4,24,128]{3,2,1,0:T(8,128)(2,1)S(1)} %get-tuple-element.39), channel_id=1, source_target_pairs={{0,8},{1,9},{2,10},{3,11},{4,12},{5,13},{6,14},{7,15},{8,16},{9,17... | collective-permute-start | bytes 442376 | tf_op jit(solution)/shard_map/ppermute | solution.py:18
  59.6 22.2 %collective-permute-start.3 = (bf16[6,4,24,128]{3,2,1,0:T(8,128)(2,1)S(1)}, bf16[6,4,24,128]{3,2,1,0:T(8,128)(2,1)S(1)}, u32[]{:S(2)}, u32[]{:S(2)}) collective-permute-start(bf16[6,4,24,128]{3,2,1,0:T(8,128)(2,1)S(1)} %get-tuple-element.40), channel_id=1, source_target_pairs={{0,56},{1,57},{2,58},{3,59},{4,60},{5,61},{6,62},{7,63},{8,0},{9,1... | collective-permute-start | bytes 442376 | tf_op jit(solution)/shard_map/ppermute | solution.py:18
  82.3 1.2 copy-start
  82.3 1.2 copy-start.1
  83.4 1.6 copy-start.2
  83.4 1.6 copy-start.3
  88.6 0.7 collective-permute-start.4
  89.3 43.7 %collective-permute-start.5 = (bf16[4,528,128]{2,1,0:T(8,128)(2,1)S(1)}, bf16[4,528,128]{2,1,0:T(8,128)(2,1)S(1)}, u32[]{:S(2)}, u32[]{:S(2)}) collective-permute-start(bf16[4,528,128]{2,1,0:T(8,128)(2,1)S(1)} %get-tuple-element.26), channel_id=1, source_target_pairs={{0,64},{1,65},{2,66},{3,67},{4,68},{5,69},{6,70},{7,71},{8,72},{9,... | collective-permute-start | bytes 1622024 | tf_op jit(solution)/shard_map/ppermute | solution.py:294
  136.3 0.7 collective-permute-start.6
  137.7 31.5 %all-to-all-start.2 = ((f32[64,1,256]{2,1,0:T(1,128)}), f32[64,1,256]{2,1,0:T(1,128)S(1)}, u32[]{:S(2)}, u32[]{:S(2)}) async-start(f32[64,1,256]{2,1,0:T(1,128)} %broadcast_in_dim.36), calls=%async_computation.2 | async-start | bytes 131072 | tf_op jit(solution)/shard_map/all_to_all | solution.py:24
  144.3 24.9 %collective-permute-start.7 = (bf16[4,480,128]{2,1,0:T(8,128)(2,1)S(1)}, bf16[4,480,128]{2,1,0:T(8,128)(2,1)S(1)}, u32[]{:S(2)}, u32[]{:S(2)}) collective-permute-start(bf16[4,480,128]{2,1,0:T(8,128)(2,1)S(1)} %get-tuple-element.31), channel_id=1, source_target_pairs={{64,128},{65,129},{66,130},{67,131},{68,132},{69,133},{70,134},{71... | collective-permute-start | bytes 1474568 | tf_op jit(solution)/shard_map/ppermute | solution.py:294
  172.3 11.5 %collective-permute-start.8 = (f32[2,128]{1,0:T(2,128)S(1)}, f32[2,128]{1,0:T(2,128)S(1)}, u32[]{:S(2)}, u32[]{:S(2)}) collective-permute-start(f32[2,128]{1,0:T(2,128)S(1)} %get-tuple-element.34), channel_id=1, source_target_pairs={{128,192},{129,193},{130,194},{131,195},{132,196},{133,197},{134,1... | collective-permute-start | bytes 3080 | tf_op jit(solution)/shard_map/ppermute | solution.py:291
  184.5 38.4 %all-to-all-start.3 = ((f32[64,1,256]{2,1,0:T(1,128)}), f32[64,1,256]{2,1,0:T(1,128)S(1)}, u32[]{:S(2)}, u32[]{:S(2)}) async-start(f32[64,1,256]{2,1,0:T(1,128)} %broadcast_in_dim.38), calls=%async_computation.3 | async-start | bytes 131072 | tf_op jit(solution)/shard_map/all_to_all | solution.py:24
  198.0 25.0 %collective-permute-start.9 = (bf16[4,432,128]{2,1,0:T(8,128)(2,1)S(1)}, bf16[4,432,128]{2,1,0:T(8,128)(2,1)S(1)}, u32[]{:S(2)}, u32[]{:S(2)}) collective-permute-start(bf16[4,432,128]{2,1,0:T(8,128)(2,1)S(1)} %get-tuple-element.36), channel_id=1, source_target_pairs={{128,192},{129,193},{130,194},{131,195},{132,196},{133,197},{134,1... | collective-permute-start | bytes 1327112 | tf_op jit(solution)/shard_map/ppermute | solution.py:294

commit v3 on v2

--- a/solution.py
+++ b/solution.py
@@ -6,6 +6,7 @@
 from jax.experimental import pallas as pl
 from jax.experimental.pallas import tpu as pltpu
 from jax.sharding import PartitionSpec as P
+
 
 GROUPS = 32
 EPSILON = 1e-06
@@ -91,7 +92,9 @@
     return jnp.dot(cols[frame, :rows], weights, preferred_element_type=jnp.float32)
 
 
-def context_kernel(side, wide, place_ref, cache_ref, kernel_ref, bias_ref, part_ref, act, cols):
+def context_kernel(side, wide, place_ref, cache_ref, kernel_hbm, bias_ref, part_ref, act, cols, kernel_ref, sem):
+    fetch = pltpu.make_async_copy(kernel_hbm.at[:2], kernel_ref, sem)
+    fetch.start()
     context = cache_ref.shape[0]
     channels = cache_ref.shape[-1]
     flags = [place_ref[i] for i in range(4)]
@@ -102,6 +105,7 @@
         act[f, : wide * wide] = jnp.where(valid, values, 0.0).reshape(wide * wide, channels)
         act[f, wide * wide :] = jnp.zeros((act.shape[1] - wide * wide, channels), jnp.float32)
         unfold(act, cols, f, wide, rows, channels)
+    fetch.wait()
     w0, w1 = kernel_ref[0], kernel_ref[1]
     bias = bias_ref[...].reshape(1, channels)
     pair = matmul(cols, 1, rows, jnp.concatenate([w1, w0], axis=1))
@@ -116,11 +120,13 @@
     return pl.pallas_call(
         functools.partial(context_kernel, side, wide),
         out_shape=jax.ShapeDtypeStruct((2, rows, channels), jnp.float32),
-        in_specs=[pl.BlockSpec(memory_space=pltpu.SMEM), vmem, vmem, vmem],
+        in_specs=[pl.BlockSpec(memory_space=pltpu.SMEM), vmem, pl.BlockSpec(memory_space=pltpu.HBM), vmem],
         out_specs=vmem,
         scratch_shapes=[
             pltpu.VMEM((cache.shape[0], wide * wide + 8, channels), jnp.float32),
             pltpu.VMEM((cache.shape[0], rows, TAPS * TAPS * channels), jnp.bfloat16),
+            pltpu.VMEM((2, *kernel.shape[1:]), kernel.dtype),
+            pltpu.SemaphoreType.DMA,
         ],
         compiler_params=pltpu.CompilerParams(vmem_limit_bytes=VMEM_LIMIT),
         name="context",
@@ -128,10 +134,12 @@
 
 
 def section_kernel(
-    shape, tick, place_ref, x_ref, sums_ref, part_ref, kernel_ref, bias_ref, gain_ref, offset_ref,
-    kept_ref, next_ref, result_ref, out_sums_ref, act, held, cols, made,
+    shape, tick, place_ref, x_ref, sums_ref, part_ref, kernel_hbm, bias_ref, gain_ref, offset_ref,
+    kept_ref, next_ref, result_ref, out_sums_ref, act, held, cols, made, kernel_ref, sem,
 ):
-    count, side, wide, sections, pixels, members = shape
+    fetch = pltpu.make_async_copy(kernel_hbm, kernel_ref, sem)
+    fetch.start()
+    count, side, wide, _, pixels, members = shape
     rows_in = wide - 2 * tick
     rows_out = rows_in - 2
     channels = x_ref.shape[-1]
@@ -157,6 +165,7 @@
         active = jnp.where(valid, active, 0.0).reshape(flat_in, channels)
         act[f, :flat_in] = active
         unfold(act, cols, f, wide, flat_out, channels)
+    fetch.wait()
     w0, w1, w2 = (kernel_ref[i] for i in range(TAPS))
     both_1 = jnp.concatenate([w1, w0], axis=1)
     both_2 = jnp.concatenate([w2, w1], axis=1)
@@ -204,7 +213,7 @@
 
 
 def section_step(shape, tick, place, x, sums, part, kernel, bias, gain, offset, kept):
-    count, side, wide, sections, pixels, members = shape
+    count, side, wide, sections, _, _ = shape
     channels = x.shape[-1]
     rows_out = wide - 2 * tick - 2
     last = tick == sections - 1
@@ -231,16 +240,18 @@
     return pl.pallas_call(
         body,
         out_shape=tuple(outs),
-        in_specs=[pl.BlockSpec(memory_space=pltpu.SMEM)] + [vmem] * (len(inputs) - 1),
+        in_specs=[pl.BlockSpec(memory_space=pltpu.SMEM), vmem, vmem, vmem, pl.BlockSpec(memory_space=pltpu.HBM)]
+        + [vmem] * (len(inputs) - 5),
         out_specs=tuple([vmem] * len(outs)),
         scratch_shapes=[
             pltpu.VMEM((count, full, channels), jnp.float32),
             pltpu.VMEM((count, full, channels), jnp.float32),
             pltpu.VMEM((count, rows_out * wide, TAPS * TAPS * channels), jnp.bfloat16),
             pltpu.VMEM((count, rows_out * wide, channels), jnp.float32),
+            pltpu.VMEM(kernel.shape, kernel.dtype),
+            pltpu.SemaphoreType.DMA,
         ],
         compiler_params=pltpu.CompilerParams(vmem_limit_bytes=VMEM_LIMIT),
-        name=f"section_{tick}",
     )(*inputs)
 
 
@@ -264,19 +275,20 @@
     kernel = conv_weight[0].reshape(TAPS, TAPS * TAPS * channels, channels)
 
     old = cache[0, :, 0]
+    context = old.shape[0]
     sums = first_sums(x, members)
-    sums, seq = lax.optimization_barrier((sums, jnp.concatenate([old, x], axis=0)))
-    sums = of_everyone(sums)
+    seq = jnp.concatenate([old, x], axis=0)
     left = shifted(seq[:, :, side - halo :], 1)
     right = shifted(seq[:, :, :halo], -1)
     middle = jnp.concatenate([left, seq, right], axis=2)
     above = shifted(middle[:, side - halo :], across)
     below = shifted(middle[:, :halo], -across)
-    whole = jnp.concatenate([above, middle, below], axis=1)
-    whole = whole.reshape(whole.shape[0], wide * wide, channels)
-    context = old.shape[0]
-    x = whole[context:]
-    part = context_part(side, wide, place, whole[:context], kernel, conv_bias)
+    sums = of_everyone(sums)
+    held_cache, x = (
+        jnp.concatenate([above[c], middle[c], below[c]], axis=1).reshape(-1, wide * wide, channels)
+        for c in (slice(0, context), slice(context, None))
+    )
+    part = context_part(side, wide, place, held_cache, kernel, conv_bias)
 
     result = None
     for tick in range(sections):
@@ -290,8 +302,8 @@
         hop = [(tick, tick + 1)]
         sums = lax.ppermute(sums, "section", hop)
         sums, x = lax.optimization_barrier((sums, x))
+        x = lax.ppermute(x, "section", hop)
         sums = of_everyone(sums)
-        x = lax.ppermute(x, "section", hop)
     return result[None, :, None]
 
 

time: 227 us -> 231 us (1.018)
  Pallas kernels: 16.5 us -> 20.5 us
    pallas_call x4, Pallas kernels: 13.3 us -> 16.7 us  [section_step(): pl.pallas_call(body, out_shape=tuple(outs), in_specs=[pl.BlockSpec(memory...]
  transfers between devices with their start and end apart: 13 -> 13, of which waited for: 5 -> 5; matrix products, arithmetic and copies ran while one was open for 1% -> 1% of each run, Pallas kernels for 1% -> 2%
where the time goes in v3:
time: 231 us; the launch traced here: 230 us
  starting transfers between devices  84.8 us (37%)
  waiting for transfers between devices  76.4 us (33%)
  blocking collectives  43 us (19%)
  Pallas kernels  20.5 us (9%)
  local copies, waits for them, and re-layouts  3.33 us (1%)
    ppermute x4, starting transfers between devices, shifted(): lax.ppermute(array, 'tile', [(i, (i + by) % peers) for i in range(peers)])  52.8 us
    all_to_all x3, waiting for transfers between devices, of_everyone(): lax.all_to_all(copies, 'tile', 0, 0, tiled=True)  47.7 us
    all_to_all x1, blocking collectives, of_everyone(): lax.all_to_all(copies, 'tile', 0, 0, tiled=True)  43 us
    all_to_all x3, starting transfers between devices, of_everyone(): lax.all_to_all(copies, 'tile', 0, 0, tiled=True)  26.6 us
    ppermute x4, waiting for transfers between devices, shifted(): lax.ppermute(array, 'tile', [(i, (i + by) % peers) for i in range(peers)])  18.5 us
    pallas_call x4, Pallas kernels, section_step(): pl.pallas_call(body, out_shape=tuple(outs), in_specs=[pl.BlockSpec(memory...  16.7 us
    ppermute x3, waiting for transfers between devices, local(): sums = lax.ppermute(sums, 'section', hop)  10.2 us
  transfers between devices with their start and end apart: 13, of which 5 were waited for; matrix products, arithmetic and copies ran while one was open for 1% of the time, Pallas kernels for 2%

profile of v3, /device:TPU:46, one launch (start us, length us, event | category | flops | bytes accessed | tf_op | source)
XLA Modules:
  0.0 230.4 jit_solution(16909197262995338047)
XLA Ops:
  0.0 1.1 pad_maximum_fusion.4
  1.1 0.1 collective-permute-start
  1.2 43.0 %collective-permute-start.1 = (bf16[6,16,4,128]{3,2,1,0:T(4,128)(2,1)S(1)}, bf16[6,16,4,128]{3,2,1,0:T(4,128)(2,1)S(1)}, u32[]{:S(2)}, u32[]{:S(2)}) collective-permute-start(bf16[6,16,4,128]{3,2,1,0:T(4,128)(2,1)S(1)} %get-tuple-element.38), channel_id=1, source_target_pairs={{0,63},{1,0},{2,1},{3,2},{4,3},{5,4},{6,5},{7,6},{8,7},{9,8},{10,9... | collective-permute-start | bytes 294920 | tf_op jit(solution)/shard_map/ppermute | solution.py:19
  44.2 1.8 shard_map.64
  45.9 1.3 broadcast_in_dim.32
  47.3 6.5 %all-to-all-start = ((f32[64,1,256]{2,1,0:T(1,128)}), f32[64,1,256]{2,1,0:T(1,128)S(1)}, u32[]{:S(2)}, u32[]{:S(2)}) async-start(f32[64,1,256]{2,1,0:T(1,128)} %broadcast_in_dim.32), calls=%async_computation | async-start | bytes 131072 | tf_op jit(solution)/shard_map/all_to_all | solution.py:25
  53.8 0.3 pad_maximum_fusion
  54.2 6.4 %collective-permute-start.2 = (bf16[6,4,24,128]{3,2,1,0:T(8,128)(2,1)S(1)}, bf16[6,4,24,128]{3,2,1,0:T(8,128)(2,1)S(1)}, u32[]{:S(2)}, u32[]{:S(2)}) collective-permute-start(bf16[6,4,24,128]{3,2,1,0:T(8,128)(2,1)S(1)} %get-tuple-element.35), channel_id=1, source_target_pairs={{0,8},{1,9},{2,10},{3,11},{4,12},{5,13},{6,14},{7,15},{8,16},{9,17... | collective-permute-start | bytes 442376 | tf_op jit(solution)/shard_map/ppermute | solution.py:19
  60.5 3.5 %collective-permute-start.3 = (bf16[6,4,24,128]{3,2,1,0:T(8,128)(2,1)S(1)}, bf16[6,4,24,128]{3,2,1,0:T(8,128)(2,1)S(1)}, u32[]{:S(2)}, u32[]{:S(2)}) collective-permute-start(bf16[6,4,24,128]{3,2,1,0:T(8,128)(2,1)S(1)} %get-tuple-element.36), channel_id=1, source_target_pairs={{0,56},{1,57},{2,58},{3,59},{4,60},{5,61},{6,62},{7,63},{8,0},{9,1... | collective-permute-start | bytes 442376 | tf_op jit(solution)/shard_map/ppermute | solution.py:19
  64.0 0.1 stack.39.place_ref.refs_0_
  64.2 0.0 copy-start
  64.2 0.0 copy-start.1
  64.2 10.8 %collective-permute-done.2 = bf16[6,4,24,128]{3,2,1,0:T(8,128)(2,1)S(1)} collective-permute-done((bf16[6,4,24,128]{3,2,1,0:T(8,128)(2,1)S(1)}, bf16[6,4,24,128]{3,2,1,0:T(8,128)(2,1)S(1)}, u32[]{:S(2)}, u32[]{:S(2)}) %collective-permute-start.2) | collective-permute-done | bytes 147488 | tf_op jit(solution)/shard_map/ppermute | solution.py:19
  75.0 7.7 %collective-permute-done.3 = bf16[6,4,24,128]{3,2,1,0:T(8,128)(2,1)S(1)} collective-permute-done((bf16[6,4,24,128]{3,2,1,0:T(8,128)(2,1)S(1)}, bf16[6,4,24,128]{3,2,1,0:T(8,128)(2,1)S(1)}, u32[]{:S(2)}, u32[]{:S(2)}) %collective-permute-start.3) | collective-permute-done | bytes 147488 | tf_op jit(solution)/shard_map/ppermute | solution.py:19
  82.8 0.0 slice-start
  82.8 2.0 context.1.refs_3_
  84.8 0.0 copy-start.2
  84.8 0.0 copy-start.3
  84.8 0.1 pad_maximum_fusion.1
  84.9 0.0 all-to-all-done
  84.9 0.1 reduce_sum.36
  85.0 0.4 copy-done.2
  85.4 0.0 copy-done.3
  85.4 4.6 %shard_map.65 = (bf16[4,528,128]{2,1,0:T(8,128)(2,1)S(1)}, bf16[4,16,16,128]{3,2,1,0:T(8,128)(2,1)S(1)}, f32[2,128]{1,0:T(2,128)S(1)}) custom-call(s32[5]{0:T(128)S(1)} %stack.39.place_ref.refs_0_, bf16[4,576,128]{2,1,0:T(8,128)(2,1)S(1)} %bitcast.26, f32[2,128]{1,0:T(2,128)S(1)} %bitcast.31, f32[2,528,128]{2,1,0:T(8,128)S(1)} %context.1.refs_3_, ...), custom_call_target="tpu_custom_call" | custom-call | tf_op jit(solution)/shard_map/pallas_call | solution.py:240
  90.0 0.7 collective-permute-start.4
  90.7 0.0 collective-permute-done.4
  90.7 0.7 collective-permute-start.5
  91.4 43.0 %all_to_all.20 = f32[64,1,256]{2,1,0:T(1,128)S(1)} all-to-all(f32[64,1,256]{2,1,0:T(1,128)S(1)} %broadcast_in_dim.34), channel_id=1, replica_groups=mesh['parts'=2,'section'=4,'tile'=64] {'tile'}, dimensions={0} | all-to-all | bytes 131072 | tf_op jit(solution)/shard_map/all_to_all | solution.py:25
  134.4 0.1 reduce_sum.37
  134.5 4.2 %shard_map.66 = (bf16[4,480,128]{2,1,0:T(8,128)(2,1)S(1)}, bf16[4,16,16,128]{3,2,1,0:T(8,128)(2,1)S(1)}, f32[2,128]{1,0:T(2,128)S(1)}) custom-call(s32[5]{0:T(128)S(1)} %stack.39.place_ref.refs_0_, bf16[4,528,128]{2,1,0:T(8,128)(2,1)S(1)} %collective-permute-done.5.refs_1_, f32[2,128]{1,0:T(2,128)S(1)} %bitcast.29, f32[2,528,128]{2,1,0:T(8,128)S(1)} %context.1.refs_3_, ...), custom_call_target="tpu_custom_call" | custom-call | tf_op jit(solution)/shard_map/pallas_call | solution.py:240
  138.7 0.7 collective-permute-start.6
  139.3 0.0 collective-permute-done.6
  139.4 0.7 broadcast_in_dim.36
  140.0 6.7 %all-to-all-start.2 = ((f32[64,1,256]{2,1,0:T(1,128)}), f32[64,1,256]{2,1,0:T(1,128)S(1)}, u32[]{:S(2)}, u32[]{:S(2)}) async-start(f32[64,1,256]{2,1,0:T(1,128)} %broadcast_in_dim.36), calls=%async_computation.2 | async-start | bytes 131072 | tf_op jit(solution)/shard_map/all_to_all | solution.py:25
  146.7 0.7 collective-permute-start.7
  147.4 24.1 %all-to-all-done.2 = f32[64,1,256]{2,1,0:T(1,128)S(1)} async-done(((f32[64,1,256]{2,1,0:T(1,128)}), f32[64,1,256]{2,1,0:T(1,128)S(1)}, u32[]{:S(2)}, u32[]{:S(2)}) %all-to-all-start.2) | async-done | bytes 65568 | tf_op jit(solution)/shard_map/all_to_all | solution.py:25
  171.5 0.1 reduce_sum.38
  171.6 0.0 collective-permute-done.7.refs_1_
  171.6 4.0 %shard_map.67 = (bf16[4,432,128]{2,1,0:T(8,128)(2,1)S(1)}, bf16[4,16,16,128]{3,2,1,0:T(8,128)(2,1)S(1)}, f32[2,128]{1,0:T(2,128)S(1)}) custom-call(s32[5]{0:T(128)S(1)} %stack.39.place_ref.refs_0_, bf16[4,480,128]{2,1,0:T(8,128)(2,1)S(1)} %collective-permute-done.7.refs_1_, f32[2,128]{1,0:T(2,128)S(1)} %bitcast.30, f32[2,528,128]{2,1,0:T(8,128)S(1)} %context.1.refs_3_, ...), custom_call_target="tpu_custom_call" | custom-call | tf_op jit(solution)/shard_map/pallas_call | solution.py:240
  175.6 1.3 collective-permute-start.8
  176.9 10.2 %collective-permute-done.8 = f32[2,128]{1,0:T(2,128)S(1)} collective-permute-done((f32[2,128]{1,0:T(2,128)S(1)}, f32[2,128]{1,0:T(2,128)S(1)}, u32[]{:S(2)}, u32[]{:S(2)}) %collective-permute-start.8) | collective-permute-done | bytes 1056 | tf_op jit(solution)/shard_map/ppermute | solution.py:303
  187.1 0.7 broadcast_in_dim.38
  187.8 13.5 %all-to-all-start.3 = ((f32[64,1,256]{2,1,0:T(1,128)}), f32[64,1,256]{2,1,0:T(1,128)S(1)}, u32[]{:S(2)}, u32[]{:S(2)}) async-start(f32[64,1,256]{2,1,0:T(1,128)} %broadcast_in_dim.38), calls=%async_computation.3 | async-start | bytes 131072 | tf_op jit(solution)/shard_map/all_to_all | solution.py:25
  201.3 1.3 collective-permute-start.9
  202.6 23.6 %all-to-all-done.3 = f32[64,1,256]{2,1,0:T(1,128)S(1)} async-done(((f32[64,1,256]{2,1,0:T(1,128)}), f32[64,1,256]{2,1,0:T(1,128)S(1)}, u32[]{:S(2)}, u32[]{:S(2)}) %all-to-all-start.3) | async-done | bytes 65568 | tf_op jit(solution)/shard_map/all_to_all | solution.py:25
  226.1 0.1 reduce_sum.39
  226.2 0.0 collective-permute-done.9.refs_1_
  226.2 4.0 %shard_map.68 = bf16[4,16,16,128]{3,2,1,0:T(8,128)(2,1)} custom-call(s32[5]{0:T(128)S(1)} %stack.39.place_ref.refs_0_, bf16[4,432,128]{2,1,0:T(8,128)(2,1)S(1)} %collective-permute-done.9.refs_1_, f32[2,128]{1,0:T(2,128)S(1)} %bitcast.28, f32[2,528,128]{2,1,0:T(8,128)S(1)} %context.1.refs_3_, bf16[3,1152,128]{2,1,0:T(8,128)(2,1)S(1)} %bitcast.25, ...), custom_call_target="tpu_custom_call" | custom-call | tf_op jit(solution)/shard_map/pallas_call | solution.py:240
  (20 shorter events, 0.2 us)
Async XLA Ops:
  0.0 53.8 %copy-start.6 = (bf16[1,2,1,16,16,128]{5,4,3,2,1,0:T(8,128)(2,1)S(1)}, bf16[1,2,1,16,16,128]{5,4,3,2,1,0:T(8,128)(2,1)}, u32[]{:S(2)}) copy-start(bf16[1,2,1,16,16,128]{5,4,3,2,1,0:T(8,128)(2,1)} %param.7) | copy-start | bytes 393220
  0.0 53.8 %copy-start.5 = (bf16[4,1,16,16,128]{4,3,2,1,0:T(8,128)(2,1)S(1)}, bf16[4,1,16,16,128]{4,3,2,1,0:T(8,128)(2,1)}, u32[]{:S(2)}) copy-start(bf16[4,1,16,16,128]{4,3,2,1,0:T(8,128)(2,1)} %param.6) | copy-start | bytes 786436
  1.1 52.6 %collective-permute-start = (bf16[6,16,4,128]{3,2,1,0:T(4,128)(2,1)S(1)}, bf16[6,16,4,128]{3,2,1,0:T(4,128)(2,1)S(1)}, u32[]{:S(2)}, u32[]{:S(2)}) collective-permute-start(bf16[6,16,4,128]{3,2,1,0:T(4,128)(2,1)S(1)} %get-tuple-element.37), channel_id=1, source_target_pairs={{0,1},{1,2},{2,3},{3,4},{4,5},{5,6},{6,7},{7,8},{8,9},{9,10},{10,1... | collective-permute-start | bytes 294920 | tf_op jit(solution)/shard_map/ppermute | solution.py:19
  1.2 52.5 %collective-permute-start.1 = (bf16[6,16,4,128]{3,2,1,0:T(4,128)(2,1)S(1)}, bf16[6,16,4,128]{3,2,1,0:T(4,128)(2,1)S(1)}, u32[]{:S(2)}, u32[]{:S(2)}) collective-permute-start(bf16[6,16,4,128]{3,2,1,0:T(4,128)(2,1)S(1)} %get-tuple-element.38), channel_id=1, source_target_pairs={{0,63},{1,0},{2,1},{3,2},{4,3},{5,4},{6,5},{7,6},{8,7},{9,8},{10,9... | collective-permute-start | bytes 294920 | tf_op jit(solution)/shard_map/ppermute | solution.py:19
  47.3 37.6 %all-to-all-start = ((f32[64,1,256]{2,1,0:T(1,128)}), f32[64,1,256]{2,1,0:T(1,128)S(1)}, u32[]{:S(2)}, u32[]{:S(2)}) async-start(f32[64,1,256]{2,1,0:T(1,128)} %broadcast_in_dim.32), calls=%async_computation | async-start | bytes 131072 | tf_op jit(solution)/shard_map/all_to_all | solution.py:25
  54.1 10.1 %copy-start.4 = (bf16[6,16,24,128]{3,2,1,0:T(8,128)(2,1)}, bf16[6,16,24,128]{3,2,1,0:T(8,128)(2,1)S(1)}, u32[]{:S(2)}) copy-start(bf16[6,16,24,128]{3,2,1,0:T(8,128)(2,1)S(1)} %pad_maximum_fusion) | copy-start | bytes 1769476
  54.2 20.8 %collective-permute-start.2 = (bf16[6,4,24,128]{3,2,1,0:T(8,128)(2,1)S(1)}, bf16[6,4,24,128]{3,2,1,0:T(8,128)(2,1)S(1)}, u32[]{:S(2)}, u32[]{:S(2)}) collective-permute-start(bf16[6,4,24,128]{3,2,1,0:T(8,128)(2,1)S(1)} %get-tuple-element.35), channel_id=1, source_target_pairs={{0,8},{1,9},{2,10},{3,11},{4,12},{5,13},{6,14},{7,15},{8,16},{9,17... | collective-permute-start | bytes 442376 | tf_op jit(solution)/shard_map/ppermute | solution.py:19
  60.5 22.2 %collective-permute-start.3 = (bf16[6,4,24,128]{3,2,1,0:T(8,128)(2,1)S(1)}, bf16[6,4,24,128]{3,2,1,0:T(8,128)(2,1)S(1)}, u32[]{:S(2)}, u32[]{:S(2)}) collective-permute-start(bf16[6,4,24,128]{3,2,1,0:T(8,128)(2,1)S(1)} %get-tuple-element.36), channel_id=1, source_target_pairs={{0,56},{1,57},{2,58},{3,59},{4,60},{5,61},{6,62},{7,63},{8,0},{9,1... | collective-permute-start | bytes 442376 | tf_op jit(solution)/shard_map/ppermute | solution.py:19
  64.2 18.6 %copy-start = (bf16[1,3,3,3,128,128]{5,4,3,2,1,0:T(8,128)(2,1)S(1)}, bf16[1,3,3,3,128,128]{5,4,3,2,1,0:T(8,128)(2,1)}, u32[]{:S(2)}) copy-start(bf16[1,3,3,3,128,128]{5,4,3,2,1,0:T(8,128)(2,1)} %param.8) | copy-start | bytes 2654212
  64.2 18.6 %copy-start.1 = (f32[1,128]{1,0:T(1,128)S(1)}, f32[1,128]{1,0:T(1,128)}, u32[]{:S(2)}) copy-start(f32[1,128]{1,0:T(1,128)} %refs_5_.7) | copy-start | bytes 1540
  82.8 2.1 slice-start
  84.8 0.7 copy-start.2
  84.8 0.7 copy-start.3
  90.0 0.7 collective-permute-start.4
  90.7 43.8 %collective-permute-start.5 = (bf16[4,528,128]{2,1,0:T(8,128)(2,1)S(1)}, bf16[4,528,128]{2,1,0:T(8,128)(2,1)S(1)}, u32[]{:S(2)}, u32[]{:S(2)}) collective-permute-start(bf16[4,528,128]{2,1,0:T(8,128)(2,1)S(1)} %get-tuple-element.22), channel_id=1, source_target_pairs={{0,64},{1,65},{2,66},{3,67},{4,68},{5,69},{6,70},{7,71},{8,72},{9,... | collective-permute-start | bytes 1622024 | tf_op jit(solution)/shard_map/ppermute | solution.py:305
  138.7 0.7 collective-permute-start.6
  140.0 31.5 %all-to-all-start.2 = ((f32[64,1,256]{2,1,0:T(1,128)}), f32[64,1,256]{2,1,0:T(1,128)S(1)}, u32[]{:S(2)}, u32[]{:S(2)}) async-start(f32[64,1,256]{2,1,0:T(1,128)} %broadcast_in_dim.36), calls=%async_computation.2 | async-start | bytes 131072 | tf_op jit(solution)/shard_map/all_to_all | solution.py:25
  146.7 24.9 %collective-permute-start.7 = (bf16[4,480,128]{2,1,0:T(8,128)(2,1)S(1)}, bf16[4,480,128]{2,1,0:T(8,128)(2,1)S(1)}, u32[]{:S(2)}, u32[]{:S(2)}) collective-permute-start(bf16[4,480,128]{2,1,0:T(8,128)(2,1)S(1)} %get-tuple-element.27), channel_id=1, source_target_pairs={{64,128},{65,129},{66,130},{67,131},{68,132},{69,133},{70,134},{71... | collective-permute-start | bytes 1474568 | tf_op jit(solution)/shard_map/ppermute | solution.py:305
  175.6 11.5 %collective-permute-start.8 = (f32[2,128]{1,0:T(2,128)S(1)}, f32[2,128]{1,0:T(2,128)S(1)}, u32[]{:S(2)}, u32[]{:S(2)}) collective-permute-start(f32[2,128]{1,0:T(2,128)S(1)} %get-tuple-element.30), channel_id=1, source_target_pairs={{128,192},{129,193},{130,194},{131,195},{132,196},{133,197},{134,1... | collective-permute-start | bytes 3080 | tf_op jit(solution)/shard_map/ppermute | solution.py:303
  187.8 38.4 %all-to-all-start.3 = ((f32[64,1,256]{2,1,0:T(1,128)}), f32[64,1,256]{2,1,0:T(1,128)S(1)}, u32[]{:S(2)}, u32[]{:S(2)}) async-start(f32[64,1,256]{2,1,0:T(1,128)} %broadcast_in_dim.38), calls=%async_computation.3 | async-start | bytes 131072 | tf_op jit(solution)/shard_map/all_to_all | solution.py:25
  201.3 25.0 %collective-permute-start.9 = (bf16[4,432,128]{2,1,0:T(8,128)(2,1)S(1)}, bf16[4,432,128]{2,1,0:T(8,128)(2,1)S(1)}, u32[]{:S(2)}, u32[]{:S(2)}) collective-permute-start(bf16[4,432,128]{2,1,0:T(8,128)(2,1)S(1)} %get-tuple-element.32), channel_id=1, source_target_pairs={{128,192},{129,193},{130,194},{131,195},{132,196},{133,197},{134,1... | collective-permute-start | bytes 1327112 | tf_op jit(solution)/shard_map/ppermute | solution.py:305

commit v4 on v3

--- a/solution.py
+++ b/solution.py
@@ -92,9 +92,7 @@
     return jnp.dot(cols[frame, :rows], weights, preferred_element_type=jnp.float32)
 
 
-def context_kernel(side, wide, place_ref, cache_ref, kernel_hbm, bias_ref, part_ref, act, cols, kernel_ref, sem):
-    fetch = pltpu.make_async_copy(kernel_hbm.at[:2], kernel_ref, sem)
-    fetch.start()
+def context_kernel(side, wide, place_ref, cache_ref, kernel_ref, bias_ref, part_ref, act, cols):
     context = cache_ref.shape[0]
     channels = cache_ref.shape[-1]
     flags = [place_ref[i] for i in range(4)]
@@ -105,7 +103,6 @@
         act[f, : wide * wide] = jnp.where(valid, values, 0.0).reshape(wide * wide, channels)
         act[f, wide * wide :] = jnp.zeros((act.shape[1] - wide * wide, channels), jnp.float32)
         unfold(act, cols, f, wide, rows, channels)
-    fetch.wait()
     w0, w1 = kernel_ref[0], kernel_ref[1]
     bias = bias_ref[...].reshape(1, channels)
     pair = matmul(cols, 1, rows, jnp.concatenate([w1, w0], axis=1))
@@ -120,13 +117,11 @@
     return pl.pallas_call(
         functools.partial(context_kernel, side, wide),
         out_shape=jax.ShapeDtypeStruct((2, rows, channels), jnp.float32),
-        in_specs=[pl.BlockSpec(memory_space=pltpu.SMEM), vmem, pl.BlockSpec(memory_space=pltpu.HBM), vmem],
+        in_specs=[pl.BlockSpec(memory_space=pltpu.SMEM), vmem, vmem, vmem],
         out_specs=vmem,
         scratch_shapes=[
             pltpu.VMEM((cache.shape[0], wide * wide + 8, channels), jnp.float32),
             pltpu.VMEM((cache.shape[0], rows, TAPS * TAPS * channels), jnp.bfloat16),
-            pltpu.VMEM((2, *kernel.shape[1:]), kernel.dtype),
-            pltpu.SemaphoreType.DMA,
         ],
         compiler_params=pltpu.CompilerParams(vmem_limit_bytes=VMEM_LIMIT),
         name="context",
@@ -134,11 +129,9 @@
 
 
 def section_kernel(
-    shape, tick, place_ref, x_ref, sums_ref, part_ref, kernel_hbm, bias_ref, gain_ref, offset_ref,
-    kept_ref, next_ref, result_ref, out_sums_ref, act, held, cols, made, kernel_ref, sem,
+    shape, tick, place_ref, x_ref, sums_ref, part_ref, kernel_ref, bias_ref, gain_ref, offset_ref,
+    kept_ref, next_ref, result_ref, out_sums_ref, act, held, cols, made,
 ):
-    fetch = pltpu.make_async_copy(kernel_hbm, kernel_ref, sem)
-    fetch.start()
     count, side, wide, _, pixels, members = shape
     rows_in = wide - 2 * tick
     rows_out = rows_in - 2
@@ -153,7 +146,15 @@
     valid = masked(flags, halo - tick, rows_in, wide, side, channels)
     gain = gain_ref[...].reshape(1, channels)
     offset = offset_ref[...].reshape(1, channels)
-    for f in range(count):
+    w0, w1, w2 = (kernel_ref[i] for i in range(TAPS))
+    both_1 = jnp.concatenate([w1, w0], axis=1)
+    both_2 = jnp.concatenate([w2, w1], axis=1)
+    bias = bias_ref[...].reshape(1, channels)
+    base = tick * (wide + 1)
+    edge = halo - tick - 1
+    sums, squares = [], []
+
+    def prepare(f):
         mean = unpacked(mean_row, f, members)
         variance = jnp.maximum(unpacked(square_row, f, members) - mean * mean, 0.0)
         scale = gain / jnp.sqrt(variance + EPSILON)
@@ -165,48 +166,46 @@
         active = jnp.where(valid, active, 0.0).reshape(flat_in, channels)
         act[f, :flat_in] = active
         unfold(act, cols, f, wide, flat_out, channels)
-    fetch.wait()
-    w0, w1, w2 = (kernel_ref[i] for i in range(TAPS))
-    both_1 = jnp.concatenate([w1, w0], axis=1)
-    both_2 = jnp.concatenate([w2, w1], axis=1)
-    bias = bias_ref[...].reshape(1, channels)
-    base = tick * (wide + 1)
 
     def finish(g, value):
         new = value + held[g, wide + 1 : wide + 1 + flat_out]
-        made[g, :flat_out] = new.astype(jnp.bfloat16).astype(jnp.float32)
-
-    for f in range(0, count, 2):
-        pair = matmul(cols, f, flat_out, both_2)
-        first = pair[:, :channels]
-        second = pair[:, channels:] + matmul(cols, f + 1, flat_out, w2)
-        if f == 0:
-            finish(f, first + part_ref[0, base : base + flat_out])
-            finish(f + 1, second + part_ref[1, base : base + flat_out])
-        else:
-            pair = matmul(cols, f - 1, flat_out, both_1)
-            first = first + pair[:, :channels] + matmul(cols, f - 2, flat_out, w0)
-            finish(f, first + bias)
-            finish(f + 1, second + pair[:, channels:] + bias)
-    edge = halo - tick - 1
-    sums, squares = [], []
-    for f in range(count):
+        new = new.astype(jnp.bfloat16)
+        made[g, :flat_out] = new.astype(jnp.float32)
         if next_ref is not None:
-            next_ref[f] = made[f, :flat_out].astype(jnp.bfloat16)
+            next_ref[g] = new
         total_f = jnp.zeros((side, channels), jnp.float32)
         square_f = jnp.zeros((side, channels), jnp.float32)
         for y in range(side):
             at = (y + edge) * wide + edge
-            row = made[f, at : at + side]
+            row = made[g, at : at + side]
             if out_sums_ref is not None:
                 total_f = total_f + row
                 square_f = square_f + row * row
             row = row.astype(jnp.bfloat16)
             if kept_ref is not None:
-                row = jnp.where(position == tick, row, kept_ref[f, y])
-            result_ref[f, y] = row
+                row = jnp.where(position == tick, row, kept_ref[g, y])
+            result_ref[g, y] = row
         sums.append(jnp.sum(total_f, axis=0, keepdims=True))
         squares.append(jnp.sum(square_f, axis=0, keepdims=True))
+
+    for f in range(0, count, 2):
+        prepare(f)
+        pair = matmul(cols, f, flat_out, both_2)
+        first, second = pair[:, :channels], pair[:, channels:]
+        if f == 0:
+            finish(f, first + part_ref[0, base : base + flat_out])
+            made[f + 1, :flat_out] = second + part_ref[1, base : base + flat_out]
+        else:
+            finish(f, first + made[f, :flat_out])
+            made[f + 1, :flat_out] = made[f + 1, :flat_out] + second
+        if f + 2 < count:
+            made[f + 2, :flat_out] = matmul(cols, f, flat_out, w0) + bias
+        prepare(f + 1)
+        finish(f + 1, matmul(cols, f + 1, flat_out, w2) + made[f + 1, :flat_out])
+        if f + 2 < count:
+            pair = matmul(cols, f + 1, flat_out, both_1)
+            made[f + 2, :flat_out] = made[f + 2, :flat_out] + pair[:, :channels]
+            made[f + 3, :flat_out] = pair[:, channels:] + bias
     if out_sums_ref is not None:
         out_sums_ref[0:1, :] = packed(jnp.concatenate(sums, axis=0), members)
         out_sums_ref[1:2, :] = packed(jnp.concatenate(squares, axis=0), members)
@@ -240,16 +239,13 @@
     return pl.pallas_call(
         body,
         out_shape=tuple(outs),
-        in_specs=[pl.BlockSpec(memory_space=pltpu.SMEM), vmem, vmem, vmem, pl.BlockSpec(memory_space=pltpu.HBM)]
-        + [vmem] * (len(inputs) - 5),
+        in_specs=[pl.BlockSpec(memory_space=pltpu.SMEM)] + [vmem] * (len(inputs) - 1),
         out_specs=tuple([vmem] * len(outs)),
         scratch_shapes=[
             pltpu.VMEM((count, full, channels), jnp.float32),
             pltpu.VMEM((count, full, channels), jnp.float32),
             pltpu.VMEM((count, rows_out * wide, TAPS * TAPS * channels), jnp.bfloat16),
             pltpu.VMEM((count, rows_out * wide, channels), jnp.float32),
-            pltpu.VMEM(kernel.shape, kernel.dtype),
-            pltpu.SemaphoreType.DMA,
         ],
         compiler_params=pltpu.CompilerParams(vmem_limit_bytes=VMEM_LIMIT),
     )(*inputs)
@@ -301,7 +297,6 @@
         x, result, sums = made
         hop = [(tick, tick + 1)]
         sums = lax.ppermute(sums, "section", hop)
-        sums, x = lax.optimization_barrier((sums, x))
         x = lax.ppermute(x, "section", hop)
         sums = of_everyone(sums)
     return result[None, :, None]

time: 231 us -> 236 us (1.022)
  waiting for transfers between devices: 76.4 us -> 85.7 us
  Pallas kernels: 20.5 us -> 16.3 us
    ppermute x3, waiting for transfers between devices: 10.2 us -> 19.5 us  [local(): sums = lax.ppermute(sums, 'section', hop)]
    pallas_call x4, Pallas kernels: 16.7 us -> 13.1 us  [section_step(): pl.pallas_call(body, out_shape=tuple(outs), in_specs=[pl.BlockSpec(memory...]
  transfers between devices with their start and end apart: 13 -> 13, of which waited for: 5 -> 5; matrix products, arithmetic and copies ran while one was open for 1% -> 1% of each run, Pallas kernels for 2% -> 1%
where the time goes in v4:
time: 236 us; the launch traced here: 235 us
  waiting for transfers between devices  85.7 us (36%)
  starting transfers between devices  84.7 us (36%)
  blocking collectives  43 us (18%)
  Pallas kernels  16.3 us (7%)
  local copies, waits for them, and re-layouts  3.33 us (1%)
    ppermute x4, starting transfers between devices, shifted(): lax.ppermute(array, 'tile', [(i, (i + by) % peers) for i in range(peers)])  52.8 us
    all_to_all x3, waiting for transfers between devices, of_everyone(): lax.all_to_all(copies, 'tile', 0, 0, tiled=True)  47.7 us
    all_to_all x1, blocking collectives, of_everyone(): lax.all_to_all(copies, 'tile', 0, 0, tiled=True)  43 us
    all_to_all x3, starting transfers between devices, of_everyone(): lax.all_to_all(copies, 'tile', 0, 0, tiled=True)  26.6 us
    ppermute x3, waiting for transfers between devices, local(): sums = lax.ppermute(sums, 'section', hop)  19.5 us
    ppermute x4, waiting for transfers between devices, shifted(): lax.ppermute(array, 'tile', [(i, (i + by) % peers) for i in range(peers)])  18.5 us
    pallas_call x4, Pallas kernels, section_step(): pl.pallas_call(body, out_shape=tuple(outs), in_specs=[pl.BlockSpec(memory...  13.1 us
  transfers between devices with their start and end apart: 13, of which 5 were waited for; matrix products, arithmetic and copies ran while one was open for 1% of the time, Pallas kernels for 1%

profile of v4, /device:TPU:46, one launch (start us, length us, event | category | flops | bytes accessed | tf_op | source)
XLA Modules:
  0.0 235.4 jit_solution(4559736087778784924)
XLA Ops:
  0.0 1.1 pad_maximum_fusion.4
  1.1 0.1 collective-permute-start
  1.2 43.0 %collective-permute-start.1 = (bf16[6,16,4,128]{3,2,1,0:T(4,128)(2,1)S(1)}, bf16[6,16,4,128]{3,2,1,0:T(4,128)(2,1)S(1)}, u32[]{:S(2)}, u32[]{:S(2)}) collective-permute-start(bf16[6,16,4,128]{3,2,1,0:T(4,128)(2,1)S(1)} %get-tuple-element.26), channel_id=1, source_target_pairs={{0,63},{1,0},{2,1},{3,2},{4,3},{5,4},{6,5},{7,6},{8,7},{9,8},{10,9... | collective-permute-start | bytes 294920 | tf_op jit(solution)/shard_map/ppermute | solution.py:19
  44.2 1.8 shard_map.64
  45.9 1.3 broadcast_in_dim.32
  47.3 6.5 %all-to-all-start = ((f32[64,1,256]{2,1,0:T(1,128)}), f32[64,1,256]{2,1,0:T(1,128)S(1)}, u32[]{:S(2)}, u32[]{:S(2)}) async-start(f32[64,1,256]{2,1,0:T(1,128)} %broadcast_in_dim.32), calls=%async_computation | async-start | bytes 131072 | tf_op jit(solution)/shard_map/all_to_all | solution.py:25
  53.8 0.3 pad_maximum_fusion
  54.2 6.4 %collective-permute-start.2 = (bf16[6,4,24,128]{3,2,1,0:T(8,128)(2,1)S(1)}, bf16[6,4,24,128]{3,2,1,0:T(8,128)(2,1)S(1)}, u32[]{:S(2)}, u32[]{:S(2)}) collective-permute-start(bf16[6,4,24,128]{3,2,1,0:T(8,128)(2,1)S(1)} %get-tuple-element.23), channel_id=1, source_target_pairs={{0,8},{1,9},{2,10},{3,11},{4,12},{5,13},{6,14},{7,15},{8,16},{9,17... | collective-permute-start | bytes 442376 | tf_op jit(solution)/shard_map/ppermute | solution.py:19
  60.5 3.5 %collective-permute-start.3 = (bf16[6,4,24,128]{3,2,1,0:T(8,128)(2,1)S(1)}, bf16[6,4,24,128]{3,2,1,0:T(8,128)(2,1)S(1)}, u32[]{:S(2)}, u32[]{:S(2)}) collective-permute-start(bf16[6,4,24,128]{3,2,1,0:T(8,128)(2,1)S(1)} %get-tuple-element.24), channel_id=1, source_target_pairs={{0,56},{1,57},{2,58},{3,59},{4,60},{5,61},{6,62},{7,63},{8,0},{9,1... | collective-permute-start | bytes 442376 | tf_op jit(solution)/shard_map/ppermute | solution.py:19
  64.0 0.1 stack.39.place_ref.refs_0_
  64.2 0.0 copy-start
  64.2 0.0 copy-start.1
  64.2 10.8 %collective-permute-done.2 = bf16[6,4,24,128]{3,2,1,0:T(8,128)(2,1)S(1)} collective-permute-done((bf16[6,4,24,128]{3,2,1,0:T(8,128)(2,1)S(1)}, bf16[6,4,24,128]{3,2,1,0:T(8,128)(2,1)S(1)}, u32[]{:S(2)}, u32[]{:S(2)}) %collective-permute-start.2) | collective-permute-done | bytes 147488 | tf_op jit(solution)/shard_map/ppermute | solution.py:19
  75.0 7.7 %collective-permute-done.3 = bf16[6,4,24,128]{3,2,1,0:T(8,128)(2,1)S(1)} collective-permute-done((bf16[6,4,24,128]{3,2,1,0:T(8,128)(2,1)S(1)}, bf16[6,4,24,128]{3,2,1,0:T(8,128)(2,1)S(1)}, u32[]{:S(2)}, u32[]{:S(2)}) %collective-permute-start.3) | collective-permute-done | bytes 147488 | tf_op jit(solution)/shard_map/ppermute | solution.py:19
  82.8 0.0 slice-start
  82.8 1.5 context.1.refs_3_
  84.3 0.0 copy-start.2
  84.3 0.0 copy-start.3
  84.4 0.1 pad_maximum_fusion.1
  84.4 0.0 all-to-all-done
  84.4 0.1 reduce_sum.36
  84.5 0.4 copy-done.2
  84.9 0.0 copy-done.3
  85.0 3.5 %shard_map.65 = (bf16[4,528,128]{2,1,0:T(8,128)(2,1)S(1)}, bf16[4,16,16,128]{3,2,1,0:T(8,128)(2,1)S(1)}, f32[2,128]{1,0:T(2,128)S(1)}) custom-call(s32[5]{0:T(128)S(1)} %stack.39.place_ref.refs_0_, bf16[4,576,128]{2,1,0:T(8,128)(2,1)S(1)} %bitcast.26, f32[2,128]{1,0:T(2,128)S(1)} %bitcast.31, f32[2,528,128]{2,1,0:T(8,128)S(1)} %context.1.refs_3_, ...), custom_call_target="tpu_custom_call" | custom-call | tf_op jit(solution)/shard_map/pallas_call | solution.py:239
  88.4 0.7 collective-permute-start.4
  89.1 0.7 collective-permute-start.5
  89.8 0.0 collective-permute-done.5
  89.9 43.0 %all_to_all.20 = f32[64,1,256]{2,1,0:T(1,128)S(1)} all-to-all(f32[64,1,256]{2,1,0:T(1,128)S(1)} %broadcast_in_dim.34), channel_id=1, replica_groups=mesh['parts'=2,'section'=4,'tile'=64] {'tile'}, dimensions={0} | all-to-all | bytes 131072 | tf_op jit(solution)/shard_map/all_to_all | solution.py:25
  132.8 0.1 reduce_sum.37
  132.9 0.0 collective-permute-done.4.refs_1_
  132.9 3.2 %shard_map.66 = (bf16[4,480,128]{2,1,0:T(8,128)(2,1)S(1)}, bf16[4,16,16,128]{3,2,1,0:T(8,128)(2,1)S(1)}, f32[2,128]{1,0:T(2,128)S(1)}) custom-call(s32[5]{0:T(128)S(1)} %stack.39.place_ref.refs_0_, bf16[4,528,128]{2,1,0:T(8,128)(2,1)S(1)} %collective-permute-done.4.refs_1_, f32[2,128]{1,0:T(2,128)S(1)} %bitcast.29, f32[2,528,128]{2,1,0:T(8,128)S(1)} %context.1.refs_3_, ...), custom_call_target="tpu_custom_call" | custom-call | tf_op jit(solution)/shard_map/pallas_call | solution.py:239
  136.1 0.7 collective-permute-start.7
  136.8 0.7 broadcast_in_dim.36
  137.5 6.7 %all-to-all-start.2 = ((f32[64,1,256]{2,1,0:T(1,128)}), f32[64,1,256]{2,1,0:T(1,128)S(1)}, u32[]{:S(2)}, u32[]{:S(2)}) async-start(f32[64,1,256]{2,1,0:T(1,128)} %broadcast_in_dim.36), calls=%async_computation.2 | async-start | bytes 131072 | tf_op jit(solution)/shard_map/all_to_all | solution.py:25
  144.1 0.7 collective-permute-start.6
  144.8 24.1 %all-to-all-done.2 = f32[64,1,256]{2,1,0:T(1,128)S(1)} async-done(((f32[64,1,256]{2,1,0:T(1,128)}), f32[64,1,256]{2,1,0:T(1,128)S(1)}, u32[]{:S(2)}, u32[]{:S(2)}) %all-to-all-start.2) | async-done | bytes 65568 | tf_op jit(solution)/shard_map/all_to_all | solution.py:25
  169.0 0.1 reduce_sum.38
  169.1 0.0 collective-permute-done.6.refs_1_
  169.1 3.1 %shard_map.67 = (bf16[4,432,128]{2,1,0:T(8,128)(2,1)S(1)}, bf16[4,16,16,128]{3,2,1,0:T(8,128)(2,1)S(1)}, f32[2,128]{1,0:T(2,128)S(1)}) custom-call(s32[5]{0:T(128)S(1)} %stack.39.place_ref.refs_0_, bf16[4,480,128]{2,1,0:T(8,128)(2,1)S(1)} %collective-permute-done.6.refs_1_, f32[2,128]{1,0:T(2,128)S(1)} %bitcast.30, f32[2,528,128]{2,1,0:T(8,128)S(1)} %context.1.refs_3_, ...), custom_call_target="tpu_custom_call" | custom-call | tf_op jit(solution)/shard_map/pallas_call | solution.py:239
  172.1 1.3 collective-permute-start.9
  173.5 19.5 %collective-permute-done.9 = f32[2,128]{1,0:T(2,128)S(1)} collective-permute-done((f32[2,128]{1,0:T(2,128)S(1)}, f32[2,128]{1,0:T(2,128)S(1)}, u32[]{:S(2)}, u32[]{:S(2)}) %collective-permute-start.9) | collective-permute-done | bytes 1056 | tf_op jit(solution)/shard_map/ppermute | solution.py:299
  193.0 0.7 broadcast_in_dim.38
  193.6 13.5 %all-to-all-start.3 = ((f32[64,1,256]{2,1,0:T(1,128)}), f32[64,1,256]{2,1,0:T(1,128)S(1)}, u32[]{:S(2)}, u32[]{:S(2)}) async-start(f32[64,1,256]{2,1,0:T(1,128)} %broadcast_in_dim.38), calls=%async_computation.3 | async-start | bytes 131072 | tf_op jit(solution)/shard_map/all_to_all | solution.py:25
  207.1 1.3 collective-permute-start.8
  208.4 23.6 %all-to-all-done.3 = f32[64,1,256]{2,1,0:T(1,128)S(1)} async-done(((f32[64,1,256]{2,1,0:T(1,128)}), f32[64,1,256]{2,1,0:T(1,128)S(1)}, u32[]{:S(2)}, u32[]{:S(2)}) %all-to-all-start.3) | async-done | bytes 65568 | tf_op jit(solution)/shard_map/all_to_all | solution.py:25
  232.0 0.1 reduce_sum.39
  232.1 0.0 collective-permute-done.8.refs_1_
  232.1 3.3 %shard_map.68 = bf16[4,16,16,128]{3,2,1,0:T(8,128)(2,1)} custom-call(s32[5]{0:T(128)S(1)} %stack.39.place_ref.refs_0_, bf16[4,432,128]{2,1,0:T(8,128)(2,1)S(1)} %collective-permute-done.8.refs_1_, f32[2,128]{1,0:T(2,128)S(1)} %bitcast.28, f32[2,528,128]{2,1,0:T(8,128)S(1)} %context.1.refs_3_, bf16[3,1152,128]{2,1,0:T(8,128)(2,1)S(1)} %bitcast.25, ...), custom_call_target="tpu_custom_call" | custom-call | tf_op jit(solution)/shard_map/pallas_call | solution.py:239
  (20 shorter events, 0.2 us)
Async XLA Ops:
  0.0 53.8 %copy-start.6 = (bf16[1,2,1,16,16,128]{5,4,3,2,1,0:T(8,128)(2,1)S(1)}, bf16[1,2,1,16,16,128]{5,4,3,2,1,0:T(8,128)(2,1)}, u32[]{:S(2)}) copy-start(bf16[1,2,1,16,16,128]{5,4,3,2,1,0:T(8,128)(2,1)} %param.7) | copy-start | bytes 393220
  0.0 53.8 %copy-start.5 = (bf16[4,1,16,16,128]{4,3,2,1,0:T(8,128)(2,1)S(1)}, bf16[4,1,16,16,128]{4,3,2,1,0:T(8,128)(2,1)}, u32[]{:S(2)}) copy-start(bf16[4,1,16,16,128]{4,3,2,1,0:T(8,128)(2,1)} %param.6) | copy-start | bytes 786436
  1.1 52.6 %collective-permute-start = (bf16[6,16,4,128]{3,2,1,0:T(4,128)(2,1)S(1)}, bf16[6,16,4,128]{3,2,1,0:T(4,128)(2,1)S(1)}, u32[]{:S(2)}, u32[]{:S(2)}) collective-permute-start(bf16[6,16,4,128]{3,2,1,0:T(4,128)(2,1)S(1)} %get-tuple-element.25), channel_id=1, source_target_pairs={{0,1},{1,2},{2,3},{3,4},{4,5},{5,6},{6,7},{7,8},{8,9},{9,10},{10,1... | collective-permute-start | bytes 294920 | tf_op jit(solution)/shard_map/ppermute | solution.py:19
  1.2 52.5 %collective-permute-start.1 = (bf16[6,16,4,128]{3,2,1,0:T(4,128)(2,1)S(1)}, bf16[6,16,4,128]{3,2,1,0:T(4,128)(2,1)S(1)}, u32[]{:S(2)}, u32[]{:S(2)}) collective-permute-start(bf16[6,16,4,128]{3,2,1,0:T(4,128)(2,1)S(1)} %get-tuple-element.26), channel_id=1, source_target_pairs={{0,63},{1,0},{2,1},{3,2},{4,3},{5,4},{6,5},{7,6},{8,7},{9,8},{10,9... | collective-permute-start | bytes 294920 | tf_op jit(solution)/shard_map/ppermute | solution.py:19
  47.3 37.2 %all-to-all-start = ((f32[64,1,256]{2,1,0:T(1,128)}), f32[64,1,256]{2,1,0:T(1,128)S(1)}, u32[]{:S(2)}, u32[]{:S(2)}) async-start(f32[64,1,256]{2,1,0:T(1,128)} %broadcast_in_dim.32), calls=%async_computation | async-start | bytes 131072 | tf_op jit(solution)/shard_map/all_to_all | solution.py:25
  54.1 10.1 %copy-start.4 = (bf16[6,16,24,128]{3,2,1,0:T(8,128)(2,1)}, bf16[6,16,24,128]{3,2,1,0:T(8,128)(2,1)S(1)}, u32[]{:S(2)}) copy-start(bf16[6,16,24,128]{3,2,1,0:T(8,128)(2,1)S(1)} %pad_maximum_fusion) | copy-start | bytes 1769476
  54.2 20.8 %collective-permute-start.2 = (bf16[6,4,24,128]{3,2,1,0:T(8,128)(2,1)S(1)}, bf16[6,4,24,128]{3,2,1,0:T(8,128)(2,1)S(1)}, u32[]{:S(2)}, u32[]{:S(2)}) collective-permute-start(bf16[6,4,24,128]{3,2,1,0:T(8,128)(2,1)S(1)} %get-tuple-element.23), channel_id=1, source_target_pairs={{0,8},{1,9},{2,10},{3,11},{4,12},{5,13},{6,14},{7,15},{8,16},{9,17... | collective-permute-start | bytes 442376 | tf_op jit(solution)/shard_map/ppermute | solution.py:19
  60.5 22.2 %collective-permute-start.3 = (bf16[6,4,24,128]{3,2,1,0:T(8,128)(2,1)S(1)}, bf16[6,4,24,128]{3,2,1,0:T(8,128)(2,1)S(1)}, u32[]{:S(2)}, u32[]{:S(2)}) collective-permute-start(bf16[6,4,24,128]{3,2,1,0:T(8,128)(2,1)S(1)} %get-tuple-element.24), channel_id=1, source_target_pairs={{0,56},{1,57},{2,58},{3,59},{4,60},{5,61},{6,62},{7,63},{8,0},{9,1... | collective-permute-start | bytes 442376 | tf_op jit(solution)/shard_map/ppermute | solution.py:19
  64.2 18.6 %copy-start = (bf16[1,3,3,3,128,128]{5,4,3,2,1,0:T(8,128)(2,1)S(1)}, bf16[1,3,3,3,128,128]{5,4,3,2,1,0:T(8,128)(2,1)}, u32[]{:S(2)}) copy-start(bf16[1,3,3,3,128,128]{5,4,3,2,1,0:T(8,128)(2,1)} %param.8) | copy-start | bytes 2654212
  64.2 18.6 %copy-start.1 = (f32[1,128]{1,0:T(1,128)S(1)}, f32[1,128]{1,0:T(1,128)}, u32[]{:S(2)}) copy-start(f32[1,128]{1,0:T(1,128)} %refs_5_.7) | copy-start | bytes 1540
  82.8 1.6 slice-start
  84.3 0.7 copy-start.2
  84.3 0.7 copy-start.3
  88.4 44.5 %collective-permute-start.4 = (bf16[4,528,128]{2,1,0:T(8,128)(2,1)S(1)}, bf16[4,528,128]{2,1,0:T(8,128)(2,1)S(1)}, u32[]{:S(2)}, u32[]{:S(2)}) collective-permute-start(bf16[4,528,128]{2,1,0:T(8,128)(2,1)S(1)} %get-tuple-element.14), channel_id=1, source_target_pairs={{0,64},{1,65},{2,66},{3,67},{4,68},{5,69},{6,70},{7,71},{8,72},{9,... | collective-permute-start | bytes 1622024 | tf_op jit(solution)/shard_map/ppermute | solution.py:300
  89.1 0.7 collective-permute-start.5
  136.1 0.7 collective-permute-start.7
  137.5 31.5 %all-to-all-start.2 = ((f32[64,1,256]{2,1,0:T(1,128)}), f32[64,1,256]{2,1,0:T(1,128)S(1)}, u32[]{:S(2)}, u32[]{:S(2)}) async-start(f32[64,1,256]{2,1,0:T(1,128)} %broadcast_in_dim.36), calls=%async_computation.2 | async-start | bytes 131072 | tf_op jit(solution)/shard_map/all_to_all | solution.py:25
  144.1 24.9 %collective-permute-start.6 = (bf16[4,480,128]{2,1,0:T(8,128)(2,1)S(1)}, bf16[4,480,128]{2,1,0:T(8,128)(2,1)S(1)}, u32[]{:S(2)}, u32[]{:S(2)}) collective-permute-start(bf16[4,480,128]{2,1,0:T(8,128)(2,1)S(1)} %get-tuple-element.17), channel_id=1, source_target_pairs={{64,128},{65,129},{66,130},{67,131},{68,132},{69,133},{70,134},{71... | collective-permute-start | bytes 1474568 | tf_op jit(solution)/shard_map/ppermute | solution.py:300
  172.1 20.8 %collective-permute-start.9 = (f32[2,128]{1,0:T(2,128)S(1)}, f32[2,128]{1,0:T(2,128)S(1)}, u32[]{:S(2)}, u32[]{:S(2)}) collective-permute-start(f32[2,128]{1,0:T(2,128)S(1)} %get-tuple-element.21), channel_id=1, source_target_pairs={{128,192},{129,193},{130,194},{131,195},{132,196},{133,197},{134,1... | collective-permute-start | bytes 3080 | tf_op jit(solution)/shard_map/ppermute | solution.py:299
  193.6 38.4 %all-to-all-start.3 = ((f32[64,1,256]{2,1,0:T(1,128)}), f32[64,1,256]{2,1,0:T(1,128)S(1)}, u32[]{:S(2)}, u32[]{:S(2)}) async-start(f32[64,1,256]{2,1,0:T(1,128)} %broadcast_in_dim.38), calls=%async_computation.3 | async-start | bytes 131072 | tf_op jit(solution)/shard_map/all_to_all | solution.py:25
  207.1 25.0 %collective-permute-start.8 = (bf16[4,432,128]{2,1,0:T(8,128)(2,1)S(1)}, bf16[4,432,128]{2,1,0:T(8,128)(2,1)S(1)}, u32[]{:S(2)}, u32[]{:S(2)}) collective-permute-start(bf16[4,432,128]{2,1,0:T(8,128)(2,1)S(1)} %get-tuple-element.20), channel_id=1, source_target_pairs={{128,192},{129,193},{130,194},{131,195},{132,196},{133,197},{134,1... | collective-permute-start | bytes 1327112 | tf_op jit(solution)/shard_map/ppermute | solution.py:300

commit v5 on v4

--- a/solution.py
+++ b/solution.py
@@ -19,10 +19,36 @@
     return lax.ppermute(array, "tile", [(i, (i + by) % peers) for i in range(peers)])
 
 
+def both_cores(sums):
+    pairs = [[i, i + 1] for i in range(0, lax.axis_size("tile"), 2)]
+    return jnp.sum(lax.all_gather(sums, "tile", axis_index_groups=pairs), axis=0)
+
+
+def to_next(sums, section):
+    tiles = lax.axis_size("tile")
+    axes = ("section", "tile")
+    here, there = section * tiles, (section + 1) * tiles
+    same = lax.ppermute(sums, axes, [(here + t, there + t) for t in range(tiles)])
+    other = lax.ppermute(sums, axes, [(here + t, there + (t ^ 1)) for t in range(tiles)])
+    return same + other
+
+
 def of_everyone(sums):
-    peers = lax.axis_size("tile")
-    copies = jnp.broadcast_to(sums.reshape(1, 1, sums.size), (peers, 1, sums.size))
-    return jnp.sum(lax.all_to_all(copies, "tile", 0, 0, tiled=True), axis=0).reshape(sums.shape)
+    chips = lax.axis_size("tile") // 2
+    groups = [[core + 2 * i for i in range(chips)] for core in range(2)]
+    copies = jnp.broadcast_to(sums.reshape(1, 1, sums.size), (chips, 1, sums.size))
+    all_sums = lax.all_to_all(copies, "tile", 0, 0, tiled=True, axis_index_groups=groups)
+    return jnp.sum(all_sums, axis=0).reshape(sums.shape)
+
+
+def swapped(array, across, first):
+    tiles = lax.axis_size("tile")
+    pairs = []
+    for t in range(tiles):
+        placed = (t + across + 2) % tiles
+        down = ((placed // across) % 2 == 0) == first
+        pairs.append((t, (t + (across if down else -across)) % tiles))
+    return lax.ppermute(array, "tile", pairs)
 
 
 def over_lanes(value, members):
@@ -65,6 +91,8 @@
         out_shape=jax.ShapeDtypeStruct((2, frames.shape[-1]), jnp.float32),
         in_specs=[pl.BlockSpec(memory_space=pltpu.VMEM)],
         out_specs=pl.BlockSpec(memory_space=pltpu.VMEM),
+        compiler_params=pltpu.CompilerParams(vmem_limit_bytes=VMEM_LIMIT),
+        name="first_sums",
     )(frames)
 
 
@@ -277,8 +305,13 @@
     left = shifted(seq[:, :, side - halo :], 1)
     right = shifted(seq[:, :, :halo], -1)
     middle = jnp.concatenate([left, seq, right], axis=2)
-    above = shifted(middle[:, side - halo :], across)
-    below = shifted(middle[:, :halo], -across)
+    even = row_at % 2 == 0
+    top, bottom = middle[:, :halo], middle[:, side - halo :]
+    one = swapped(jnp.where(even, bottom, top), across, True)
+    two = swapped(jnp.where(even, top, bottom), across, False)
+    above = jnp.where(even, two, one)
+    below = jnp.where(even, one, two)
+    sums = both_cores(sums)
     sums = of_everyone(sums)
     held_cache, x = (
         jnp.concatenate([above[c], middle[c], below[c]], axis=1).reshape(-1, wide * wide, channels)
@@ -296,7 +329,7 @@
             break
         x, result, sums = made
         hop = [(tick, tick + 1)]
-        sums = lax.ppermute(sums, "section", hop)
+        sums = to_next(sums, tick)
         x = lax.ppermute(x, "section", hop)
         sums = of_everyone(sums)
     return result[None, :, None]

time: 236 us -> 219 us (0.928)
  waiting for transfers between devices: 85.7 us -> 46.2 us
  blocking collectives: 43 us -> 80.5 us
  starting transfers between devices: 84.7 us -> 72 us
    all_to_all x1 -> x3, blocking collectives: 43 us -> 78.6 us  [of_everyone(): lax.all_to_all(copies, 'tile', 0, 0, tiled=True, axis_index_groups=groups)]
    all_to_all x3 -> x1, waiting for transfers between devices: 47.7 us -> 19.9 us  [of_everyone(): lax.all_to_all(copies, 'tile', 0, 0, tiled=True, axis_index_groups=groups)]
    ppermute x4 -> x2, waiting for transfers between devices: 18.5 us -> 2.24 us  [shifted(): lax.ppermute(array, 'tile', [(i, (i + by) % peers) for i in range(peers)])]
    all_to_all x3 -> x1, starting transfers between devices: 26.6 us -> 14.8 us  [of_everyone(): lax.all_to_all(copies, 'tile', 0, 0, tiled=True, axis_index_groups=groups)]
    ppermute x4 -> x2, starting transfers between devices: 52.8 us -> 43 us  [shifted(): lax.ppermute(array, 'tile', [(i, (i + by) % peers) for i in range(peers)])]
    ppermute x3 -> x8, starting transfers between devices: 2.62 us -> 11.4 us  [the longest x2 6.18 us: swapped(): return lax.ppermute(array, 'tile', pairs)]
    ppermute x3 -> x8, waiting for transfers between devices: 19.5 us -> 24.1 us  [the longest x3 20.6 us: to_next(): lax.ppermute(sums, axes, [(here + t, there + (t ^ 1)) for t in range(tile...]
  transfers between devices with their start and end apart: 13 -> 14, of which waited for: 5 -> 4; matrix products, arithmetic and copies ran while one was open for 1% -> 1% of each run, Pallas kernels for 1% -> 1%
where the time goes in v5:
time: 219 us
  blocking collectives  80.5 us (37%)
  starting transfers between devices  72 us (33%)
  waiting for transfers between devices  46.2 us (21%)
  Pallas kernels  14.8 us (7%)
  other arithmetic  2.79 us (1%)
    all_to_all x3, blocking collectives, of_everyone(): lax.all_to_all(copies, 'tile', 0, 0, tiled=True, axis_index_groups=groups)  78.6 us
    ppermute x2, starting transfers between devices, shifted(): lax.ppermute(array, 'tile', [(i, (i + by) % peers) for i in range(peers)])  43 us
    ppermute x3, waiting for transfers between devices, to_next(): lax.ppermute(sums, axes, [(here + t, there + (t ^ 1)) for t in range(tile...  20.6 us
    all_to_all x1, waiting for transfers between devices, of_everyone(): lax.all_to_all(copies, 'tile', 0, 0, tiled=True, axis_index_groups=groups)  19.9 us
    all_to_all x1, starting transfers between devices, of_everyone(): lax.all_to_all(copies, 'tile', 0, 0, tiled=True, axis_index_groups=groups)  14.8 us
    pallas_call x4, Pallas kernels, section_step(): pl.pallas_call(body, out_shape=tuple(outs), in_specs=[pl.BlockSpec(memory...  13.1 us
    ppermute x2, starting transfers between devices, swapped(): return lax.ppermute(array, 'tile', pairs)  6.18 us
  transfers between devices with their start and end apart: 14, of which 4 were waited for; matrix products, arithmetic and copies ran while one was open for 1% of the time, Pallas kernels for 1%

profile of v5, /device:TPU:46, one launch (start us, length us, event | category | flops | bytes accessed | tf_op | source)
XLA Modules:
  0.0 218.6 jit_solution(15541185006705926412)
XLA Ops:
  0.0 1.1 pad_maximum_fusion.4
  1.1 0.1 collective-permute-start
  1.2 43.0 %collective-permute-start.1 = (bf16[6,16,4,128]{3,2,1,0:T(4,128)(2,1)S(1)}, bf16[6,16,4,128]{3,2,1,0:T(4,128)(2,1)S(1)}, u32[]{:S(2)}, u32[]{:S(2)}) collective-permute-start(bf16[6,16,4,128]{3,2,1,0:T(4,128)(2,1)S(1)} %get-tuple-element.26), channel_id=1, source_target_pairs={{0,63},{1,0},{2,1},{3,2},{4,3},{5,4},{6,5},{7,6},{8,7},{9,8},{10,9... | collective-permute-start | bytes 294920 | tf_op jit(solution)/shard_map/ppermute | solution.py:19
  44.1 2.2 %collective-permute-done = bf16[6,16,4,128]{3,2,1,0:T(4,128)(2,1)S(1)} collective-permute-done((bf16[6,16,4,128]{3,2,1,0:T(4,128)(2,1)S(1)}, bf16[6,16,4,128]{3,2,1,0:T(4,128)(2,1)S(1)}, u32[]{:S(2)}, u32[]{:S(2)}) %collective-permute-start) | collective-permute-done | bytes 98336 | tf_op jit(solution)/shard_map/ppermute | solution.py:19
  46.4 0.0 collective-permute-done.1
  46.4 1.3 pad_maximum_fusion
  47.7 2.0 collective-permute-start.2
  49.7 4.2 %collective-permute-start.3 = (bf16[6,4,24,128]{3,2,1,0:T(8,128)(2,1)S(1)}, bf16[6,4,24,128]{3,2,1,0:T(8,128)(2,1)S(1)}, u32[]{:S(2)}, u32[]{:S(2)}) collective-permute-start(bf16[6,4,24,128]{3,2,1,0:T(8,128)(2,1)S(1)} %get-tuple-element.24), channel_id=1, source_target_pairs={{0,56},{1,57},{2,58},{3,59},{4,60},{5,61},{6,14},{7,15},{8,16},{9,... | collective-permute-start | bytes 442376 | tf_op jit(solution)/shard_map/ppermute | solution.py:51
  53.9 0.2 first_sums.1
  54.1 1.9 all-gather.1
  56.0 0.6 broadcast_in_dim.32
  56.7 14.8 %all-to-all-start = ((f32[32,1,256]{2,1,0:T(1,128)}), f32[32,1,256]{2,1,0:T(1,128)S(1)}, u32[]{:S(2)}, u32[]{:S(2)}) async-start(f32[32,1,256]{2,1,0:T(1,128)} %broadcast_in_dim.32), calls=%async_computation | async-start | bytes 65536 | tf_op jit(solution)/shard_map/all_to_all | solution.py:40
  71.5 0.1 stack.39.place_ref.refs_0_
  71.6 0.0 collective-permute-done.2
  71.6 0.0 slice-start
  71.6 0.0 collective-permute-done.3
  71.7 1.1 slice-done
  72.9 0.0 slice-start.1
  72.9 1.5 context.1.refs_3_
  74.4 0.0 copy-start.3
  74.4 0.0 copy-start.4
  74.4 0.1 pad_maximum_fusion.1
  74.5 19.9 %all-to-all-done = f32[32,1,256]{2,1,0:T(1,128)S(1)} async-done(((f32[32,1,256]{2,1,0:T(1,128)}), f32[32,1,256]{2,1,0:T(1,128)S(1)}, u32[]{:S(2)}, u32[]{:S(2)}) %all-to-all-start) | async-done | bytes 32800 | tf_op jit(solution)/shard_map/all_to_all | solution.py:40
  94.4 0.1 reduce_sum.46
  94.5 3.5 %shard_map.64 = (bf16[4,528,128]{2,1,0:T(8,128)(2,1)S(1)}, bf16[4,16,16,128]{3,2,1,0:T(8,128)(2,1)S(1)}, f32[2,128]{1,0:T(2,128)S(1)}) custom-call(s32[5]{0:T(128)S(1)} %stack.39.place_ref.refs_0_, bf16[4,576,128]{2,1,0:T(8,128)(2,1)S(1)} %bitcast.30, f32[2,128]{1,0:T(2,128)S(1)} %bitcast.38, f32[2,528,128]{2,1,0:T(8,128)S(1)} %context.1.refs_3_, ...), custom_call_target="tpu_custom_call" | custom-call | tf_op jit(solution)/shard_map/pallas_call | solution.py:267
  98.0 0.7 collective-permute-start.4
  98.7 0.7 collective-permute-start.6
  99.4 0.7 collective-permute-start.5
  100.0 0.0 collective-permute-done.5
  100.1 26.2 %all_to_all.20 = f32[32,1,256]{2,1,0:T(1,128)S(1)} all-to-all(f32[32,1,256]{2,1,0:T(1,128)S(1)} %broadcast_in_dim.34), channel_id=1, replica_groups={{0,2,4,6,8,10,12,14,16,18,20,22,24,26,28,30,32,34,36,38,40,42,44,46,48,..., dimensions={0} | all-to-all | bytes 65536 | tf_op jit(solution)/shard_map/all_to_all | solution.py:40
  126.3 0.1 reduce_sum.47
  126.4 3.2 %shard_map.65 = (bf16[4,480,128]{2,1,0:T(8,128)(2,1)S(1)}, bf16[4,16,16,128]{3,2,1,0:T(8,128)(2,1)S(1)}, f32[2,128]{1,0:T(2,128)S(1)}) custom-call(s32[5]{0:T(128)S(1)} %stack.39.place_ref.refs_0_, bf16[4,528,128]{2,1,0:T(8,128)(2,1)S(1)} %collective-permute-done.4.refs_1_, f32[2,128]{1,0:T(2,128)S(1)} %bitcast.36, f32[2,528,128]{2,1,0:T(8,128)S(1)} %context.1.refs_3_, ...), custom_call_target="tpu_custom_call" | custom-call | tf_op jit(solution)/shard_map/pallas_call | solution.py:267
  129.6 0.7 collective-permute-start.7
  130.3 0.7 collective-permute-start.9
  130.9 0.7 collective-permute-start.8
  131.6 0.0 collective-permute-done.9
  131.7 26.2 %all_to_all.21 = f32[32,1,256]{2,1,0:T(1,128)S(1)} all-to-all(f32[32,1,256]{2,1,0:T(1,128)S(1)} %broadcast_in_dim.36), channel_id=1, replica_groups={{0,2,4,6,8,10,12,14,16,18,20,22,24,26,28,30,32,34,36,38,40,42,44,46,48,..., dimensions={0} | all-to-all | bytes 65536 | tf_op jit(solution)/shard_map/all_to_all | solution.py:40
  157.9 0.1 reduce_sum.48
  157.9 3.1 %shard_map.66 = (bf16[4,432,128]{2,1,0:T(8,128)(2,1)S(1)}, bf16[4,16,16,128]{3,2,1,0:T(8,128)(2,1)S(1)}, f32[2,128]{1,0:T(2,128)S(1)}) custom-call(s32[5]{0:T(128)S(1)} %stack.39.place_ref.refs_0_, bf16[4,480,128]{2,1,0:T(8,128)(2,1)S(1)} %collective-permute-done.7.refs_1_, f32[2,128]{1,0:T(2,128)S(1)} %bitcast.37, f32[2,528,128]{2,1,0:T(8,128)S(1)} %context.1.refs_3_, ...), custom_call_target="tpu_custom_call" | custom-call | tf_op jit(solution)/shard_map/pallas_call | solution.py:267
  161.0 1.3 collective-permute-start.12
  162.3 1.3 collective-permute-start.11
  163.6 1.3 collective-permute-start.10
  164.9 20.5 %collective-permute-done.12 = f32[2,128]{1,0:T(2,128)S(1)} collective-permute-done((f32[2,128]{1,0:T(2,128)S(1)}, f32[2,128]{1,0:T(2,128)S(1)}, u32[]{:S(2)}, u32[]{:S(2)}) %collective-permute-start.12) | collective-permute-done | bytes 1056 | tf_op jit(solution)/shard_map/ppermute | solution.py:32
  185.5 3.5 %collective-permute-done.11 = f32[2,128]{1,0:T(2,128)S(1)} collective-permute-done((f32[2,128]{1,0:T(2,128)S(1)}, f32[2,128]{1,0:T(2,128)S(1)}, u32[]{:S(2)}, u32[]{:S(2)}) %collective-permute-start.11) | collective-permute-done | bytes 1056 | tf_op jit(solution)/shard_map/ppermute | solution.py:31
  189.0 26.2 %all_to_all.22 = f32[32,1,256]{2,1,0:T(1,128)S(1)} all-to-all(f32[32,1,256]{2,1,0:T(1,128)S(1)} %broadcast_in_dim.38), channel_id=1, replica_groups={{0,2,4,6,8,10,12,14,16,18,20,22,24,26,28,30,32,34,36,38,40,42,44,46,48,..., dimensions={0} | all-to-all | bytes 65536 | tf_op jit(solution)/shard_map/all_to_all | solution.py:40
  215.2 0.1 reduce_sum.49
  215.3 0.0 collective-permute-done.10.refs_1_
  215.3 3.3 %shard_map.67 = bf16[4,16,16,128]{3,2,1,0:T(8,128)(2,1)} custom-call(s32[5]{0:T(128)S(1)} %stack.39.place_ref.refs_0_, bf16[4,432,128]{2,1,0:T(8,128)(2,1)S(1)} %collective-permute-done.10.refs_1_, f32[2,128]{1,0:T(2,128)S(1)} %bitcast.35, f32[2,528,128]{2,1,0:T(8,128)S(1)} %context.1.refs_3_, bf16[3,1152,128]{2,1,0:T(8,128)(2,1)S(1)} %bitcast.29, ...), custom_call_target="tpu_custom_call" | custom-call | tf_op jit(solution)/shard_map/pallas_call | solution.py:267
  (29 shorter events, 0.2 us)
Async XLA Ops:
  1.1 45.3 %collective-permute-start = (bf16[6,16,4,128]{3,2,1,0:T(4,128)(2,1)S(1)}, bf16[6,16,4,128]{3,2,1,0:T(4,128)(2,1)S(1)}, u32[]{:S(2)}, u32[]{:S(2)}) collective-permute-start(bf16[6,16,4,128]{3,2,1,0:T(4,128)(2,1)S(1)} %get-tuple-element.25), channel_id=1, source_target_pairs={{0,1},{1,2},{2,3},{3,4},{4,5},{5,6},{6,7},{7,8},{8,9},{9,10},{10,1... | collective-permute-start | bytes 294920 | tf_op jit(solution)/shard_map/ppermute | solution.py:19
  1.2 45.2 %collective-permute-start.1 = (bf16[6,16,4,128]{3,2,1,0:T(4,128)(2,1)S(1)}, bf16[6,16,4,128]{3,2,1,0:T(4,128)(2,1)S(1)}, u32[]{:S(2)}, u32[]{:S(2)}) collective-permute-start(bf16[6,16,4,128]{3,2,1,0:T(4,128)(2,1)S(1)} %get-tuple-element.26), channel_id=1, source_target_pairs={{0,63},{1,0},{2,1},{3,2},{4,3},{5,4},{6,5},{7,6},{8,7},{9,8},{10,9... | collective-permute-start | bytes 294920 | tf_op jit(solution)/shard_map/ppermute | solution.py:19
  44.1 9.8 %copy-start.1 = (bf16[4,1,16,16,128]{4,3,2,1,0:T(8,128)(2,1)S(1)}, bf16[4,1,16,16,128]{4,3,2,1,0:T(8,128)(2,1)}, u32[]{:S(2)}) copy-start(bf16[4,1,16,16,128]{4,3,2,1,0:T(8,128)(2,1)} %param.6) | copy-start | bytes 786436
  47.7 23.9 %copy-start.5 = (bf16[6,16,24,128]{3,2,1,0:T(8,128)(2,1)}, bf16[6,16,24,128]{3,2,1,0:T(8,128)(2,1)S(1)}, u32[]{:S(2)}) copy-start(bf16[6,16,24,128]{3,2,1,0:T(8,128)(2,1)S(1)} %pad_maximum_fusion) | copy-start | bytes 1769476
  47.7 23.9 %collective-permute-start.2 = (bf16[6,4,24,128]{3,2,1,0:T(8,128)(2,1)S(1)}, bf16[6,4,24,128]{3,2,1,0:T(8,128)(2,1)S(1)}, u32[]{:S(2)}, u32[]{:S(2)}) collective-permute-start(bf16[6,4,24,128]{3,2,1,0:T(8,128)(2,1)S(1)} %get-tuple-element.23), channel_id=1, source_target_pairs={{0,8},{1,9},{2,10},{3,11},{4,12},{5,13},{6,62},{7,63},{8,0},{9,1},... | collective-permute-start | bytes 442376 | tf_op jit(solution)/shard_map/ppermute | solution.py:51
  49.7 22.0 %collective-permute-start.3 = (bf16[6,4,24,128]{3,2,1,0:T(8,128)(2,1)S(1)}, bf16[6,4,24,128]{3,2,1,0:T(8,128)(2,1)S(1)}, u32[]{:S(2)}, u32[]{:S(2)}) collective-permute-start(bf16[6,4,24,128]{3,2,1,0:T(8,128)(2,1)S(1)} %get-tuple-element.24), channel_id=1, source_target_pairs={{0,56},{1,57},{2,58},{3,59},{4,60},{5,61},{6,14},{7,15},{8,16},{9,... | collective-permute-start | bytes 442376 | tf_op jit(solution)/shard_map/ppermute | solution.py:51
  56.7 37.8 %all-to-all-start = ((f32[32,1,256]{2,1,0:T(1,128)}), f32[32,1,256]{2,1,0:T(1,128)S(1)}, u32[]{:S(2)}, u32[]{:S(2)}) async-start(f32[32,1,256]{2,1,0:T(1,128)} %broadcast_in_dim.32), calls=%async_computation | async-start | bytes 65536 | tf_op jit(solution)/shard_map/all_to_all | solution.py:40
  71.6 1.3 copy-start
  71.6 1.3 copy-start.2
  71.6 1.2 slice-start
  72.9 1.5 slice-start.1
  74.4 20.1 %copy-start.3 = (f32[1,128]{1,0:T(1,128)S(1)}, f32[1,128]{1,0:T(1,128)}, u32[]{:S(2)}) copy-start(f32[1,128]{1,0:T(1,128)} %refs_6_.7) | copy-start | bytes 1540
  74.4 20.1 %copy-start.4 = (f32[1,128]{1,0:T(1,128)S(1)}, f32[1,128]{1,0:T(1,128)}, u32[]{:S(2)}) copy-start(f32[1,128]{1,0:T(1,128)} %refs_7_.7) | copy-start | bytes 1540
  98.0 28.4 %collective-permute-start.4 = (bf16[4,528,128]{2,1,0:T(8,128)(2,1)S(1)}, bf16[4,528,128]{2,1,0:T(8,128)(2,1)S(1)}, u32[]{:S(2)}, u32[]{:S(2)}) collective-permute-start(bf16[4,528,128]{2,1,0:T(8,128)(2,1)S(1)} %get-tuple-element.14), channel_id=1, source_target_pairs={{0,64},{1,65},{2,66},{3,67},{4,68},{5,69},{6,70},{7,71},{8,72},{9,... | collective-permute-start | bytes 1622024 | tf_op jit(solution)/shard_map/ppermute | solution.py:333
  98.7 1.3 collective-permute-start.6
  99.4 0.7 collective-permute-start.5
  129.6 28.3 %collective-permute-start.7 = (bf16[4,480,128]{2,1,0:T(8,128)(2,1)S(1)}, bf16[4,480,128]{2,1,0:T(8,128)(2,1)S(1)}, u32[]{:S(2)}, u32[]{:S(2)}) collective-permute-start(bf16[4,480,128]{2,1,0:T(8,128)(2,1)S(1)} %get-tuple-element.17), channel_id=1, source_target_pairs={{64,128},{65,129},{66,130},{67,131},{68,132},{69,133},{70,134},{71... | collective-permute-start | bytes 1474568 | tf_op jit(solution)/shard_map/ppermute | solution.py:333
  130.3 1.3 collective-permute-start.9
  130.9 0.7 collective-permute-start.8
  161.0 24.5 %collective-permute-start.12 = (f32[2,128]{1,0:T(2,128)S(1)}, f32[2,128]{1,0:T(2,128)S(1)}, u32[]{:S(2)}, u32[]{:S(2)}) collective-permute-start(f32[2,128]{1,0:T(2,128)S(1)} %get-tuple-element.21), channel_id=1, source_target_pairs={{128,193},{129,192},{130,195},{131,194},{132,197},{133,196},{134,1... | collective-permute-start | bytes 3080 | tf_op jit(solution)/shard_map/ppermute | solution.py:32
  162.3 26.7 %collective-permute-start.11 = (f32[2,128]{1,0:T(2,128)S(1)}, f32[2,128]{1,0:T(2,128)S(1)}, u32[]{:S(2)}, u32[]{:S(2)}) collective-permute-start(f32[2,128]{1,0:T(2,128)S(1)} %get-tuple-element.21), channel_id=1, source_target_pairs={{128,192},{129,193},{130,194},{131,195},{132,196},{133,197},{134,1... | collective-permute-start | bytes 3080 | tf_op jit(solution)/shard_map/ppermute | solution.py:31
  163.6 51.7 %collective-permute-start.10 = (bf16[4,432,128]{2,1,0:T(8,128)(2,1)S(1)}, bf16[4,432,128]{2,1,0:T(8,128)(2,1)S(1)}, u32[]{:S(2)}, u32[]{:S(2)}) collective-permute-start(bf16[4,432,128]{2,1,0:T(8,128)(2,1)S(1)} %get-tuple-element.20), channel_id=1, source_target_pairs={{128,192},{129,193},{130,194},{131,195},{132,196},{133,197},{134,1... | collective-permute-start | bytes 1327112 | tf_op jit(solution)/shard_map/ppermute | solution.py:333

commit v6 on v5

--- a/solution.py
+++ b/solution.py
@@ -35,20 +35,11 @@
 
 def of_everyone(sums):
     chips = lax.axis_size("tile") // 2
-    groups = [[core + 2 * i for i in range(chips)] for core in range(2)]
+    ends = [i // 2 if i % 2 == 0 else chips - 1 - i // 2 for i in range(chips)]
+    groups = [[core + 2 * i for i in ends] for core in range(2)]
     copies = jnp.broadcast_to(sums.reshape(1, 1, sums.size), (chips, 1, sums.size))
     all_sums = lax.all_to_all(copies, "tile", 0, 0, tiled=True, axis_index_groups=groups)
     return jnp.sum(all_sums, axis=0).reshape(sums.shape)
-
-
-def swapped(array, across, first):
-    tiles = lax.axis_size("tile")
-    pairs = []
-    for t in range(tiles):
-        placed = (t + across + 2) % tiles
-        down = ((placed // across) % 2 == 0) == first
-        pairs.append((t, (t + (across if down else -across)) % tiles))
-    return lax.ppermute(array, "tile", pairs)
 
 
 def over_lanes(value, members):
@@ -77,17 +68,16 @@
     return over_lanes(jnp.where(lane % members == frame, row, 0.0), members)
 
 
-def sums_kernel(members, x_ref, sums_ref):
-    values = x_ref[...].astype(jnp.float32)
-    count = values.shape[0]
+def sums_kernel(count, members, x_ref, sums_ref):
+    values = x_ref[x_ref.shape[0] - count :].astype(jnp.float32)
     values = values.reshape(count, -1, values.shape[-1])
     sums_ref[0:1, :] = packed(jnp.sum(values, axis=1), members)
     sums_ref[1:2, :] = packed(jnp.sum(values * values, axis=1), members)
 
 
-def first_sums(frames, members):
+def first_sums(frames, count, members):
     return pl.pallas_call(
-        functools.partial(sums_kernel, members),
+        functools.partial(sums_kernel, count, members),
         out_shape=jax.ShapeDtypeStruct((2, frames.shape[-1]), jnp.float32),
         in_specs=[pl.BlockSpec(memory_space=pltpu.VMEM)],
         out_specs=pl.BlockSpec(memory_space=pltpu.VMEM),
@@ -300,18 +290,14 @@
 
     old = cache[0, :, 0]
     context = old.shape[0]
-    sums = first_sums(x, members)
-    seq = jnp.concatenate([old, x], axis=0)
+    seq = lax.optimization_barrier(jnp.concatenate([old, x], axis=0))
     left = shifted(seq[:, :, side - halo :], 1)
     right = shifted(seq[:, :, :halo], -1)
+    sums = both_cores(first_sums(seq, count, members))
+    left, right, sums = lax.optimization_barrier((left, right, sums))
     middle = jnp.concatenate([left, seq, right], axis=2)
-    even = row_at % 2 == 0
-    top, bottom = middle[:, :halo], middle[:, side - halo :]
-    one = swapped(jnp.where(even, bottom, top), across, True)
-    two = swapped(jnp.where(even, top, bottom), across, False)
-    above = jnp.where(even, two, one)
-    below = jnp.where(even, one, two)
-    sums = both_cores(sums)
+    above = shifted(middle[:, side - halo :], across)
+    below = shifted(middle[:, :halo], -across)
     sums = of_everyone(sums)
     held_cache, x = (
         jnp.concatenate([above[c], middle[c], below[c]], axis=1).reshape(-1, wide * wide, channels)

time: 219 us -> 209 us (0.954)
  starting transfers between devices: 72 us -> 65.5 us
    all_to_all x1, starting transfers between devices: 14.8 us -> 4.77 us  [of_everyone(): lax.all_to_all(copies, 'tile', 0, 0, tiled=True, axis_index_groups=groups)]
    ppermute x2 -> x4, starting transfers between devices: 43 us -> 52.8 us  [shifted(): lax.ppermute(array, 'tile', [(i, (i + by) % peers) for i in range(peers)])]
    ppermute x2 -> x0, starting transfers between devices: 6.18 us -> none  [swapped(): return lax.ppermute(array, 'tile', pairs)]
    ppermute x2 -> x4, waiting for transfers between devices: 2.24 us -> 5.12 us  [shifted(): lax.ppermute(array, 'tile', [(i, (i + by) % peers) for i in range(peers)])]
    all_to_all x1, waiting for transfers between devices: 19.9 us -> 17.5 us  [of_everyone(): lax.all_to_all(copies, 'tile', 0, 0, tiled=True, axis_index_groups=groups)]
  transfers between devices with their start and end apart: 14 -> 14, of which waited for: 4 -> 7; matrix products, arithmetic and copies ran while one was open for 1% -> 1% of each run, Pallas kernels for 1% -> 1%
where the time goes in v6:
time: 209 us
  blocking collectives  79 us (38%)
  starting transfers between devices  65.5 us (31%)
  waiting for transfers between devices  46.4 us (22%)
  Pallas kernels  14.8 us (7%)
    all_to_all x3, blocking collectives, of_everyone(): lax.all_to_all(copies, 'tile', 0, 0, tiled=True, axis_index_groups=groups)  77.2 us
    ppermute x4, starting transfers between devices, shifted(): lax.ppermute(array, 'tile', [(i, (i + by) % peers) for i in range(peers)])  52.8 us
    ppermute x3, waiting for transfers between devices, to_next(): lax.ppermute(sums, axes, [(here + t, there + (t ^ 1)) for t in range(tile...  20.3 us
    all_to_all x1, waiting for transfers between devices, of_everyone(): lax.all_to_all(copies, 'tile', 0, 0, tiled=True, axis_index_groups=groups)  17.5 us
    pallas_call x4, Pallas kernels, section_step(): pl.pallas_call(body, out_shape=tuple(outs), in_specs=[pl.BlockSpec(memory...  13.1 us
    ppermute x4, waiting for transfers between devices, shifted(): lax.ppermute(array, 'tile', [(i, (i + by) % peers) for i in range(peers)])  5.12 us
    all_to_all x1, starting transfers between devices, of_everyone(): lax.all_to_all(copies, 'tile', 0, 0, tiled=True, axis_index_groups=groups)  4.77 us
  transfers between devices with their start and end apart: 14, of which 7 were waited for; matrix products, arithmetic and copies ran while one was open for 1% of the time, Pallas kernels for 1%

profile of v6, /device:TPU:46, one launch (start us, length us, event | category | flops | bytes accessed | tf_op | source)
XLA Modules:
  0.0 208.8 jit_solution(4771020783176214257)
XLA Ops:
  0.0 1.0 pad_maximum_fusion.2.x_ref
  1.0 0.1 fusion.1
  1.1 43.0 %collective-permute-start.1 = (bf16[6,16,4,128]{3,2,1,0:T(4,128)(2,1)S(1)}, bf16[6,16,4,128]{3,2,1,0:T(4,128)(2,1)S(1)}, u32[]{:S(2)}, u32[]{:S(2)}) collective-permute-start(bf16[6,16,4,128]{3,2,1,0:T(4,128)(2,1)S(1)} %get-tuple-element.31), channel_id=1, source_target_pairs={{0,63},{1,0},{2,1},{3,2},{4,3},{5,4},{6,5},{7,6},{8,7},{9,8},{10,9... | collective-permute-start | bytes 294920 | tf_op jit(solution)/shard_map/ppermute | solution.py:19
  44.1 0.0 collective-permute-start
  44.1 0.2 first_sums.1
  44.3 1.8 all-gather.1
  46.1 0.1 collective-permute-done.1
  46.3 3.0 %collective-permute-done = bf16[6,16,4,128]{3,2,1,0:T(4,128)(2,1)S(1)} collective-permute-done((bf16[6,16,4,128]{3,2,1,0:T(4,128)(2,1)S(1)}, bf16[6,16,4,128]{3,2,1,0:T(4,128)(2,1)S(1)}, u32[]{:S(2)}, u32[]{:S(2)}) %collective-permute-start) | collective-permute-done | bytes 98336 | tf_op jit(solution)/shard_map/ppermute | solution.py:19
  49.3 0.3 pad_maximum_fusion
  49.7 2.0 collective-permute-start.2
  51.7 7.9 %collective-permute-start.3 = (bf16[6,4,24,128]{3,2,1,0:T(8,128)(2,1)S(1)}, bf16[6,4,24,128]{3,2,1,0:T(8,128)(2,1)S(1)}, u32[]{:S(2)}, u32[]{:S(2)}) collective-permute-start(bf16[6,4,24,128]{3,2,1,0:T(8,128)(2,1)S(1)} %get-tuple-element.30), channel_id=1, source_target_pairs={{0,56},{1,57},{2,58},{3,59},{4,60},{5,61},{6,62},{7,63},{8,0},{9,1... | collective-permute-start | bytes 442376 | tf_op jit(solution)/shard_map/ppermute | solution.py:19
  59.5 0.6 broadcast_in_dim.32
  60.2 4.8 %all-to-all-start = ((f32[32,1,256]{2,1,0:T(1,128)}), f32[32,1,256]{2,1,0:T(1,128)S(1)}, u32[]{:S(2)}, u32[]{:S(2)}) async-start(f32[32,1,256]{2,1,0:T(1,128)} %broadcast_in_dim.32), calls=%async_computation | async-start | bytes 65536 | tf_op jit(solution)/shard_map/all_to_all | solution.py:41
  65.0 0.1 stack.39.place_ref.refs_0_
  65.1 0.0 copy-start
  65.1 0.0 copy-start.1
  65.1 0.8 collective-permute-done.2
  65.9 1.1 collective-permute-done.3
  67.2 1.5 context.1.refs_3_
  68.7 0.0 copy-start.2
  68.7 0.0 copy-start.3
  68.7 0.1 pad_maximum_fusion.1
  68.8 17.5 %all-to-all-done = f32[32,1,256]{2,1,0:T(1,128)S(1)} async-done(((f32[32,1,256]{2,1,0:T(1,128)}), f32[32,1,256]{2,1,0:T(1,128)S(1)}, u32[]{:S(2)}, u32[]{:S(2)}) %all-to-all-start) | async-done | bytes 32800 | tf_op jit(solution)/shard_map/all_to_all | solution.py:41
  86.3 0.1 reduce_sum.46
  86.4 3.5 %shard_map.64 = (bf16[4,528,128]{2,1,0:T(8,128)(2,1)S(1)}, bf16[4,16,16,128]{3,2,1,0:T(8,128)(2,1)S(1)}, f32[2,128]{1,0:T(2,128)S(1)}) custom-call(s32[5]{0:T(128)S(1)} %stack.39.place_ref.refs_0_, bf16[4,576,128]{2,1,0:T(8,128)(2,1)S(1)} %bitcast.30, f32[2,128]{1,0:T(2,128)S(1)} %bitcast.35, f32[2,528,128]{2,1,0:T(8,128)S(1)} %context.1.refs_3_, ...), custom_call_target="tpu_custom_call" | custom-call | tf_op jit(solution)/shard_map/pallas_call | solution.py:257
  89.9 0.7 collective-permute-start.4
  90.6 0.7 collective-permute-start.6
  91.2 0.7 collective-permute-start.5
  91.9 0.0 collective-permute-done.6
  91.9 0.0 collective-permute-done.5
  92.0 26.5 %all_to_all.20 = f32[32,1,256]{2,1,0:T(1,128)S(1)} all-to-all(f32[32,1,256]{2,1,0:T(1,128)S(1)} %broadcast_in_dim.34), channel_id=1, replica_groups={{0,62,2,60,4,58,6,56,8,54,10,52,12,50,14,48,16,46,18,44,20,42,22,40,24,..., dimensions={0} | all-to-all | bytes 65536 | tf_op jit(solution)/shard_map/all_to_all | solution.py:41
  118.4 0.1 reduce_sum.47
  118.5 0.0 collective-permute-done.4.refs_1_
  118.5 3.2 %shard_map.65 = (bf16[4,480,128]{2,1,0:T(8,128)(2,1)S(1)}, bf16[4,16,16,128]{3,2,1,0:T(8,128)(2,1)S(1)}, f32[2,128]{1,0:T(2,128)S(1)}) custom-call(s32[5]{0:T(128)S(1)} %stack.39.place_ref.refs_0_, bf16[4,528,128]{2,1,0:T(8,128)(2,1)S(1)} %collective-permute-done.4.refs_1_, f32[2,128]{1,0:T(2,128)S(1)} %bitcast.33, f32[2,528,128]{2,1,0:T(8,128)S(1)} %context.1.refs_3_, ...), custom_call_target="tpu_custom_call" | custom-call | tf_op jit(solution)/shard_map/pallas_call | solution.py:257
  121.7 0.7 collective-permute-start.7
  122.4 0.7 collective-permute-start.9
  123.1 0.7 collective-permute-start.8
  123.8 25.4 %all_to_all.21 = f32[32,1,256]{2,1,0:T(1,128)S(1)} all-to-all(f32[32,1,256]{2,1,0:T(1,128)S(1)} %broadcast_in_dim.36), channel_id=1, replica_groups={{0,62,2,60,4,58,6,56,8,54,10,52,12,50,14,48,16,46,18,44,20,42,22,40,24,..., dimensions={0} | all-to-all | bytes 65536 | tf_op jit(solution)/shard_map/all_to_all | solution.py:41
  149.2 0.1 reduce_sum.48
  149.3 3.1 %shard_map.66 = (bf16[4,432,128]{2,1,0:T(8,128)(2,1)S(1)}, bf16[4,16,16,128]{3,2,1,0:T(8,128)(2,1)S(1)}, f32[2,128]{1,0:T(2,128)S(1)}) custom-call(s32[5]{0:T(128)S(1)} %stack.39.place_ref.refs_0_, bf16[4,480,128]{2,1,0:T(8,128)(2,1)S(1)} %collective-permute-done.7.refs_1_, f32[2,128]{1,0:T(2,128)S(1)} %bitcast.34, f32[2,528,128]{2,1,0:T(8,128)S(1)} %context.1.refs_3_, ...), custom_call_target="tpu_custom_call" | custom-call | tf_op jit(solution)/shard_map/pallas_call | solution.py:257
  152.4 1.3 collective-permute-start.12
  153.7 1.3 collective-permute-start.11
  155.0 1.3 collective-permute-start.10
  156.3 20.3 %collective-permute-done.12 = f32[2,128]{1,0:T(2,128)S(1)} collective-permute-done((f32[2,128]{1,0:T(2,128)S(1)}, f32[2,128]{1,0:T(2,128)S(1)}, u32[]{:S(2)}, u32[]{:S(2)}) %collective-permute-start.12) | collective-permute-done | bytes 1056 | tf_op jit(solution)/shard_map/ppermute | solution.py:32
  176.6 3.5 %collective-permute-done.11 = f32[2,128]{1,0:T(2,128)S(1)} collective-permute-done((f32[2,128]{1,0:T(2,128)S(1)}, f32[2,128]{1,0:T(2,128)S(1)}, u32[]{:S(2)}, u32[]{:S(2)}) %collective-permute-start.11) | collective-permute-done | bytes 1056 | tf_op jit(solution)/shard_map/ppermute | solution.py:31
  180.2 25.2 %all_to_all.22 = f32[32,1,256]{2,1,0:T(1,128)S(1)} all-to-all(f32[32,1,256]{2,1,0:T(1,128)S(1)} %broadcast_in_dim.38), channel_id=1, replica_groups={{0,62,2,60,4,58,6,56,8,54,10,52,12,50,14,48,16,46,18,44,20,42,22,40,24,..., dimensions={0} | all-to-all | bytes 65536 | tf_op jit(solution)/shard_map/all_to_all | solution.py:41
  205.4 0.1 reduce_sum.49
  205.5 3.3 %shard_map.67 = bf16[4,16,16,128]{3,2,1,0:T(8,128)(2,1)} custom-call(s32[5]{0:T(128)S(1)} %stack.39.place_ref.refs_0_, bf16[4,432,128]{2,1,0:T(8,128)(2,1)S(1)} %collective-permute-done.10.refs_1_, f32[2,128]{1,0:T(2,128)S(1)} %bitcast.32, f32[2,528,128]{2,1,0:T(8,128)S(1)} %context.1.refs_3_, bf16[3,1152,128]{2,1,0:T(8,128)(2,1)S(1)} %bitcast.29, ...), custom_call_target="tpu_custom_call" | custom-call | tf_op jit(solution)/shard_map/pallas_call | solution.py:257
  (26 shorter events, 0.2 us)
Async XLA Ops:
  1.1 45.2 %collective-permute-start.1 = (bf16[6,16,4,128]{3,2,1,0:T(4,128)(2,1)S(1)}, bf16[6,16,4,128]{3,2,1,0:T(4,128)(2,1)S(1)}, u32[]{:S(2)}, u32[]{:S(2)}) collective-permute-start(bf16[6,16,4,128]{3,2,1,0:T(4,128)(2,1)S(1)} %get-tuple-element.31), channel_id=1, source_target_pairs={{0,63},{1,0},{2,1},{3,2},{4,3},{5,4},{6,5},{7,6},{8,7},{9,8},{10,9... | collective-permute-start | bytes 294920 | tf_op jit(solution)/shard_map/ppermute | solution.py:19
  44.1 5.3 %collective-permute-start = (bf16[6,16,4,128]{3,2,1,0:T(4,128)(2,1)S(1)}, bf16[6,16,4,128]{3,2,1,0:T(4,128)(2,1)S(1)}, u32[]{:S(2)}, u32[]{:S(2)}) collective-permute-start(bf16[6,16,4,128]{3,2,1,0:T(4,128)(2,1)S(1)} %get-tuple-element.32), channel_id=1, source_target_pairs={{0,1},{1,2},{2,3},{3,4},{4,5},{5,6},{6,7},{7,8},{8,9},{9,10},{10,1... | collective-permute-start | bytes 294920 | tf_op jit(solution)/shard_map/ppermute | solution.py:19
  49.6 15.5 %copy-start.4 = (bf16[6,16,24,128]{3,2,1,0:T(8,128)(2,1)}, bf16[6,16,24,128]{3,2,1,0:T(8,128)(2,1)S(1)}, u32[]{:S(2)}) copy-start(bf16[6,16,24,128]{3,2,1,0:T(8,128)(2,1)S(1)} %pad_maximum_fusion) | copy-start | bytes 1769476
  49.7 16.2 %collective-permute-start.2 = (bf16[6,4,24,128]{3,2,1,0:T(8,128)(2,1)S(1)}, bf16[6,4,24,128]{3,2,1,0:T(8,128)(2,1)S(1)}, u32[]{:S(2)}, u32[]{:S(2)}) collective-permute-start(bf16[6,4,24,128]{3,2,1,0:T(8,128)(2,1)S(1)} %get-tuple-element.29), channel_id=1, source_target_pairs={{0,8},{1,9},{2,10},{3,11},{4,12},{5,13},{6,14},{7,15},{8,16},{9,17... | collective-permute-start | bytes 442376 | tf_op jit(solution)/shard_map/ppermute | solution.py:19
  51.7 15.4 %collective-permute-start.3 = (bf16[6,4,24,128]{3,2,1,0:T(8,128)(2,1)S(1)}, bf16[6,4,24,128]{3,2,1,0:T(8,128)(2,1)S(1)}, u32[]{:S(2)}, u32[]{:S(2)}) collective-permute-start(bf16[6,4,24,128]{3,2,1,0:T(8,128)(2,1)S(1)} %get-tuple-element.30), channel_id=1, source_target_pairs={{0,56},{1,57},{2,58},{3,59},{4,60},{5,61},{6,62},{7,63},{8,0},{9,1... | collective-permute-start | bytes 442376 | tf_op jit(solution)/shard_map/ppermute | solution.py:19
  60.2 26.1 %all-to-all-start = ((f32[32,1,256]{2,1,0:T(1,128)}), f32[32,1,256]{2,1,0:T(1,128)S(1)}, u32[]{:S(2)}, u32[]{:S(2)}) async-start(f32[32,1,256]{2,1,0:T(1,128)} %broadcast_in_dim.32), calls=%async_computation | async-start | bytes 65536 | tf_op jit(solution)/shard_map/all_to_all | solution.py:41
  65.1 2.0 copy-start
  65.1 2.0 copy-start.1
  67.1 1.6 slice-start
  68.7 17.7 %copy-start.2 = (f32[1,128]{1,0:T(1,128)S(1)}, f32[1,128]{1,0:T(1,128)}, u32[]{:S(2)}) copy-start(f32[1,128]{1,0:T(1,128)} %refs_6_.7) | copy-start | bytes 1540
  68.7 17.7 %copy-start.3 = (f32[1,128]{1,0:T(1,128)S(1)}, f32[1,128]{1,0:T(1,128)}, u32[]{:S(2)}) copy-start(f32[1,128]{1,0:T(1,128)} %refs_7_.7) | copy-start | bytes 1540
  89.9 28.6 %collective-permute-start.4 = (bf16[4,528,128]{2,1,0:T(8,128)(2,1)S(1)}, bf16[4,528,128]{2,1,0:T(8,128)(2,1)S(1)}, u32[]{:S(2)}, u32[]{:S(2)}) collective-permute-start(bf16[4,528,128]{2,1,0:T(8,128)(2,1)S(1)} %get-tuple-element.20), channel_id=1, source_target_pairs={{0,64},{1,65},{2,66},{3,67},{4,68},{5,69},{6,70},{7,71},{8,72},{9,... | collective-permute-start | bytes 1622024 | tf_op jit(solution)/shard_map/ppermute | solution.py:319
  90.6 1.3 collective-permute-start.6
  91.2 0.7 collective-permute-start.5
  121.7 27.6 %collective-permute-start.7 = (bf16[4,480,128]{2,1,0:T(8,128)(2,1)S(1)}, bf16[4,480,128]{2,1,0:T(8,128)(2,1)S(1)}, u32[]{:S(2)}, u32[]{:S(2)}) collective-permute-start(bf16[4,480,128]{2,1,0:T(8,128)(2,1)S(1)} %get-tuple-element.23), channel_id=1, source_target_pairs={{64,128},{65,129},{66,130},{67,131},{68,132},{69,133},{70,134},{71... | collective-permute-start | bytes 1474568 | tf_op jit(solution)/shard_map/ppermute | solution.py:319
  122.4 1.3 collective-permute-start.9
  123.1 0.7 collective-permute-start.8
  152.4 24.2 %collective-permute-start.12 = (f32[2,128]{1,0:T(2,128)S(1)}, f32[2,128]{1,0:T(2,128)S(1)}, u32[]{:S(2)}, u32[]{:S(2)}) collective-permute-start(f32[2,128]{1,0:T(2,128)S(1)} %get-tuple-element.27), channel_id=1, source_target_pairs={{128,193},{129,192},{130,195},{131,194},{132,197},{133,196},{134,1... | collective-permute-start | bytes 3080 | tf_op jit(solution)/shard_map/ppermute | solution.py:32
  153.7 26.4 %collective-permute-start.11 = (f32[2,128]{1,0:T(2,128)S(1)}, f32[2,128]{1,0:T(2,128)S(1)}, u32[]{:S(2)}, u32[]{:S(2)}) collective-permute-start(f32[2,128]{1,0:T(2,128)S(1)} %get-tuple-element.27), channel_id=1, source_target_pairs={{128,192},{129,193},{130,194},{131,195},{132,196},{133,197},{134,1... | collective-permute-start | bytes 3080 | tf_op jit(solution)/shard_map/ppermute | solution.py:31
  155.0 50.5 %collective-permute-start.10 = (bf16[4,432,128]{2,1,0:T(8,128)(2,1)S(1)}, bf16[4,432,128]{2,1,0:T(8,128)(2,1)S(1)}, u32[]{:S(2)}, u32[]{:S(2)}) collective-permute-start(bf16[4,432,128]{2,1,0:T(8,128)(2,1)S(1)} %get-tuple-element.26), channel_id=1, source_target_pairs={{128,192},{129,193},{130,194},{131,195},{132,196},{133,197},{134,1... | collective-permute-start | bytes 1327112 | tf_op jit(solution)/shard_map/ppermute | solution.py:319
